TPU v7x, 8 devices: a whole 2x2x1 slice. The times are simulated.
8 devices in a mesh: ep: 8 (over z, y, x, core).
Axes of the slice: x: 2, y: 2, z: 1, core: 2. Of those that a mesh axis runs over, the one named last changes fastest.
Arguments:
- x: bfloat16 [32768, 1024], P('ep')
- gate_w: bfloat16 [1024, 32], replicated
- up_w: bfloat16 [32, 1024, 512], P('ep')
- down_w: bfloat16 [32, 512, 1024], P('ep')
- expert_picks: int32 [32, 2048], P('ep')
- loss_w: bfloat16 [32768, 1024], P('ep')
Outputs:
- output 1: bfloat16 [32768, 1024], P('ep')
- output 2: float32 [], replicated
- output 3: bfloat16 [32768, 1024], P('ep')
- output 4: bfloat16 [32, 1024, 512], P('ep')
- output 5: bfloat16 [32, 512, 1024], P('ep')
- output 6: float32 [1024, 32], replicated
All inputs are finite; a program needn't handle non-finite values.
Results may differ from a plain program's by a relative error of at most 0.0107506.
Values are sent between devices in bfloat16 or wider.
A program may use at most 1 GiB of HBM per device.

v0:
```python
import math
import jax
import jax.numpy as jnp
from jax import lax
from jax.sharding import PartitionSpec as P


def solution(mesh):
    group_size = mesh.shape['ep']

    def device_step(x, gate_w, up_w, down_w, expert_picks, loss_w):
        tok_dev, hidden = x.shape
        local_experts, capacity = expert_picks.shape
        shard_picks = capacity // group_size
        loss_scale = 1.0 / math.sqrt(tok_dev * group_size * hidden)
        my_index = lax.axis_index('ep')
        expert_col = jnp.arange(group_size)[None, :, None] * local_experts + jnp.arange(local_experts)[:, None, None]

        wanted = expert_picks.reshape(local_experts, group_size, shard_picks)
        asked_ids = lax.all_to_all(wanted, 'ep', 1, 1, tiled=True) - my_index * tok_dev
        flat_ids = asked_ids.reshape(-1)

        logits = jnp.dot(x, gate_w, preferred_element_type=jnp.float32)
        gate_probs = jax.nn.softmax(logits, axis=-1)
        gate_vals = gate_probs[asked_ids, expert_col]
        tok_rows = lax.all_to_all(x[asked_ids], 'ep', 1, 1, tiled=True).reshape(local_experts, capacity, hidden)

        pre_act = jnp.einsum('lch,lhf->lcf', tok_rows, up_w, preferred_element_type=jnp.float32)
        gelu_val, gelu_pull = jax.vjp(jax.nn.gelu, pre_act)
        hidden_act = gelu_val.astype(jnp.bfloat16)
        expert_out = jnp.einsum('lcf,lfh->lch', hidden_act, down_w, preferred_element_type=jnp.float32).astype(jnp.bfloat16)
        out_back = lax.all_to_all(expert_out.reshape(local_experts, group_size, shard_picks, hidden), 'ep', 1, 1, tiled=True).astype(jnp.float32)

        mixed_f32 = x.astype(jnp.float32) + jax.ops.segment_sum((gate_vals[..., None] * out_back).reshape(-1, hidden), flat_ids, num_segments=tok_dev)
        y = mixed_f32.astype(jnp.bfloat16)
        weight_f32 = loss_w.astype(jnp.float32)
        loss_total = lax.psum(jnp.sum(y.astype(jnp.float32) * weight_f32), 'ep') * loss_scale

        dy_rows = loss_w[asked_ids].astype(jnp.float32) * loss_scale
        grad_out = (gate_vals[..., None] * dy_rows).astype(jnp.bfloat16)
        grad_gate_vals = jnp.sum(dy_rows * out_back, axis=-1)
        grad_out_in = lax.all_to_all(grad_out, 'ep', 1, 1, tiled=True).reshape(local_experts, capacity, hidden)

        grad_down = jnp.einsum('lcf,lch->lfh', hidden_act, grad_out_in, preferred_element_type=jnp.float32).astype(jnp.bfloat16)
        grad_act = jnp.einsum('lch,lfh->lcf', grad_out_in, down_w, preferred_element_type=jnp.float32).astype(jnp.bfloat16)
        grad_pre = gelu_pull(grad_act.astype(jnp.float32))[0].astype(jnp.bfloat16)
        grad_up = jnp.einsum('lch,lcf->lhf', tok_rows, grad_pre, preferred_element_type=jnp.float32).astype(jnp.bfloat16)
        grad_rows = jnp.einsum('lcf,lhf->lch', grad_pre, up_w, preferred_element_type=jnp.float32).astype(jnp.bfloat16)
        rows_back = lax.all_to_all(grad_rows.reshape(local_experts, group_size, shard_picks, hidden), 'ep', 1, 1, tiled=True)

        probs_grad = jnp.zeros(gate_probs.shape, jnp.float32).at[asked_ids, expert_col].add(grad_gate_vals)
        grad_logits = (gate_probs * (probs_grad - jnp.sum(gate_probs * probs_grad, axis=-1, keepdims=True))).astype(jnp.bfloat16)
        grad_gate = lax.psum(lax.dot_general(x, grad_logits, (((0,), (0,)), ((), ())), preferred_element_type=jnp.float32), 'ep')
        grad_x = (weight_f32 * loss_scale
                  + jax.ops.segment_sum(rows_back.astype(jnp.float32).reshape(-1, hidden), flat_ids, num_segments=tok_dev)
                  + lax.dot_general(grad_logits, gate_w, (((1,), (1,)), ((), ())), preferred_element_type=jnp.float32))
        return y, loss_total, grad_x.astype(jnp.bfloat16), grad_up, grad_down, grad_gate

    return jax.shard_map(device_step, mesh=mesh,
                         in_specs=(P('ep'), P(), P('ep'), P('ep'), P('ep'), P('ep')),
                         out_specs=(P('ep'), P(), P('ep'), P('ep'), P('ep'), P()),
                         check_vma=False)
```

profile of v0, /device:TPU:0, one launch (start us, length us, event | category | flops | bytes accessed | tf_op | source)
XLA Modules:
  0.0 1256.6 jit_solution(12530860195378821649)
XLA Ops:
  7.2 0.0 copy-start
  7.2 4.3 all-to-all-start
  11.5 4.6 all-to-all-done
  16.1 0.0 copy-start.3
  16.2 45.1 %gather_fusion.1 = bf16[8192,1024]{1,0:T(8,128)(2,1)} fusion(bf16[4096,1024]{1,0:T(8,128)(2,1)} %param.6, s32[8192]{0:T(1024)S(1)} %broadcast_clamp_fusion), kind=kCustom, calls=%fused_computation.1 | custom fusion | bytes 33587200 | tf_op jit(solution)/shard_map/gather | solution.py:26
  61.4 8.2 copy.63
  69.5 185.4 %all_to_all.25 = bf16[4,8,256,1024]{3,2,0,1:T(8,128)(2,1)S(1)} all-to-all(bf16[4,8,256,1024]{3,2,0,1:T(8,128)(2,1)S(1)} %copy.63), channel_id=1, replica_groups=mesh['ep'=8] {'ep'}, dimensions={1} | all-to-all | bytes 33554432 | tf_op jit(solution)/shard_map/all_to_all | solution.py:26
  254.9 0.0 copy-start.8
  254.9 7.1 copy.64
  262.0 0.0 copy-done.8
  262.0 15.6 %fusion.23 = f32[4,2048,512]{2,1,0:T(8,128)} fusion(bf16[4,2048,1024]{2,1,0:T(8,128)(2,1)} %bitcast.67, bf16[4,1024,512]{2,1,0:T(8,128)(2,1)S(1)} %copy-done.8), kind=kOutput, calls=%fused_computation.64 | convolution fusion | flops 8589934592 | bytes 37748736 | tf_op jit(solution)/shard_map/lch,lhf->lcf/dot_general | solution.py:28
  277.7 17.9 %convolution_convert_fusion.1 = bf16[4,2048,1024]{2,1,0:T(8,128)(2,1)} fusion(bf16[4,512,1024]{2,1,0:T(8,128)(2,1)} %param.9, f32[4,2048,512]{2,1,0:T(8,128)} %fusion.23), kind=kOutput, calls=%fused_computation.30 | convolution fusion | flops 8636071936 | bytes 37748736 | tf_op jit(solution)/shard_map/lcf,lfh->lch/dot_general | solution.py:31
  295.6 13.9 %copy.65 = bf16[4,8,256,1024]{3,2,0,1:T(8,128)(2,1)} copy(bf16[4,8,256,1024]{3,2,1,0:T(8,128)(2,1)} %bitcast.71) | data formatting | bytes 33554432 | tf_op jit(solution)/shard_map/reshape | solution.py:32
  309.5 5.1 all-to-all-start.2
  314.6 0.0 copy-done
  314.6 6.0 fusion.22
  320.5 0.1 fusion.17
  320.6 0.1 clamp_shift-left_fusion
  320.7 0.0 copy-done.3
  320.7 0.1 shift-left_or_fusion
  320.8 0.1 broadcast_in_dim.7
  320.9 0.0 copy-done.6
  320.9 0.1 multiply_reduce_fusion
  321.0 0.0 copy-done.5
  321.0 0.1 and_reduce_fusion
  321.2 45.1 %gather_fusion.2 = bf16[8192,1024]{1,0:T(8,128)(2,1)} fusion(bf16[4096,1024]{1,0:T(8,128)(2,1)} %param.11, s32[8192]{0:T(1024)S(1)} %broadcast_clamp_fusion), kind=kCustom, calls=%fused_computation.2 | custom fusion | bytes 33587200 | tf_op jit(solution)/shard_map/gather | solution.py:39
  366.3 18.6 %bitcast_convert_fusion = f32[4,8,256,1024]{3,2,1,0:T(8,128)} fusion(bf16[8192,1024]{1,0:T(8,128)(2,1)} %gather_fusion.2), kind=kLoop, calls=%fused_computation.61 | loop fusion | flops 8388608 | bytes 50331648 | tf_op jit(solution)/shard_map/convert_element_type | solution.py:39
  384.9 113.6 %all-to-all-done.2 = bf16[4,8,256,1024]{3,2,0,1:T(8,128)(2,1)} async-done(((bf16[4,8,256,1024]{3,2,0,1:T(8,128)(2,1)}), bf16[4,8,256,1024]{3,2,0,1:T(8,128)(2,1)}, u32[]{:S(2)}, u32[]{:S(2)}) %all-to-all-start.2) | async-done | bytes 16777248 | tf_op jit(solution)/shard_map/all_to_all | solution.py:32
  498.5 16.4 %fusion = f32[4,8,256]{2,0,1:T(4,128)S(1)} fusion(bf16[4,8,256,1024]{3,2,0,1:T(8,128)(2,1)} %all-to-all-done.2, f32[4,8,256,1024]{3,2,1,0:T(8,128)} %bitcast_convert_fusion), kind=kLoop, calls=%fused_computation.8 | loop fusion | flops 33546240 | bytes 50364416 | tf_op jit(solution)/shard_map/reduce_sum | solution.py:41
  514.9 43.3 %scatter_custom_fusion.2 = f32[131072]{0:T(1024)S(1)} fusion(s32[8192]{0:T(1024)S(1)} %bitcast.82, f32[8192]{0:T(1024)S(1)} %bitcast.83, f32[]{:T(128)} %constant.17.clone.1), kind=kCustom, calls=%fused_computation.42 | custom fusion | flops 8192 | bytes 524292
  558.3 0.1 reshape.87
  558.4 0.1 fusion.15
  558.5 65.5 %gather_fusion = f32[8192]{0:T(1024)S(1)} fusion(f32[4096,32]{0,1:T(8,128)S(1)} %get-tuple-element.7, s32[8192]{0:T(1024)S(1)} %bitcast.63), kind=kCustom, calls=%fused_computation | custom fusion | bytes 131072 | tf_op jit(solution)/shard_map/gather | solution.py:25
  624.2 9.2 multiply_convert_fusion
  633.3 185.6 %all_to_all.26 = bf16[4,8,256,1024]{3,2,0,1:T(8,128)(2,1)S(1)} all-to-all(bf16[4,8,256,1024]{3,2,0,1:T(8,128)(2,1)S(1)} %multiply_convert_fusion), channel_id=1, replica_groups=mesh['ep'=8] {'ep'}, dimensions={1} | all-to-all | bytes 33554432 | tf_op jit(solution)/shard_map/all_to_all | solution.py:42
  818.9 7.2 copy.72
  826.1 0.0 copy-done.7
  826.1 26.0 %fusion.5 = bf16[4,2048,512]{2,1,0:T(8,128)(2,1)} fusion(f32[4,2048,512]{2,1,0:T(8,128)} %fusion.23, bf16[4,2048,1024]{2,1,0:T(8,128)(2,1)} %bitcast.69, bf16[4,512,1024]{2,1,0:T(8,128)(2,1)S(1)} %copy-done.7), kind=kOutput, calls=%fused_computation.20 | convolution fusion | flops 8682209280 | bytes 46137344 | tf_op jit(solution)/shard_map/lch,lfh->lcf/dot_general | solution.py:45
  852.1 15.8 %convolution_convert_fusion = bf16[4,2048,1024]{2,1,0:T(8,128)(2,1)} fusion(bf16[4,2048,512]{2,1,0:T(8,128)(2,1)} %fusion.5, bf16[4,1024,512]{2,1,0:T(8,128)(2,1)} %param.8), kind=kOutput, calls=%fused_computation.29 | convolution fusion | flops 8598323200 | bytes 29360128 | tf_op jit(solution)/shard_map/lcf,lhf->lch/dot_general | solution.py:48
  867.9 13.8 %copy.73 = bf16[4,8,256,1024]{3,2,0,1:T(8,128)(2,1)} copy(bf16[4,8,256,1024]{3,2,1,0:T(8,128)(2,1)} %bitcast.72) | data formatting | bytes 33554432 | tf_op jit(solution)/shard_map/reshape | solution.py:49
  881.7 4.5 all-to-all-start.4
  886.1 0.0 copy-start.4
  886.2 0.3 all-reduce.2.cloned.1.call-start
  886.4 11.3 convert_element_type.52
  897.7 0.0 copy-done.4
  897.7 0.1 fusion.14
  897.8 0.0 copy-start.1
  897.8 0.7 copy-done.1
  898.5 5.6 convolution_bitcast_fusion
  904.1 0.0 all-reduce.2.cloned.1.call-update
  904.1 8.8 convert_multiply_fusion.1
  913.0 11.1 copy.66
  924.0 82.4 %scatter_fusion = f32[4096,1024]{1,0:T(8,128)} fusion(f32[4096,1024]{1,0:T(8,128)} %convert_element_type.52, s32[8192]{0:T(1024)S(1)} %bitcast.73, f32[8192,1024]{1,0:T(8,128)} %bitcast.65), kind=kCustom, calls=%fused_computation.3 | custom fusion | flops 8388608 | bytes 100696064 | tf_op jit(solution)/shard_map/scatter-add | solution.py:34
  1006.4 13.1 %fusion.1 = (f32[]{:T(128)}, bf16[4096,1024]{1,0:T(8,128)(2,1)}) fusion(bf16[4096,1024]{1,0:T(8,128)(2,1)} %param.11, f32[4096,1024]{1,0:T(8,128)} %scatter_fusion), kind=kLoop, calls=%fused_computation.16 | loop fusion | flops 20971520 | bytes 33554436 | tf_op jit(solution)/shard_map/reduce_sum | solution.py:37
  1019.6 68.8 %psum.14 = f32[]{:T(128)} all-reduce(f32[]{:T(128)} %get-tuple-element.10), channel_id=1, replica_groups=mesh['ep'=8] {'ep'}, use_global_device_ids=true, to_apply=%region_4.0 | all-reduce | flops 1 | bytes 8 | tf_op jit(solution)/shard_map/psum | solution.py:37
  1089.0 0.0 copy-done.2
  1089.0 11.5 fusion.2
  1100.5 19.6 %convolution_convert_fusion.2 = bf16[4,512,1024]{2,1,0:T(8,128)(2,1)} fusion(bf16[4,2048,1024]{2,1,0:T(8,128)(2,1)} %bitcast.70, f32[4,2048,512]{2,1,0:T(8,128)} %fusion.23), kind=kOutput, calls=%fused_computation.31 | convolution fusion | flops 8629780480 | bytes 37748736 | tf_op jit(solution)/shard_map/lcf,lch->lfh/dot_general | solution.py:44
  1120.1 16.5 %convolution_convert_fusion.3 = bf16[4,1024,512]{2,1,0:T(8,128)(2,1)} fusion(bf16[4,2048,1024]{2,1,0:T(8,128)(2,1)} %bitcast.68, bf16[4,2048,512]{2,1,0:T(8,128)(2,1)} %fusion.5), kind=kOutput, calls=%fused_computation.32 | convolution fusion | flops 8592031744 | bytes 29360128 | tf_op jit(solution)/shard_map/lch,lcf->lhf/dot_general | solution.py:47
  1136.5 0.0 all-to-all-done.4
  1136.5 18.6 %copy.74 = f32[4,8,256,1024]{3,2,1,0:T(8,128)} copy(bf16[4,8,256,1024]{3,2,0,1:T(8,128)(2,1)} %all-to-all-done.4) | data formatting | bytes 50331648 | tf_op jit(solution)/shard_map/reshape | solution.py:55
  1155.1 82.4 %scatter_fusion.1 = f32[4096,1024]{1,0:T(8,128)} fusion(f32[4096,1024]{1,0:T(8,128)} %fusion.2, s32[8192]{0:T(1024)S(1)} %bitcast.74, f32[8192,1024]{1,0:T(8,128)} %bitcast.64), kind=kCustom, calls=%fused_computation.4 | custom fusion | flops 8388608 | bytes 100696064 | tf_op jit(solution)/shard_map/scatter-add | solution.py:55
  1237.5 9.1 convert_element_type.66
  1246.5 1.6 copy.99
  (24 shorter events, 0.2 us)
Async XLA Ops:
  7.2 307.4 %copy-start = (bf16[1024,32]{0,1:T(8,128)(2,1)S(1)}, bf16[1024,32]{0,1:T(8,128)(2,1)}, u32[]{:S(2)}) copy-start(bf16[1024,32]{0,1:T(8,128)(2,1)} %param.7) | copy-start | bytes 196612
  7.2 8.9 all-to-all-start
  16.1 304.6 %copy-start.3 = (s32[4,8,256]{2,0,1:T(4,128)}, s32[4,8,256]{2,0,1:T(4,128)S(1)}, u32[]{:S(2)}) copy-start(s32[4,8,256]{2,0,1:T(4,128)S(1)} %get-tuple-element.9) | copy-start | bytes 98308
  254.9 7.1 copy-start.8
  309.5 11.5 copy-start.6
  309.5 11.6 copy-start.5
  309.5 189.1 %all-to-all-start.2 = ((bf16[4,8,256,1024]{3,2,0,1:T(8,128)(2,1)}), bf16[4,8,256,1024]{3,2,0,1:T(8,128)(2,1)}, u32[]{:S(2)}, u32[]{:S(2)}) async-start(bf16[4,8,256,1024]{3,2,0,1:T(8,128)(2,1)} %copy.65), calls=%async_computation.2 | async-start | bytes 33554432 | tf_op jit(solution)/shard_map/all_to_all | solution.py:32
  818.9 7.2 copy-start.7
  881.7 254.8 %all-to-all-start.4 = ((bf16[4,8,256,1024]{3,2,0,1:T(8,128)(2,1)}), bf16[4,8,256,1024]{3,2,0,1:T(8,128)(2,1)}, u32[]{:S(2)}, u32[]{:S(2)}) async-start(bf16[4,8,256,1024]{3,2,0,1:T(8,128)(2,1)} %copy.73), calls=%async_computation.4 | async-start | bytes 33554432 | tf_op jit(solution)/shard_map/all_to_all | solution.py:49
  886.1 11.5 copy-start.4
  886.2 360.4 %all-reduce.2.cloned.1.call-start = ((), (), s32[]{:S(2)}) async-start(), calls=%async_computation.5 | async-start | bytes 262144 | tf_op jit(solution)/shard_map/psum | solution.py:53
  897.8 0.7 copy-start.1
  1006.4 82.6 %copy-start.2 = (bf16[4096,32]{0,1:T(8,128)(2,1)S(1)}, bf16[4096,32]{0,1:T(8,128)(2,1)}, u32[]{:S(2)}) copy-start(bf16[4096,32]{0,1:T(8,128)(2,1)} %copy-done.1) | copy-start | bytes 786436
Sparse Core Ops, SparseCore 0:
  904.2 167.1 all-reduce.1
where the time goes:
time: 1270 us; the launch traced here: 1260 us
  blocking collectives  440 us (35%)
  other arithmetic  295 us (23%)
  local copies, waits for them, and re-layouts  238 us (19%)
  matrix products  134 us (11%)
  waiting for transfers between devices  118 us (9%)
  between operations  16.6 us (1%)
  starting transfers between devices  14.1 us (1%)
    all_to_all x1, blocking collectives, device_step(): lax.all_to_all(grad_out, 'ep', 1, 1, tiled=True)  186 us
    all_to_all x1, blocking collectives, device_step(): lax.all_to_all(x[asked_ids], 'ep', 1, 1, tiled=True)  185 us
    all_to_all x1, waiting for transfers between devices, device_step(): lax.all_to_all(expert_out.reshape(local_experts, group_size, shard_picks,...  114 us
    scatter-add x1, other arithmetic, device_step(): jax.ops.segment_sum((gate_vals[..., None] * out_back).reshape(-1, hidden)...  82.4 us
    scatter-add x1, other arithmetic, device_step(): jax.ops.segment_sum(rows_back.astype(jnp.float32).reshape(-1, hidden), fl...  82.4 us
    psum x1, blocking collectives, device_step(): lax.psum(jnp.sum(y.astype(jnp.float32) * weight_f32), 'ep') * loss_scale  68.8 us
    gather x3, local copies, waits for them, and re-layouts, device_step(): gate_vals = gate_probs[asked_ids, expert_col]  65.6 us
    gather x2, local copies, waits for them, and re-layouts, device_step(): x[asked_ids]  53.3 us
  transfers between devices with their start and end apart: 4, of which 2 were waited for; matrix products, arithmetic and copies ran while one was open for 29% of the time, Pallas kernels for 0%

commit v1 on v0

v1 whole, which is shorter than its diff:
```python
import functools
import math
import jax
import jax.numpy as jnp
from jax import lax
from jax.experimental import pallas as pl
from jax.experimental.pallas import tpu as pltpu
from jax.sharding import PartitionSpec as P


F32, BF16 = jnp.float32, jnp.bfloat16
LANES = 128
CHUNK = 512
MIB = 2**20


def as_tiles(ref, cols):
    return ref.reshape(ref.shape[0] * LANES // (8 * cols), cols // LANES, 8, LANES)


def put_rows(ref, start, value):
    rows, cols = value.shape
    tiles = as_tiles(ref, cols)
    for c in range(cols // LANES):
        tiles[pl.ds(start // 8, rows // 8), c] = value[:, c * LANES:(c + 1) * LANES].reshape(rows // 8, 8, LANES)


def get_rows(ref, start, rows, cols):
    tiles = as_tiles(ref, cols)
    parts = [tiles[pl.ds(start // 8, rows // 8), c].reshape(rows, LANES) for c in range(cols // LANES)]
    return jnp.concatenate(parts, axis=1)


def row_base(row):
    return ((row >> 3) << 6) | (row & 7)


def gather_body(idx, *refs, num_src, rows, block):
    srcs = refs[:num_src]
    out, src32, stage, buf, sem = refs[num_src:]
    step = pl.program_id(0)
    chunks = rows // CHUNK

    @pl.when(step == 0)
    def _():
        def load(k):
            src = srcs[k] if num_src > 1 else srcs[0].at[pl.ds(k * CHUNK, CHUNK)]
            return pltpu.make_async_copy(src, buf.at[k % 2], sem.at[k % 2])

        load(0).start()
        for k in range(chunks):
            if k + 1 < chunks:
                load(k + 1).start()
            load(k).wait()
            put_rows(src32, k * CHUNK, buf[k % 2].astype(F32))

    unroll = 16

    def body(i, carry):
        vals = [src32[pl.ds(idx[step * block + i * unroll + j], 8, stride=8), :] for j in range(unroll)]
        for j in range(unroll):
            stage[pl.ds(i * (unroll * 8) + (j // 8) * 64 + j % 8, 8, stride=8), :] = vals[j]
        return carry

    lax.fori_loop(0, block // unroll, body, 0)
    out[...] = get_rows(stage, 0, block, out.shape[1]).astype(BF16)


def gather_rows(idx, srcs, num_out):
    rows, cols = sum(s.shape[0] for s in srcs), srcs[0].shape[1]
    block = 512
    return pl.pallas_call(
        functools.partial(gather_body, num_src=len(srcs), rows=rows, block=block),
        grid_spec=pltpu.PrefetchScalarGridSpec(
            num_scalar_prefetch=1, grid=(num_out // block,),
            in_specs=[pl.BlockSpec(memory_space=pl.ANY)] * len(srcs),
            out_specs=pl.BlockSpec((block, cols), lambda i, idx: (i, 0)),
            scratch_shapes=[pltpu.VMEM((rows * 8, LANES), F32), pltpu.VMEM((block * 8, LANES), F32),
                            pltpu.VMEM((2, CHUNK, cols), BF16), pltpu.SemaphoreType.DMA((2,))]),
        out_shape=jax.ShapeDtypeStruct((num_out, cols), BF16),
        compiler_params=pltpu.CompilerParams(dimension_semantics=("arbitrary",), vmem_limit_bytes=40 * MIB),
        cost_estimate=pl.CostEstimate(flops=num_out * 1_000_000, bytes_accessed=num_out * cols * 4, transcendentals=0))(idx, *srcs)


def dot(a, b):
    return lax.dot_general(a, b, (((1,), (0,)), ((), ())), preferred_element_type=F32)


def dot_nt(a, b):
    return lax.dot_general(a, b, (((1,), (1,)), ((), ())), preferred_element_type=F32)


def dot_tn(a, b):
    return lax.dot_general(a, b, (((0,), (0,)), ((), ())), preferred_element_type=F32)


def softmax_rows(x_rows, gate_pad, experts):
    logits = dot(x_rows, gate_pad)
    lane = lax.broadcasted_iota(jnp.int32, logits.shape, 1)
    live = lane < experts
    logits = jnp.where(live, logits, -jnp.inf)
    e = jnp.exp(logits - jnp.max(logits, axis=1, keepdims=True))
    return e / jnp.sum(e, axis=1, keepdims=True), lane


def gelu_parts(a):
    c = math.sqrt(2.0 / math.pi)
    sq = a * a
    t = jnp.tanh(c * (a + 0.044715 * (sq * a)))
    half = 0.5 * (1.0 + t)
    return a * half, half + (0.5 * a) * (1.0 - t * t) * (c + (3.0 * 0.044715 * c) * sq)


def owner_body(ids, x_ref, r_ref, w1_ref, w2_ref, gate_ref, *refs, first, experts, scale):
    h_ref, g_ref, aux_ref = refs[-3:]
    expert = ids[first + pl.program_id(0)]
    x_rows = x_ref[...]
    w1, w2 = w1_ref[0], w2_ref[0]
    probs, lane = softmax_rows(x_rows, gate_ref[...], experts)
    gate = jnp.sum(jnp.where(lane == expert, probs, 0.0), axis=1, keepdims=True)
    act, slope = gelu_parts(dot(x_rows, w1))
    h = dot(act.astype(BF16), w2).astype(BF16)
    dy = r_ref[...].astype(F32) * scale
    gate_grad = jnp.sum(dy * h.astype(F32), axis=1, keepdims=True)
    dh = (gate * dy).astype(BF16)
    du = dot_nt(dh, w2).astype(BF16)
    da = (slope * du.astype(F32)).astype(BF16)
    h_ref[...] = h
    g_ref[...] = dot_nt(da, w1).astype(BF16)
    aux_ref[...] = jnp.where(lane == expert, gate_grad, jnp.where(lane == 64, gate, 0.0))


def owner_group(ids, picked_x, picked_r, w1, w2, gate_pad, bufs, first, picks, experts, scale):
    num = w1.shape[0]
    cols, width = w1.shape[1], w1.shape[2]
    total = picked_x.shape[0]
    rows = lambda i, ids: (first + i, 0)
    weight = lambda i, ids: (i, 0, 0)
    in_specs = [pl.BlockSpec((picks, cols), rows), pl.BlockSpec((picks, cols), rows),
                pl.BlockSpec((1, cols, width), weight), pl.BlockSpec((1, width, cols), weight),
                pl.BlockSpec(gate_pad.shape, lambda i, ids: (0, 0))]
    alias = {}
    if bufs:
        in_specs += [pl.BlockSpec(memory_space=pl.ANY)] * 3
        alias = {6: 0, 7: 1, 8: 2}
    return pl.pallas_call(
        functools.partial(owner_body, first=first, experts=experts, scale=scale),
        grid_spec=pltpu.PrefetchScalarGridSpec(
            num_scalar_prefetch=1, grid=(num,), in_specs=in_specs,
            out_specs=[pl.BlockSpec((picks, cols), rows), pl.BlockSpec((picks, cols), rows),
                       pl.BlockSpec((picks, LANES), rows)]),
        out_shape=[jax.ShapeDtypeStruct((total, cols), BF16), jax.ShapeDtypeStruct((total, cols), BF16),
                   jax.ShapeDtypeStruct((total, LANES), F32)],
        input_output_aliases=alias,
        compiler_params=pltpu.CompilerParams(dimension_semantics=("arbitrary",), vmem_limit_bytes=40 * MIB),
        cost_estimate=pl.CostEstimate(flops=num * 1_000_000_000, bytes_accessed=num * 4 * MIB, transcendentals=0))(ids, picked_x, picked_r, w1, w2, gate_pad, *bufs)


def expert_body(ids, x_ref, r_ref, w1_ref, w2_ref, gate_ref, up_ref, down_ref, up_acc, down_acc, *, experts, scale):
    expert = ids[pl.program_id(0)]
    step = pl.program_id(1)
    x_rows = x_ref[...]
    w1, w2 = w1_ref[0], w2_ref[0]
    probs, lane = softmax_rows(x_rows, gate_ref[...], experts)
    gate = jnp.sum(jnp.where(lane == expert, probs, 0.0), axis=1, keepdims=True)
    act, slope = gelu_parts(dot(x_rows, w1))
    dh = (gate * (r_ref[...].astype(F32) * scale)).astype(BF16)
    du = dot_nt(dh, w2).astype(BF16)
    da = (slope * du.astype(F32)).astype(BF16)

    @pl.when(step == 0)
    def _():
        up_acc[...] = jnp.zeros_like(up_acc)
        down_acc[...] = jnp.zeros_like(down_acc)

    down_acc[...] += dot_tn(act.astype(BF16), dh)
    up_acc[...] += dot_tn(x_rows, da)

    @pl.when(step == pl.num_programs(1) - 1)
    def _():
        up_ref[0] = up_acc[...].astype(BF16)
        down_ref[0] = down_acc[...].astype(BF16)


def expert_grads(ids, rows_x, rows_r, w1, w2, gate_pad, experts, scale):
    num, cols, width = w1.shape
    block = 512
    steps = rows_x.shape[0] // num // block
    rows = lambda e, i, ids: (e * steps + i, 0)
    weight = lambda e, i, ids: (e, 0, 0)
    return pl.pallas_call(
        functools.partial(expert_body, experts=experts, scale=scale),
        grid_spec=pltpu.PrefetchScalarGridSpec(
            num_scalar_prefetch=1, grid=(num, steps),
            in_specs=[pl.BlockSpec((block, cols), rows), pl.BlockSpec((block, cols), rows),
                      pl.BlockSpec((1, cols, width), weight), pl.BlockSpec((1, width, cols), weight),
                      pl.BlockSpec(gate_pad.shape, lambda e, i, ids: (0, 0))],
            out_specs=[pl.BlockSpec((1, cols, width), weight), pl.BlockSpec((1, width, cols), weight)],
            scratch_shapes=[pltpu.VMEM((cols, width), F32), pltpu.VMEM((width, cols), F32)]),
        out_shape=[jax.ShapeDtypeStruct(w1.shape, BF16), jax.ShapeDtypeStruct(w2.shape, BF16)],
        compiler_params=pltpu.CompilerParams(dimension_semantics=("arbitrary", "arbitrary"), vmem_limit_bytes=48 * MIB),
        cost_estimate=pl.CostEstimate(flops=45_000_000_000, bytes_accessed=48 * MIB, transcendentals=0),
        name="expert_grads")(ids, rows_x, rows_r, w1, w2, gate_pad)


def combine_body(idx, tok, x_ref, r_ref, h_ref, g_ref, aux_ref, gate_ref, y_ref, gx_ref, part_ref,
                 y_acc, g_acc, s_acc, y_stage, g_stage, *, chunks, blocks, experts, scale):
    step = pl.program_id(0)
    picks = h_ref.shape[0]

    @pl.when(step < chunks)
    def _():
        put_rows(y_acc, step * CHUNK, x_ref[...].astype(F32))
        put_rows(g_acc, step * CHUNK, r_ref[...].astype(F32) * scale)
        s_acc[pl.ds(step * CHUNK, CHUNK), :] = jnp.zeros((CHUNK, LANES), F32)

    @pl.when((step >= chunks) & (step < chunks + blocks))
    def _():
        put_rows(y_stage, 0, h_ref[...].astype(F32) * aux_ref[:, 64:65])
        put_rows(g_stage, 0, g_ref[...].astype(F32))
        base = (step - chunks) * picks
        unroll = 8

        def body(i, carry):
            at = [idx[base + i * unroll + j] for j in range(unroll)]
            row = [tok[base + i * unroll + j] for j in range(unroll)]
            ys = [y_acc[pl.ds(at[j], 8, stride=8), :] + y_stage[pl.ds(i * 64 + j, 8, stride=8), :] for j in range(unroll)]
            gs = [g_acc[pl.ds(at[j], 8, stride=8), :] + g_stage[pl.ds(i * 64 + j, 8, stride=8), :] for j in range(unroll)]
            ss = [s_acc[pl.ds(row[j], 1), :] + aux_ref[pl.ds(i * unroll + j, 1), :] for j in range(unroll)]
            for j in range(unroll):
                y_acc[pl.ds(at[j], 8, stride=8), :] = ys[j]
                g_acc[pl.ds(at[j], 8, stride=8), :] = gs[j]
                s_acc[pl.ds(row[j], 1), :] = ss[j]
            return carry

        lax.fori_loop(0, picks // unroll, body, 0)

    @pl.when(step >= chunks + blocks)
    def _():
        start = (step - chunks - blocks) * CHUNK
        cols = x_ref.shape[1]
        x_rows = x_ref[...]
        probs, lane = softmax_rows(x_rows, gate_ref[...], experts)
        dprobs = jnp.where(lane < experts, s_acc[pl.ds(start, CHUNK), :], 0.0)
        dlogits = (probs * (dprobs - jnp.sum(probs * dprobs, axis=1, keepdims=True))).astype(BF16)
        gx_ref[...] = (get_rows(g_acc, start, CHUNK, cols) + dot_nt(dlogits, gate_ref[...])).astype(BF16)
        y = get_rows(y_acc, start, CHUNK, cols).astype(BF16)
        y_ref[...] = y
        prod = y.astype(F32) * r_ref[...].astype(F32)

        @pl.when(step == chunks + blocks)
        def _():
            part_ref[...] = jnp.zeros_like(part_ref)

        part_ref[0:experts, :] += dot_tn(dlogits, x_rows)[0:experts]
        part_ref[experts:experts + 8, :] += prod.reshape(CHUNK // 8, 8, cols).sum(axis=0)


def combine(idx, tok, x, loss_w, h, g, aux, gate_pad, picks, experts, scale):
    tokens, cols = x.shape
    chunks, blocks = tokens // CHUNK, h.shape[0] // picks
    token_map = lambda i, idx, tok: (jnp.where(i < chunks, i, jnp.maximum(i - chunks - blocks, 0)), 0)
    block_map = lambda i, idx, tok: (jnp.clip(i - chunks, 0, blocks - 1), 0)
    out_map = lambda i, idx, tok: (jnp.maximum(i - chunks - blocks, 0), 0)
    whole = lambda i, idx, tok: (0, 0)
    return pl.pallas_call(
        functools.partial(combine_body, chunks=chunks, blocks=blocks, experts=experts, scale=scale),
        grid_spec=pltpu.PrefetchScalarGridSpec(
            num_scalar_prefetch=2, grid=(2 * chunks + blocks,),
            in_specs=[pl.BlockSpec((CHUNK, cols), token_map), pl.BlockSpec((CHUNK, cols), token_map),
                      pl.BlockSpec((picks, cols), block_map), pl.BlockSpec((picks, cols), block_map),
                      pl.BlockSpec((picks, LANES), block_map), pl.BlockSpec(gate_pad.shape, whole)],
            out_specs=[pl.BlockSpec((CHUNK, cols), out_map), pl.BlockSpec((CHUNK, cols), out_map),
                       pl.BlockSpec((experts + 8, cols), whole)],
            scratch_shapes=[pltpu.VMEM((tokens * 8, LANES), F32), pltpu.VMEM((tokens * 8, LANES), F32),
                            pltpu.VMEM((tokens, LANES), F32),
                            pltpu.VMEM((picks * 8, LANES), F32), pltpu.VMEM((picks * 8, LANES), F32)]),
        out_shape=[jax.ShapeDtypeStruct(x.shape, BF16), jax.ShapeDtypeStruct(x.shape, BF16),
                   jax.ShapeDtypeStruct((experts + 8, cols), F32)],
        compiler_params=pltpu.CompilerParams(dimension_semantics=("arbitrary",), vmem_limit_bytes=58 * MIB),
        cost_estimate=pl.CostEstimate(flops=50_000_000_000, bytes_accessed=64 * MIB, transcendentals=0),
        name="combine")(idx, tok, x, loss_w, h, g, aux, gate_pad)


def rank_picks(tok, tokens, distinct):
    side = 64
    steps = jnp.arange(side)
    hi = (tok // side)[..., None] == steps
    lo = (tok % side)[..., None] == steps
    hist = jnp.einsum('tph,tpl->thl', hi.astype(BF16), lo.astype(BF16), preferred_element_type=F32)
    seen = (hist > 0).astype(BF16)
    upto = (steps[:, None] <= steps[None, :]).astype(BF16)
    within = jnp.einsum('thl,lk->thk', seen, upto, preferred_element_type=F32)
    before = jnp.sum(jnp.where(steps[None, :, None] > steps[None, None, :], within[:, None, :, -1], 0.0), axis=-1)
    count = within + before[..., None]
    row = jnp.einsum('tph,thl->tpl', hi.astype(BF16), within.astype(BF16), preferred_element_type=F32)
    start = jnp.sum(jnp.where(hi, before[:, None, :], 0.0), axis=-1)
    place = (jnp.sum(jnp.where(lo, row, 0.0), axis=-1) + start - 1.0).astype(jnp.int32)
    flat = count.reshape(tok.shape[0], 1, tokens)
    listed = jnp.sum((flat <= jnp.arange(distinct, dtype=F32)[None, :, None]).astype(jnp.int32), axis=-1)
    return listed, place


def after(value, *earlier):
    return lax.optimization_barrier((value, *earlier))[0]


def solution(mesh):
    group = mesh.shape['ep']

    def permute(value, mask):
        return lax.ppermute(value, 'ep', [(i, i ^ mask) for i in range(group)])

    def dispatch(rows):
        size = rows.shape[0] // group
        return [rows[:size]] + [permute(rows[m * size:(m + 1) * size], m) for m in range(1, group)]

    def device_step(x, gate_w, up_w, down_w, expert_picks, loss_w):
        tokens, cols = x.shape
        experts = gate_w.shape[1]
        local, capacity = expert_picks.shape
        picks = capacity // group
        distinct = local * picks // 2
        scale = 1.0 / math.sqrt(tokens * group * cols)
        me = lax.axis_index('ep')
        order = me ^ jnp.arange(group)
        gate_pad = jnp.pad(gate_w, ((0, 0), (0, LANES - experts)))

        wanted = expert_picks.reshape(local, group, picks)
        asked = lax.all_to_all(wanted, 'ep', 1, 1, tiled=True) - me * tokens
        asked = jnp.take(asked, order, axis=1).transpose(1, 0, 2)
        wanted = (jnp.take(wanted, order, axis=1) - (order * tokens)[None, :, None]).transpose(1, 0, 2)

        half = local // 2
        part_a = after((up_w[:half], down_w[:half]), asked)
        xa, ya = [permute(v, 2) for v in part_a], [permute(v, 4) for v in part_a]
        partner = [permute(up_w, 1), permute(down_w, 1)]

        send_list, _ = rank_picks(asked.reshape(group, -1), tokens, distinct)
        send_idx = row_base(send_list).reshape(-1)
        send_x = gather_rows(send_idx, [x], group * distinct)
        send_r = gather_rows(after(send_idx, send_x), [loss_w], group * distinct)
        got_x, got_r = dispatch(send_x), dispatch(send_r)

        part_b = after((up_w[half:], down_w[half:]), send_r)
        xb, yb = [permute(v, 2) for v in part_b], [permute(v, 4) for v in part_b]

        own_tok = asked.reshape(-1)
        own_idx = row_base(own_tok)
        own_ids = (order[:, None] * local + jnp.arange(local)[None, :]).reshape(-1)
        picked_x = gather_rows(after(own_idx, send_r), [x], experts * picks)
        picked_r = gather_rows(after(own_idx, picked_x), [loss_w], experts * picks)

        def relay(vx, vy):
            return [permute(vx[0], 4), permute(vy[1], 2)]

        da, db = relay(xa, ya), relay(xb, yb)
        xa1, ya1, xb1, yb1, da1, db1 = ([permute(v, 1) for v in vs] for vs in (xa, ya, xb, yb, da, db))

        def owner(bufs, first, weights):
            ids = after(own_ids, bufs[2]) if bufs else own_ids
            return owner_group(ids, picked_x, picked_r, *weights, gate_pad, bufs, first, picks, experts, scale)

        bufs = owner([], 0, (up_w, down_w))
        bufs = owner(bufs, local, partner)
        for m, weights in ((2, xa), (4, ya), (3, xa1), (5, ya1)):
            bufs = owner(bufs, m * local, weights)

        _, place = rank_picks(wanted.reshape(group, -1), tokens, distinct)
        rows_idx = row_base(place.reshape(group, local, picks) + jnp.arange(group)[:, None, None] * distinct)
        rows_idx = rows_idx.transpose(1, 0, 2).reshape(-1)
        my_ids = me * local + jnp.arange(local)
        rows_x = gather_rows(after(rows_idx, bufs[2]), got_x, local * capacity)
        rows_r = gather_rows(after(rows_idx, rows_x), got_r, local * capacity)
        grad_up, grad_down = expert_grads(my_ids, rows_x, rows_r, up_w, down_w, gate_pad, experts, scale)

        own_ids = after(own_ids, grad_down)
        for m, weights in ((2, xb), (4, yb), (3, xb1), (5, yb1)):
            bufs = owner(bufs, m * local + half, weights)
        for m, start, weights in ((6, 0, da), (7, 0, da1), (6, half, db), (7, half, db1)):
            bufs = owner(bufs, m * local + start, weights)

        y, grad_x, part = combine(own_idx, own_tok, x, loss_w, *bufs, gate_pad, picks, experts, scale)
        for mask in (1, 2, 4):
            part = part + permute(part, mask)
        return y, jnp.sum(part[experts:]) * scale, grad_x, grad_up, grad_down, part[:experts].T

    return jax.shard_map(device_step, mesh=mesh,
                         in_specs=(P('ep'), P(), P('ep'), P('ep'), P('ep'), P('ep')),
                         out_specs=(P('ep'), P(), P('ep'), P('ep'), P('ep'), P()),
                         check_vma=False)
```

time: 1270 us -> 845 us (0.67)
  blocking collectives: 440 us -> 0 us
  Pallas kernels: 0 us -> 358 us
  other arithmetic: 295 us -> 11.8 us
  waiting for transfers between devices: 118 us -> 386 us
  local copies, waits for them, and re-layouts: 238 us -> 39.6 us
  matrix products: 134 us -> 2.72 us
  starting transfers between devices: 14.1 us -> 34.2 us
  between operations: 16.6 us -> 3.23 us
    ppermute x0 -> x43, waiting for transfers between devices: none -> 384 us  [permute(): return lax.ppermute(value, 'ep', [(i, i ^ mask) for i in range(group)])]
    all_to_all x2 -> x0, blocking collectives: 371 us -> none  [the longest x1 186 us: device_step(): lax.all_to_all(grad_out, 'ep', 1, 1, tiled=True)]
    pallas_call x0 -> x22, Pallas kernels: none -> 358 us  [the longest x6 115 us: gather_rows(): pl.pallas_call(functools.partial(gather_body, num_src=len(srcs), rows=row...]
    scatter-add x2 -> x0, other arithmetic: 165 us -> none  [the longest x1 82.4 us: device_step(): jax.ops.segment_sum((gate_vals[..., None] * out_back).reshape(-1, hidden)...]
    gather x6 -> x2, local copies, waits for them, and re-layouts: 164 us -> 1.93 us  [the longest x1 1.36 us: device_step(): jnp.take(wanted, order, axis=1) - (order * tokens)[None, :, None]]
    dot_general x9 -> x5, matrix products: 134 us -> 2.72 us  [the longest x2 1.44 us: rank_picks(): jnp.einsum('tph,tpl->thl', hi.astype(BF16), lo.astype(BF16), preferred_el...]
    all_to_all x3 -> x1, waiting for transfers between devices: 118 us -> 2.21 us  [device_step(): asked = lax.all_to_all(wanted, 'ep', 1, 1, tiled=True) - me * tokens]
    psum x1 -> x0, blocking collectives: 68.8 us -> none  [device_step(): lax.psum(jnp.sum(y.astype(jnp.float32) * weight_f32), 'ep') * loss_scale]
  transfers between devices with their start and end apart: 4 -> 44, of which waited for: 2 -> 18; matrix products, arithmetic and copies ran while one was open for 29% -> 2% of each run, Pallas kernels for 0% -> 30%
where the time goes in v1:
time: 845 us; the launch traced here: 836 us
  waiting for transfers between devices  386 us (46%)
  Pallas kernels  358 us (42%)
  local copies, waits for them, and re-layouts  39.6 us (5%)
  starting transfers between devices  34.2 us (4%)
  other arithmetic  11.8 us (1%)
    ppermute x43, waiting for transfers between devices, permute(): return lax.ppermute(value, 'ep', [(i, i ^ mask) for i in range(group)])  384 us
    pallas_call x6, Pallas kernels, gather_rows(): pl.pallas_call(functools.partial(gather_body, num_src=len(srcs), rows=row...  115 us
    pallas_call x14, Pallas kernels, owner_group(): pl.pallas_call(functools.partial(owner_body, first=first, experts=experts...  99.1 us
    pallas_call x1, Pallas kernels, combine(): pl.pallas_call(functools.partial(combine_body, chunks=chunks, blocks=bloc...  81.7 us
    pallas_call x1, Pallas kernels, expert_grads(): pl.pallas_call(functools.partial(expert_body, experts=experts, scale=scal...  61.6 us
    ppermute x43, starting transfers between devices, permute(): return lax.ppermute(value, 'ep', [(i, i ^ mask) for i in range(group)])  29.9 us
    unnamed x82, local copies, waits for them, and re-layouts  25.3 us
  transfers between devices with their start and end apart: 44, of which 18 were waited for; matrix products, arithmetic and copies ran while one was open for 2% of the time, Pallas kernels for 30%

profile of v1, /device:TPU:0, one launch (start us, length us, event | category | flops | bytes accessed | tf_op | source)
XLA Modules:
  0.0 835.6 jit_solution(3615440030299297165)
XLA Ops:
  0.6 4.3 all-to-all-start
  5.0 1.4 gather_fusion.1
  7.5 2.2 all-to-all-done
  12.0 8.8 %convert_reduce_fusion = s32[8,512]{1,0:T(8,128)S(1)} fusion(f32[8,4096]{1,0:T(8,128)S(1)} %le.48), kind=kLoop, calls=%fused_computation.2 | loop fusion | flops 50327552 | bytes 147456 | tf_op jit(solution)/shard_map/reduce_sum | solution.py:300
  20.8 15.3 %shard_map.109 = bf16[4096,1024]{1,0:T(8,128)(2,1)S(1)} custom-call(s32[4096]{0:T(1024)S(1)} %bitcast.38, bf16[4096,1024]{1,0:T(8,128)(2,1)} %x_ref.1), custom_call_target="tpu_custom_call" | custom-call | flops 4096000000 | bytes 16777216 | tf_op jit(solution)/shard_map/pallas_call | solution.py:72
  36.1 1.5 fusion.32
  38.3 1.3 collective-permute-start.12
  41.2 15.3 %shard_map.110 = bf16[4096,1024]{1,0:T(8,128)(2,1)S(1)} custom-call(s32[4096]{0:T(1024)S(1)} %bitcast.39, bf16[4096,1024]{1,0:T(8,128)(2,1)} %r_ref.1), custom_call_target="tpu_custom_call" | custom-call | flops 4096000000 | bytes 16777216 | tf_op jit(solution)/shard_map/pallas_call | solution.py:72
  57.3 6.4 collective-permute-done.11.refs_2_
  63.8 1.9 fusion.31
  65.6 19.6 %collective-permute-done.12.refs_3_ = bf16[512,1024]{1,0:T(8,128)(2,1)S(1)} collective-permute-done((bf16[512,1024]{1,0:T(8,128)(2,1)S(1)}, bf16[512,1024]{1,0:T(8,128)(2,1)S(1)}, u32[]{:S(2)}, u32[]{:S(2)}) %collective-permute-start.12) | collective-permute-done | bytes 1048608 | tf_op jit(solution)/shard_map/ppermute | solution.py:312
  86.9 44.8 %collective-permute-done.14.refs_5_ = bf16[512,1024]{1,0:T(8,128)(2,1)S(1)} collective-permute-done((bf16[512,1024]{1,0:T(8,128)(2,1)S(1)}, bf16[512,1024]{1,0:T(8,128)(2,1)S(1)}, u32[]{:S(2)}, u32[]{:S(2)}) %collective-permute-start.14) | collective-permute-done | bytes 1048608 | tf_op jit(solution)/shard_map/ppermute | solution.py:312
  132.6 3.8 fusion.34
  136.5 4.0 fusion.33
  146.0 7.7 collective-permute-done.18.refs_2_
  155.2 20.0 %collective-permute-done.19.refs_3_ = bf16[512,1024]{1,0:T(8,128)(2,1)S(1)} collective-permute-done((bf16[512,1024]{1,0:T(8,128)(2,1)S(1)}, bf16[512,1024]{1,0:T(8,128)(2,1)S(1)}, u32[]{:S(2)}, u32[]{:S(2)}) %collective-permute-start.19) | collective-permute-done | bytes 1048608 | tf_op jit(solution)/shard_map/ppermute | solution.py:312
  177.7 1.5 collective-permute-start.22
  179.2 9.2 %collective-permute-done.21.refs_5_ = bf16[512,1024]{1,0:T(8,128)(2,1)S(1)} collective-permute-done((bf16[512,1024]{1,0:T(8,128)(2,1)S(1)}, bf16[512,1024]{1,0:T(8,128)(2,1)S(1)}, u32[]{:S(2)}, u32[]{:S(2)}) %collective-permute-start.21) | collective-permute-done | bytes 1048608 | tf_op jit(solution)/shard_map/ppermute | solution.py:312
  189.4 2.8 collective-permute-start.23
  192.2 96.3 %collective-permute-done.22.refs_6_ = bf16[512,1024]{1,0:T(8,128)(2,1)S(1)} collective-permute-done((bf16[512,1024]{1,0:T(8,128)(2,1)S(1)}, bf16[512,1024]{1,0:T(8,128)(2,1)S(1)}, u32[]{:S(2)}, u32[]{:S(2)}) %collective-permute-start.22) | collective-permute-done | bytes 1048608 | tf_op jit(solution)/shard_map/ppermute | solution.py:312
  289.5 1.5 collective-permute-start.5
  290.9 19.1 %collective-permute-done.23.refs_7_ = bf16[512,1024]{1,0:T(8,128)(2,1)S(1)} collective-permute-done((bf16[512,1024]{1,0:T(8,128)(2,1)S(1)}, bf16[512,1024]{1,0:T(8,128)(2,1)S(1)}, u32[]{:S(2)}, u32[]{:S(2)}) %collective-permute-start.23) | collective-permute-done | bytes 1048608 | tf_op jit(solution)/shard_map/ppermute | solution.py:312
  312.2 1.4 collective-permute-start.25
  313.6 41.9 %collective-permute-done.5.w2_ref = bf16[2,512,1024]{2,1,0:T(8,128)(2,1)} collective-permute-done((bf16[2,512,1024]{2,1,0:T(8,128)(2,1)S(1)}, bf16[2,512,1024]{2,1,0:T(8,128)(2,1)}, u32[]{:S(2)}, u32[]{:S(2)}) %collective-permute-start.5) | collective-permute-done | bytes 2097184 | tf_op jit(solution)/shard_map/ppermute | solution.py:312
  355.5 1.5 collective-permute-start.26
  357.0 2.9 collective-permute-done.24.w1_ref
  359.9 1.5 collective-permute-start.27
  361.3 42.8 %collective-permute-done.25.w2_ref = bf16[2,512,1024]{2,1,0:T(8,128)(2,1)} collective-permute-done((bf16[2,512,1024]{2,1,0:T(8,128)(2,1)}, bf16[2,512,1024]{2,1,0:T(8,128)(2,1)}, u32[]{:S(2)}, u32[]{:S(2)}) %collective-permute-start.25) | collective-permute-done | bytes 2097184 | tf_op jit(solution)/shard_map/ppermute | solution.py:312
  406.8 41.6 %collective-permute-done.27.w2_ref = bf16[2,512,1024]{2,1,0:T(8,128)(2,1)} collective-permute-done((bf16[2,512,1024]{2,1,0:T(8,128)(2,1)}, bf16[2,512,1024]{2,1,0:T(8,128)(2,1)}, u32[]{:S(2)}, u32[]{:S(2)}) %collective-permute-start.27) | collective-permute-done | bytes 2097184 | tf_op jit(solution)/shard_map/ppermute | solution.py:312
  449.4 3.4 copy-done.2
  452.7 21.1 %shard_map.111.x_ref = bf16[8192,1024]{1,0:T(8,128)(2,1)} custom-call(s32[8192]{0:T(1024)S(1)} %and_or_fusion.idx, bf16[4096,1024]{1,0:T(8,128)(2,1)S(1)} %copy-done.2), custom_call_target="tpu_custom_call" | custom-call | flops 8192000000 | bytes 33554432 | tf_op jit(solution)/shard_map/pallas_call | solution.py:72
  473.8 3.4 copy-done.3
  477.2 21.5 %shard_map.112.r_ref = bf16[8192,1024]{1,0:T(8,128)(2,1)} custom-call(s32[8192]{0:T(1024)S(1)} %and_or_fusion.idx, bf16[4096,1024]{1,0:T(8,128)(2,1)S(1)} %copy-done.3), custom_call_target="tpu_custom_call" | custom-call | flops 8192000000 | bytes 33554432 | tf_op jit(solution)/shard_map/pallas_call | solution.py:72
  498.8 10.4 %shard_map.113 = (bf16[8192,1024]{1,0:T(8,128)(2,1)}, bf16[8192,1024]{1,0:T(8,128)(2,1)}, f32[8192,128]{1,0:T(8,128)S(1)}) custom-call(s32[32]{0:T(128)S(1)} %add.92.ids, bf16[8192,1024]{1,0:T(8,128)(2,1)} %shard_map.111.x_ref, bf16[8192,1024]{1,0:T(8,128)(2,1)} %shard_map.112.r_ref, bf16[4,1024,512]{2,1,0:T(8,128)(2,1)} %w1_ref.3, ...), custom_call_target="tpu_custom_call" | custom-call | flops 4000000000 | bytes 16777216 | tf_op jit(solution)/shard_map/pallas_call | solution.py:146
  509.2 10.4 %shard_map.114 = (bf16[8192,1024]{1,0:T(8,128)(2,1)}, bf16[8192,1024]{1,0:T(8,128)(2,1)}, f32[8192,128]{1,0:T(8,128)S(1)}) custom-call(s32[32]{0:T(128)S(1)} %add.92.ids, bf16[8192,1024]{1,0:T(8,128)(2,1)} %shard_map.111.x_ref, bf16[8192,1024]{1,0:T(8,128)(2,1)} %shard_map.112.r_ref, ...), custom_call_target="tpu_custom_call", output_to_operand_aliasing={{0}: (6, {}), {1}: (7, {}), {2}: (8, {})} | custom-call | flops 4000000000 | bytes 16777216 | tf_op jit(solution)/shard_map/pallas_call | solution.py:146
  519.6 6.5 shard_map.115
  526.1 1.5 collective-permute-start.32
  528.9 1.3 collective-permute-start.37
  530.2 6.5 shard_map.116
  536.8 6.6 shard_map.117
  543.4 6.8 shard_map.118
  550.3 1.2 copy-done.21
  551.5 21.2 %shard_map.119.x_ref = bf16[8192,1024]{1,0:T(8,128)(2,1)} custom-call(s32[8192]{0:T(1024)S(1)} %bitcast.40, bf16[512,1024]{1,0:T(8,128)(2,1)S(1)} %get-tuple-element.164.refs_0_, bf16[512,1024]{1,0:T(8,128)(2,1)S(1)} %copy-done.9, bf16[512,1024]{1,0:T(8,128)(2,1)S(1)} %copy-done.11, bf16[512,1024]{1,0:T(8,128)(2,1)S(1)} %copy-done.13, ...), custom_call_target="tpu_custom_call" | custom-call | flops 8192000000 | bytes 33554432 | tf_op jit(solution)/shard_map/pallas_call | solution.py:72
  572.8 1.2 copy-done.23
  574.0 1.2 copy-done.25
  575.3 1.2 copy-done.27
  576.5 1.2 copy-done.29
  577.7 21.1 %shard_map.120.r_ref = bf16[8192,1024]{1,0:T(8,128)(2,1)} custom-call(s32[8192]{0:T(1024)S(1)} %bitcast.41, bf16[512,1024]{1,0:T(8,128)(2,1)S(1)} %copy-done.6, bf16[512,1024]{1,0:T(8,128)(2,1)S(1)} %copy-done.23, bf16[512,1024]{1,0:T(8,128)(2,1)S(1)} %copy-done.25, bf16[512,1024]{1,0:T(8,128)(2,1)S(1)} %copy-done.27, bf16[512,1024]{1,0:T(8,128)(2,1)S(1)} %copy-done.29, ...), custom_call_target="tpu_custom_call" | custom-call | flops 8192000000 | bytes 33554432 | tf_op jit(solution)/shard_map/pallas_call | solution.py:72
  598.8 1.3 copy-done.4
  600.8 18.1 %collective-permute-done.36.w1_ref = bf16[2,1024,512]{2,1,0:T(8,128)(2,1)} collective-permute-done((bf16[2,1024,512]{2,1,0:T(8,128)(2,1)}, bf16[2,1024,512]{2,1,0:T(8,128)(2,1)}, u32[]{:S(2)}, u32[]{:S(2)}) %collective-permute-start.36) | collective-permute-done | bytes 2097184 | tf_op jit(solution)/shard_map/ppermute | solution.py:312
  620.2 61.6 %expert_grads.1 = (bf16[4,1024,512]{2,1,0:T(8,128)(2,1)}, bf16[4,512,1024]{2,1,0:T(8,128)(2,1)}) custom-call(s32[4]{0:T(128)S(1)} %iota_add_fusion.1.ids, bf16[8192,1024]{1,0:T(8,128)(2,1)} %shard_map.119.x_ref, bf16[8192,1024]{1,0:T(8,128)(2,1)} %shard_map.120.r_ref, bf16[4,1024,512]{2,1,0:T(8,128)(2,1)} %w1_ref.3, bf16[4,512,1024]{2,1,0:T(8,128)(2,1)} %w2_ref.3, ...), custom_call_target="tpu_custom_call" | custom-call | flops 44999999488 | bytes 50331648 | tf_op jit(solution)/shard_map/expert_grads/pallas_call | solution.py:191
  681.8 6.5 shard_map.121
  688.3 6.5 shard_map.122
  694.9 6.0 shard_map.123
  700.9 6.5 shard_map.124
  707.4 6.5 shard_map.125
  713.9 6.6 shard_map.126
  720.6 6.5 shard_map.127
  727.1 6.6 shard_map.128
  733.7 2.0 copy-done
  735.6 81.7 %combine.1 = (bf16[4096,1024]{1,0:T(8,128)(2,1)}, bf16[4096,1024]{1,0:T(8,128)(2,1)}, f32[40,1024]{1,0:T(8,128)}) custom-call(s32[8192]{0:T(1024)} %copy-done.7, s32[8192]{0:T(1024)} %bitcast.48, bf16[4096,1024]{1,0:T(8,128)(2,1)} %x_ref.1, bf16[4096,1024]{1,0:T(8,128)(2,1)} %r_ref.1, bf16[8192,1024]{1,0:T(8,128)(2,1)} %get-tuple-element.140.h_ref, ...), custom_call_target="tpu_custom_call" | custom-call | flops 49999998976 | bytes 67108864 | tf_op jit(solution)/shard_map/combine/pallas_call | solution.py:266
  817.9 1.2 collective-permute-done.40
  820.7 5.9 collective-permute-done.41
  827.2 5.1 collective-permute-done.42
  (174 shorter events, 33.7 us)
Async XLA Ops:
  0.6 9.1 %all-to-all-start = ((s32[4,8,256]{2,0,1:T(4,128)}), s32[4,8,256]{2,0,1:T(4,128)S(1)}, u32[]{:S(2)}, u32[]{:S(2)}) async-start(s32[4,8,256]{2,0,1:T(4,128)} %bitcast.45), calls=%async_computation | async-start | bytes 65536 | tf_op jit(solution)/shard_map/all_to_all | solution.py:330
  37.7 18.8 %collective-permute-start.10 = (bf16[512,1024]{1,0:T(8,128)(2,1)S(1)}, bf16[512,1024]{1,0:T(8,128)(2,1)S(1)}, u32[]{:S(2)}, u32[]{:S(2)}) collective-permute-start(bf16[512,1024]{1,0:T(8,128)(2,1)S(1)} %get-tuple-element.163), channel_id=1, source_target_pairs={{0,1},{1,0},{2,3},{3,2},{4,5},{5,4},{6,7},{7,6}} | collective-permute-start | bytes 3145736 | tf_op jit(solution)/shard_map/ppermute | solution.py:312
  37.7 26.1 %collective-permute-start.11 = (bf16[512,1024]{1,0:T(8,128)(2,1)S(1)}, bf16[512,1024]{1,0:T(8,128)(2,1)S(1)}, u32[]{:S(2)}, u32[]{:S(2)}) collective-permute-start(bf16[512,1024]{1,0:T(8,128)(2,1)S(1)} %get-tuple-element.162), channel_id=1, source_target_pairs={{0,2},{1,3},{2,0},{3,1},{4,6},{5,7},{6,4},{7,5}} | collective-permute-start | bytes 3145736 | tf_op jit(solution)/shard_map/ppermute | solution.py:312
  38.3 46.9 %collective-permute-start.12 = (bf16[512,1024]{1,0:T(8,128)(2,1)S(1)}, bf16[512,1024]{1,0:T(8,128)(2,1)S(1)}, u32[]{:S(2)}, u32[]{:S(2)}) collective-permute-start(bf16[512,1024]{1,0:T(8,128)(2,1)S(1)} %get-tuple-element.161), channel_id=1, source_target_pairs={{0,3},{1,2},{2,1},{3,0},{4,7},{5,6},{6,5},{7,4}} | collective-permute-start | bytes 3145736 | tf_op jit(solution)/shard_map/ppermute | solution.py:312
  39.5 46.8 %collective-permute-start.13 = (bf16[512,1024]{1,0:T(8,128)(2,1)S(1)}, bf16[512,1024]{1,0:T(8,128)(2,1)S(1)}, u32[]{:S(2)}, u32[]{:S(2)}) collective-permute-start(bf16[512,1024]{1,0:T(8,128)(2,1)S(1)} %get-tuple-element.160), channel_id=1, source_target_pairs={{0,4},{1,5},{2,6},{3,7},{4,0},{5,1},{6,2},{7,3}} | collective-permute-start | bytes 3145736 | tf_op jit(solution)/shard_map/ppermute | solution.py:312
  40.1 91.6 %collective-permute-start.14 = (bf16[512,1024]{1,0:T(8,128)(2,1)S(1)}, bf16[512,1024]{1,0:T(8,128)(2,1)S(1)}, u32[]{:S(2)}, u32[]{:S(2)}) collective-permute-start(bf16[512,1024]{1,0:T(8,128)(2,1)S(1)} %get-tuple-element.159), channel_id=1, source_target_pairs={{0,5},{1,4},{2,7},{3,6},{4,1},{5,0},{6,3},{7,2}} | collective-permute-start | bytes 3145736 | tf_op jit(solution)/shard_map/ppermute | solution.py:312
  56.5 9.1 %copy-start.8 = (bf16[512,1024]{1,0:T(8,128)(2,1)}, bf16[512,1024]{1,0:T(8,128)(2,1)S(1)}, u32[]{:S(2)}) copy-start(bf16[512,1024]{1,0:T(8,128)(2,1)S(1)} %collective-permute-done.10.refs_1_) | copy-start | bytes 3145732
  56.5 84.0 %collective-permute-start.15 = (bf16[512,1024]{1,0:T(8,128)(2,1)S(1)}, bf16[512,1024]{1,0:T(8,128)(2,1)S(1)}, u32[]{:S(2)}, u32[]{:S(2)}) collective-permute-start(bf16[512,1024]{1,0:T(8,128)(2,1)S(1)} %get-tuple-element.158), channel_id=1, source_target_pairs={{0,6},{1,7},{2,4},{3,5},{4,2},{5,3},{6,0},{7,1}} | collective-permute-start | bytes 3145736 | tf_op jit(solution)/shard_map/ppermute | solution.py:312
  63.8 78.5 %collective-permute-start.16 = (bf16[512,1024]{1,0:T(8,128)(2,1)S(1)}, bf16[512,1024]{1,0:T(8,128)(2,1)S(1)}, u32[]{:S(2)}, u32[]{:S(2)}) collective-permute-start(bf16[512,1024]{1,0:T(8,128)(2,1)S(1)} %get-tuple-element.157), channel_id=1, source_target_pairs={{0,7},{1,6},{2,5},{3,4},{4,3},{5,2},{6,1},{7,0}} | collective-permute-start | bytes 3145736 | tf_op jit(solution)/shard_map/ppermute | solution.py:312
  85.2 51.2 %copy-start.12 = (bf16[512,1024]{1,0:T(8,128)(2,1)}, bf16[512,1024]{1,0:T(8,128)(2,1)S(1)}, u32[]{:S(2)}) copy-start(bf16[512,1024]{1,0:T(8,128)(2,1)S(1)} %collective-permute-done.12.refs_3_) | copy-start | bytes 3145732
  85.2 58.8 %collective-permute-start.17 = (bf16[512,1024]{1,0:T(8,128)(2,1)S(1)}, bf16[512,1024]{1,0:T(8,128)(2,1)S(1)}, u32[]{:S(2)}, u32[]{:S(2)}) collective-permute-start(bf16[512,1024]{1,0:T(8,128)(2,1)S(1)} %get-tuple-element.155), channel_id=1, source_target_pairs={{0,1},{1,0},{2,3},{3,2},{4,5},{5,4},{6,7},{7,6}} | collective-permute-start | bytes 3145736 | tf_op jit(solution)/shard_map/ppermute | solution.py:312
  86.3 50.1 %copy-start.14 = (bf16[512,1024]{1,0:T(8,128)(2,1)}, bf16[512,1024]{1,0:T(8,128)(2,1)S(1)}, u32[]{:S(2)}) copy-start(bf16[512,1024]{1,0:T(8,128)(2,1)S(1)} %collective-permute-done.13.refs_4_) | copy-start | bytes 3145732
  86.3 67.3 %collective-permute-start.18 = (bf16[512,1024]{1,0:T(8,128)(2,1)S(1)}, bf16[512,1024]{1,0:T(8,128)(2,1)S(1)}, u32[]{:S(2)}, u32[]{:S(2)}) collective-permute-start(bf16[512,1024]{1,0:T(8,128)(2,1)S(1)} %get-tuple-element.154), channel_id=1, source_target_pairs={{0,2},{1,3},{2,0},{3,1},{4,6},{5,7},{6,4},{7,5}} | collective-permute-start | bytes 3145736 | tf_op jit(solution)/shard_map/ppermute | solution.py:312
  131.7 4.8 copy-start.16
  131.7 43.5 %collective-permute-start.19 = (bf16[512,1024]{1,0:T(8,128)(2,1)S(1)}, bf16[512,1024]{1,0:T(8,128)(2,1)S(1)}, u32[]{:S(2)}, u32[]{:S(2)}) collective-permute-start(bf16[512,1024]{1,0:T(8,128)(2,1)S(1)} %get-tuple-element.153), channel_id=1, source_target_pairs={{0,3},{1,2},{2,1},{3,0},{4,7},{5,6},{6,5},{7,4}} | collective-permute-start | bytes 3145736 | tf_op jit(solution)/shard_map/ppermute | solution.py:312
  136.4 267.9 %copy-start.37 = (bf16[1024,32]{0,1:T(8,128)(2,1)S(1)}, bf16[1024,32]{0,1:T(8,128)(2,1)}, u32[]{:S(2)}) copy-start(bf16[1024,32]{0,1:T(8,128)(2,1)} %param.9) | copy-start | bytes 196612
  141.4 35.3 %collective-permute-start.20 = (bf16[512,1024]{1,0:T(8,128)(2,1)S(1)}, bf16[512,1024]{1,0:T(8,128)(2,1)S(1)}, u32[]{:S(2)}, u32[]{:S(2)}) collective-permute-start(bf16[512,1024]{1,0:T(8,128)(2,1)S(1)} %get-tuple-element.152), channel_id=1, source_target_pairs={{0,4},{1,5},{2,6},{3,7},{4,0},{5,1},{6,2},{7,3}} | collective-permute-start | bytes 3145736 | tf_op jit(solution)/shard_map/ppermute | solution.py:312
  143.3 45.2 %collective-permute-start.21 = (bf16[512,1024]{1,0:T(8,128)(2,1)S(1)}, bf16[512,1024]{1,0:T(8,128)(2,1)S(1)}, u32[]{:S(2)}, u32[]{:S(2)}) collective-permute-start(bf16[512,1024]{1,0:T(8,128)(2,1)S(1)} %get-tuple-element.151), channel_id=1, source_target_pairs={{0,5},{1,4},{2,7},{3,6},{4,1},{5,0},{6,3},{7,2}} | collective-permute-start | bytes 3145736 | tf_op jit(solution)/shard_map/ppermute | solution.py:312
  145.0 166.7 %collective-permute-start.2 = (bf16[2,1024,512]{2,1,0:T(8,128)(2,1)S(1)}, bf16[2,1024,512]{2,1,0:T(8,128)(2,1)}, u32[]{:S(2)}, u32[]{:S(2)}) collective-permute-start(bf16[2,1024,512]{2,1,0:T(8,128)(2,1)S(1)} %get-tuple-element.86), channel_id=1, source_target_pairs={{0,2},{1,3},{2,0},{3,1},{4,6},{5,7},{6,4},{7,5}} | collective-permute-start | bytes 6291464 | tf_op jit(solution)/shard_map/ppermute | solution.py:312
  154.6 157.2 %collective-permute-start.3 = (bf16[2,512,1024]{2,1,0:T(8,128)(2,1)S(1)}, bf16[2,512,1024]{2,1,0:T(8,128)(2,1)}, u32[]{:S(2)}, u32[]{:S(2)}) collective-permute-start(bf16[2,512,1024]{2,1,0:T(8,128)(2,1)S(1)} %get-tuple-element.87), channel_id=1, source_target_pairs={{0,2},{1,3},{2,0},{3,1},{4,6},{5,7},{6,4},{7,5}} | collective-permute-start | bytes 6291464 | tf_op jit(solution)/shard_map/ppermute | solution.py:312
  176.1 136.1 %collective-permute-start.4 = (bf16[2,1024,512]{2,1,0:T(8,128)(2,1)S(1)}, bf16[2,1024,512]{2,1,0:T(8,128)(2,1)}, u32[]{:S(2)}, u32[]{:S(2)}) collective-permute-start(bf16[2,1024,512]{2,1,0:T(8,128)(2,1)S(1)} %get-tuple-element.86), channel_id=1, source_target_pairs={{0,4},{1,5},{2,6},{3,7},{4,0},{5,1},{6,2},{7,3}} | collective-permute-start | bytes 6291464 | tf_op jit(solution)/shard_map/ppermute | solution.py:312
  177.7 110.8 %collective-permute-start.22 = (bf16[512,1024]{1,0:T(8,128)(2,1)S(1)}, bf16[512,1024]{1,0:T(8,128)(2,1)S(1)}, u32[]{:S(2)}, u32[]{:S(2)}) collective-permute-start(bf16[512,1024]{1,0:T(8,128)(2,1)S(1)} %get-tuple-element.150), channel_id=1, source_target_pairs={{0,6},{1,7},{2,4},{3,5},{4,2},{5,3},{6,0},{7,1}} | collective-permute-start | bytes 3145736 | tf_op jit(solution)/shard_map/ppermute | solution.py:312
  189.4 120.6 %collective-permute-start.23 = (bf16[512,1024]{1,0:T(8,128)(2,1)S(1)}, bf16[512,1024]{1,0:T(8,128)(2,1)S(1)}, u32[]{:S(2)}, u32[]{:S(2)}) collective-permute-start(bf16[512,1024]{1,0:T(8,128)(2,1)S(1)} %get-tuple-element.149), channel_id=1, source_target_pairs={{0,7},{1,6},{2,5},{3,4},{4,3},{5,2},{6,1},{7,0}} | collective-permute-start | bytes 3145736 | tf_op jit(solution)/shard_map/ppermute | solution.py:312
  289.5 66.0 %collective-permute-start.5 = (bf16[2,512,1024]{2,1,0:T(8,128)(2,1)S(1)}, bf16[2,512,1024]{2,1,0:T(8,128)(2,1)}, u32[]{:S(2)}, u32[]{:S(2)}) collective-permute-start(bf16[2,512,1024]{2,1,0:T(8,128)(2,1)S(1)} %get-tuple-element.87), channel_id=1, source_target_pairs={{0,4},{1,5},{2,6},{3,7},{4,0},{5,1},{6,2},{7,3}} | collective-permute-start | bytes 6291464 | tf_op jit(solution)/shard_map/ppermute | solution.py:312
  311.0 48.8 %collective-permute-start.24 = (bf16[2,1024,512]{2,1,0:T(8,128)(2,1)}, bf16[2,1024,512]{2,1,0:T(8,128)(2,1)}, u32[]{:S(2)}, u32[]{:S(2)}) collective-permute-start(bf16[2,1024,512]{2,1,0:T(8,128)(2,1)} %get-tuple-element.108), channel_id=1, source_target_pairs={{0,2},{1,3},{2,0},{3,1},{4,6},{5,7},{6,4},{7,5}} | collective-permute-start | bytes 6291464 | tf_op jit(solution)/shard_map/ppermute | solution.py:312
  311.7 136.6 %collective-permute-start = (bf16[4,1024,512]{2,1,0:T(8,128)(2,1)}, bf16[4,1024,512]{2,1,0:T(8,128)(2,1)}, u32[]{:S(2)}, u32[]{:S(2)}) collective-permute-start(bf16[4,1024,512]{2,1,0:T(8,128)(2,1)} %w1_ref.3), channel_id=1, source_target_pairs={{0,1},{1,0},{2,3},{3,2},{4,5},{5,4},{6,7},{7,6}} | collective-permute-start | bytes 12582920 | tf_op jit(solution)/shard_map/ppermute | solution.py:312
  311.8 137.0 %collective-permute-start.1 = (bf16[4,512,1024]{2,1,0:T(8,128)(2,1)}, bf16[4,512,1024]{2,1,0:T(8,128)(2,1)}, u32[]{:S(2)}, u32[]{:S(2)}) collective-permute-start(bf16[4,512,1024]{2,1,0:T(8,128)(2,1)} %w2_ref.3), channel_id=1, source_target_pairs={{0,1},{1,0},{2,3},{3,2},{4,5},{5,4},{6,7},{7,6}} | collective-permute-start | bytes 12582920 | tf_op jit(solution)/shard_map/ppermute | solution.py:312
  312.2 91.9 %collective-permute-start.25 = (bf16[2,512,1024]{2,1,0:T(8,128)(2,1)}, bf16[2,512,1024]{2,1,0:T(8,128)(2,1)}, u32[]{:S(2)}, u32[]{:S(2)}) collective-permute-start(bf16[2,512,1024]{2,1,0:T(8,128)(2,1)} %get-tuple-element.109), channel_id=1, source_target_pairs={{0,2},{1,3},{2,0},{3,1},{4,6},{5,7},{6,4},{7,5}} | collective-permute-start | bytes 6291464 | tf_op jit(solution)/shard_map/ppermute | solution.py:312
  355.5 50.7 %collective-permute-start.26 = (bf16[2,1024,512]{2,1,0:T(8,128)(2,1)}, bf16[2,1024,512]{2,1,0:T(8,128)(2,1)}, u32[]{:S(2)}, u32[]{:S(2)}) collective-permute-start(bf16[2,1024,512]{2,1,0:T(8,128)(2,1)} %get-tuple-element.108), channel_id=1, source_target_pairs={{0,4},{1,5},{2,6},{3,7},{4,0},{5,1},{6,2},{7,3}} | collective-permute-start | bytes 6291464 | tf_op jit(solution)/shard_map/ppermute | solution.py:312
  359.9 88.5 %collective-permute-start.27 = (bf16[2,512,1024]{2,1,0:T(8,128)(2,1)}, bf16[2,512,1024]{2,1,0:T(8,128)(2,1)}, u32[]{:S(2)}, u32[]{:S(2)}) collective-permute-start(bf16[2,512,1024]{2,1,0:T(8,128)(2,1)} %get-tuple-element.109), channel_id=1, source_target_pairs={{0,4},{1,5},{2,6},{3,7},{4,0},{5,1},{6,2},{7,3}} | collective-permute-start | bytes 6291464 | tf_op jit(solution)/shard_map/ppermute | solution.py:312
  404.2 44.7 %collective-permute-start.6 = (bf16[2,1024,512]{2,1,0:T(8,128)(2,1)}, bf16[2,1024,512]{2,1,0:T(8,128)(2,1)}, u32[]{:S(2)}, u32[]{:S(2)}) collective-permute-start(bf16[2,1024,512]{2,1,0:T(8,128)(2,1)} %collective-permute-done.2.w1_ref), channel_id=1, source_target_pairs={{0,1},{1,0},{2,3},{3,2},{4,5},{5,4},{6,7},{7,6}} | collective-permute-start | bytes 6291464 | tf_op jit(solution)/shard_map/ppermute | solution.py:312
  404.6 322.5 %copy-start.1 = (bf16[1024,128]{1,0:T(8,128)(2,1)}, bf16[1024,128]{1,0:T(8,128)(2,1)S(1)}, u32[]{:S(2)}) copy-start(bf16[1024,128]{1,0:T(8,128)(2,1)S(1)} %pad.4.gate_ref) | copy-start | bytes 786436
  405.5 68.3 %copy-start.36 = (s32[8,2,4,128]{3,1,2,0:T(2,128)}, s32[8,2,4,128]{3,1,2,0:T(2,128)S(1)}, u32[]{:S(2)}) copy-start(s32[8,2,4,128]{3,1,2,0:T(2,128)S(1)} %copy.56) | copy-start | bytes 98308
  406.2 67.6 %copy-start.7 = (s32[8192]{0:T(1024)}, s32[8192]{0:T(1024)S(1)}, u32[]{:S(2)}) copy-start(s32[8192]{0:T(1024)S(1)} %and_or_fusion.idx) | copy-start | bytes 98308
  406.2 119.9 %collective-permute-start.7 = (bf16[2,512,1024]{2,1,0:T(8,128)(2,1)}, bf16[2,512,1024]{2,1,0:T(8,128)(2,1)}, u32[]{:S(2)}, u32[]{:S(2)}) collective-permute-start(bf16[2,512,1024]{2,1,0:T(8,128)(2,1)} %collective-permute-done.3.w2_ref), channel_id=1, source_target_pairs={{0,1},{1,0},{2,3},{3,2},{4,5},{5,4},{6,7},{7,6}} | collective-permute-start | bytes 6291464 | tf_op jit(solution)/shard_map/ppermute | solution.py:312
  448.3 79.3 %collective-permute-start.8 = (bf16[2,1024,512]{2,1,0:T(8,128)(2,1)}, bf16[2,1024,512]{2,1,0:T(8,128)(2,1)}, u32[]{:S(2)}, u32[]{:S(2)}) collective-permute-start(bf16[2,1024,512]{2,1,0:T(8,128)(2,1)} %collective-permute-done.4.w1_ref), channel_id=1, source_target_pairs={{0,1},{1,0},{2,3},{3,2},{4,5},{5,4},{6,7},{7,6}} | collective-permute-start | bytes 6291464 | tf_op jit(solution)/shard_map/ppermute | solution.py:312
  448.3 79.9 %collective-permute-start.9 = (bf16[2,512,1024]{2,1,0:T(8,128)(2,1)}, bf16[2,512,1024]{2,1,0:T(8,128)(2,1)}, u32[]{:S(2)}, u32[]{:S(2)}) collective-permute-start(bf16[2,512,1024]{2,1,0:T(8,128)(2,1)} %collective-permute-done.5.w2_ref), channel_id=1, source_target_pairs={{0,1},{1,0},{2,3},{3,2},{4,5},{5,4},{6,7},{7,6}} | collective-permute-start | bytes 6291464 | tf_op jit(solution)/shard_map/ppermute | solution.py:312
  448.8 80.1 %collective-permute-start.28 = (bf16[2,1024,512]{2,1,0:T(8,128)(2,1)}, bf16[2,1024,512]{2,1,0:T(8,128)(2,1)S(1)}, u32[]{:S(2)}, u32[]{:S(2)}) collective-permute-start(bf16[2,1024,512]{2,1,0:T(8,128)(2,1)} %collective-permute-done.24.w1_ref), channel_id=1, source_target_pairs={{0,1},{1,0},{2,3},{3,2},{4,5},{5,4},{6,7},{7,6}} | collective-permute-start | bytes 6291464 | tf_op jit(solution)/shard_map/ppermute | solution.py:312
  448.9 80.1 %collective-permute-start.29 = (bf16[2,512,1024]{2,1,0:T(8,128)(2,1)}, bf16[2,512,1024]{2,1,0:T(8,128)(2,1)S(1)}, u32[]{:S(2)}, u32[]{:S(2)}) collective-permute-start(bf16[2,512,1024]{2,1,0:T(8,128)(2,1)} %collective-permute-done.25.w2_ref), channel_id=1, source_target_pairs={{0,1},{1,0},{2,3},{3,2},{4,5},{5,4},{6,7},{7,6}} | collective-permute-start | bytes 6291464 | tf_op jit(solution)/shard_map/ppermute | solution.py:312
  473.8 3.4 copy-start.3
  526.1 74.2 %collective-permute-start.32 = (bf16[2,1024,512]{2,1,0:T(8,128)(2,1)}, bf16[2,1024,512]{2,1,0:T(8,128)(2,1)}, u32[]{:S(2)}, u32[]{:S(2)}) collective-permute-start(bf16[2,1024,512]{2,1,0:T(8,128)(2,1)} %collective-permute-done.2.w1_ref), channel_id=1, source_target_pairs={{0,4},{1,5},{2,6},{3,7},{4,0},{5,1},{6,2},{7,3}} | collective-permute-start | bytes 6291464 | tf_op jit(solution)/shard_map/ppermute | solution.py:312
  527.6 73.0 %collective-permute-start.33 = (bf16[2,512,1024]{2,1,0:T(8,128)(2,1)}, bf16[2,512,1024]{2,1,0:T(8,128)(2,1)}, u32[]{:S(2)}, u32[]{:S(2)}) collective-permute-start(bf16[2,512,1024]{2,1,0:T(8,128)(2,1)} %collective-permute-done.5.w2_ref), channel_id=1, source_target_pairs={{0,2},{1,3},{2,0},{3,1},{4,6},{5,7},{6,4},{7,5}} | collective-permute-start | bytes 6291464 | tf_op jit(solution)/shard_map/ppermute | solution.py:312
  528.2 90.8 %collective-permute-start.36 = (bf16[2,1024,512]{2,1,0:T(8,128)(2,1)}, bf16[2,1024,512]{2,1,0:T(8,128)(2,1)}, u32[]{:S(2)}, u32[]{:S(2)}) collective-permute-start(bf16[2,1024,512]{2,1,0:T(8,128)(2,1)} %collective-permute-done.24.w1_ref), channel_id=1, source_target_pairs={{0,4},{1,5},{2,6},{3,7},{4,0},{5,1},{6,2},{7,3}} | collective-permute-start | bytes 6291464 | tf_op jit(solution)/shard_map/ppermute | solution.py:312
  528.9 69.9 %collective-permute-start.30 = (bf16[2,1024,512]{2,1,0:T(8,128)(2,1)}, bf16[2,1024,512]{2,1,0:T(8,128)(2,1)S(1)}, u32[]{:S(2)}, u32[]{:S(2)}) collective-permute-start(bf16[2,1024,512]{2,1,0:T(8,128)(2,1)} %collective-permute-done.26.w1_ref), channel_id=1, source_target_pairs={{0,1},{1,0},{2,3},{3,2},{4,5},{5,4},{6,7},{7,6}} | collective-permute-start | bytes 6291464 | tf_op jit(solution)/shard_map/ppermute | solution.py:312
  528.9 91.2 %collective-permute-start.37 = (bf16[2,512,1024]{2,1,0:T(8,128)(2,1)}, bf16[2,512,1024]{2,1,0:T(8,128)(2,1)}, u32[]{:S(2)}, u32[]{:S(2)}) collective-permute-start(bf16[2,512,1024]{2,1,0:T(8,128)(2,1)} %collective-permute-done.27.w2_ref), channel_id=1, source_target_pairs={{0,2},{1,3},{2,0},{3,1},{4,6},{5,7},{6,4},{7,5}} | collective-permute-start | bytes 6291464 | tf_op jit(solution)/shard_map/ppermute | solution.py:312
  543.3 6.9 copy-start.9
  543.3 6.9 copy-start.11
  543.4 6.9 copy-start.13
  543.4 6.9 copy-start.15
  543.4 6.9 copy-start.17
  543.4 6.9 copy-start.19
  551.5 21.3 %copy-start.6 = (bf16[512,1024]{1,0:T(8,128)(2,1)S(1)}, bf16[512,1024]{1,0:T(8,128)(2,1)}, u32[]{:S(2)}) copy-start(bf16[512,1024]{1,0:T(8,128)(2,1)} %get-tuple-element.156.refs_0_) | copy-start | bytes 3145732
  551.5 21.3 %copy-start.31 = (bf16[512,1024]{1,0:T(8,128)(2,1)S(1)}, bf16[512,1024]{1,0:T(8,128)(2,1)}, u32[]{:S(2)}) copy-start(bf16[512,1024]{1,0:T(8,128)(2,1)} %copy-done.30) | copy-start | bytes 3145732
  551.5 21.3 %copy-start.33 = (bf16[512,1024]{1,0:T(8,128)(2,1)S(1)}, bf16[512,1024]{1,0:T(8,128)(2,1)}, u32[]{:S(2)}) copy-start(bf16[512,1024]{1,0:T(8,128)(2,1)} %copy-done.32) | copy-start | bytes 3145732
  551.5 21.3 %copy-start.35 = (bf16[512,1024]{1,0:T(8,128)(2,1)S(1)}, bf16[512,1024]{1,0:T(8,128)(2,1)}, u32[]{:S(2)}) copy-start(bf16[512,1024]{1,0:T(8,128)(2,1)} %copy-done.34) | copy-start | bytes 3145732
  600.1 100.8 %collective-permute-start.31 = (bf16[2,512,1024]{2,1,0:T(8,128)(2,1)}, bf16[2,512,1024]{2,1,0:T(8,128)(2,1)}, u32[]{:S(2)}, u32[]{:S(2)}) collective-permute-start(bf16[2,512,1024]{2,1,0:T(8,128)(2,1)} %collective-permute-done.27.w2_ref), channel_id=1, source_target_pairs={{0,1},{1,0},{2,3},{3,2},{4,5},{5,4},{6,7},{7,6}} | collective-permute-start | bytes 6291464 | tf_op jit(solution)/shard_map/ppermute | solution.py:312
  600.3 113.6 %collective-permute-start.34 = (bf16[2,1024,512]{2,1,0:T(8,128)(2,1)}, bf16[2,1024,512]{2,1,0:T(8,128)(2,1)}, u32[]{:S(2)}, u32[]{:S(2)}) collective-permute-start(bf16[2,1024,512]{2,1,0:T(8,128)(2,1)} %collective-permute-done.32.w1_ref), channel_id=1, source_target_pairs={{0,1},{1,0},{2,3},{3,2},{4,5},{5,4},{6,7},{7,6}} | collective-permute-start | bytes 6291464 | tf_op jit(solution)/shard_map/ppermute | solution.py:312
  600.6 113.3 %collective-permute-start.35 = (bf16[2,512,1024]{2,1,0:T(8,128)(2,1)}, bf16[2,512,1024]{2,1,0:T(8,128)(2,1)}, u32[]{:S(2)}, u32[]{:S(2)}) collective-permute-start(bf16[2,512,1024]{2,1,0:T(8,128)(2,1)} %collective-permute-done.33.w2_ref), channel_id=1, source_target_pairs={{0,1},{1,0},{2,3},{3,2},{4,5},{5,4},{6,7},{7,6}} | collective-permute-start | bytes 6291464 | tf_op jit(solution)/shard_map/ppermute | solution.py:312
  619.0 108.1 %collective-permute-start.38 = (bf16[2,1024,512]{2,1,0:T(8,128)(2,1)}, bf16[2,1024,512]{2,1,0:T(8,128)(2,1)}, u32[]{:S(2)}, u32[]{:S(2)}) collective-permute-start(bf16[2,1024,512]{2,1,0:T(8,128)(2,1)} %collective-permute-done.36.w1_ref), channel_id=1, source_target_pairs={{0,1},{1,0},{2,3},{3,2},{4,5},{5,4},{6,7},{7,6}} | collective-permute-start | bytes 6291464 | tf_op jit(solution)/shard_map/ppermute | solution.py:312
  620.2 106.9 %collective-permute-start.39 = (bf16[2,512,1024]{2,1,0:T(8,128)(2,1)}, bf16[2,512,1024]{2,1,0:T(8,128)(2,1)}, u32[]{:S(2)}, u32[]{:S(2)}) collective-permute-start(bf16[2,512,1024]{2,1,0:T(8,128)(2,1)} %collective-permute-done.37.w2_ref), channel_id=1, source_target_pairs={{0,1},{1,0},{2,3},{3,2},{4,5},{5,4},{6,7},{7,6}} | collective-permute-start | bytes 6291464 | tf_op jit(solution)/shard_map/ppermute | solution.py:312
  694.9 6.0 copy-start.5
  817.4 1.8 collective-permute-start.40
  820.1 6.5 collective-permute-start.41
  826.6 5.6 collective-permute-start.42
  (18 other events, 23.6 us)

commit v2 on v1

--- a/solution.py
+++ b/solution.py
@@ -25,10 +25,10 @@
         tiles[pl.ds(start // 8, rows // 8), c] = value[:, c * LANES:(c + 1) * LANES].reshape(rows // 8, 8, LANES)
 
 
-def get_rows(ref, start, rows, cols):
+def get_rows(ref, start, rows, cols, first=0, wide=None):
     tiles = as_tiles(ref, cols)
-    parts = [tiles[pl.ds(start // 8, rows // 8), c].reshape(rows, LANES) for c in range(cols // LANES)]
-    return jnp.concatenate(parts, axis=1)
+    spans = range(first // LANES, (first + (wide or cols)) // LANES)
+    return jnp.concatenate([tiles[pl.ds(start // 8, rows // 8), c].reshape(rows, LANES) for c in spans], axis=1)
 
 
 def row_base(row):
@@ -111,40 +111,55 @@
     return a * half, half + (0.5 * a) * (1.0 - t * t) * (c + (3.0 * 0.044715 * c) * sq)
 
 
-def owner_body(ids, x_ref, r_ref, w1_ref, w2_ref, gate_ref, *refs, first, experts, scale):
-    h_ref, g_ref, aux_ref = refs[-3:]
-    expert = ids[first + pl.program_id(0)]
-    x_rows = x_ref[...]
-    w1, w2 = w1_ref[0], w2_ref[0]
-    probs, lane = softmax_rows(x_rows, gate_ref[...], experts)
+def owner_expert(x_rows, r_rows, w1, w2, gate_pad, expert, experts, scale):
+    probs, lane = softmax_rows(x_rows, gate_pad, experts)
     gate = jnp.sum(jnp.where(lane == expert, probs, 0.0), axis=1, keepdims=True)
     act, slope = gelu_parts(dot(x_rows, w1))
     h = dot(act.astype(BF16), w2).astype(BF16)
-    dy = r_ref[...].astype(F32) * scale
+    dy = r_rows.astype(F32) * scale
     gate_grad = jnp.sum(dy * h.astype(F32), axis=1, keepdims=True)
     dh = (gate * dy).astype(BF16)
     du = dot_nt(dh, w2).astype(BF16)
     da = (slope * du.astype(F32)).astype(BF16)
-    h_ref[...] = h
-    g_ref[...] = dot_nt(da, w1).astype(BF16)
-    aux_ref[...] = jnp.where(lane == expert, gate_grad, jnp.where(lane == 64, gate, 0.0))
-
-
-def owner_group(ids, picked_x, picked_r, w1, w2, gate_pad, bufs, first, picks, experts, scale):
-    num = w1.shape[0]
-    cols, width = w1.shape[1], w1.shape[2]
+    aux = jnp.where(lane == expert, gate_grad, jnp.where(lane == 64, gate, 0.0))
+    return h, dot_nt(da, w1).astype(BF16), aux
+
+
+def owner_body(ids, x_ref, r_ref, gate_ref, *refs, first, per, num_pairs, experts, scale):
+    weights = refs[:2 * num_pairs]
+    h_ref, g_ref, aux_ref = refs[-3:]
+    step = pl.program_id(0)
+
+    def one_expert(w1_ref, w2_ref):
+        h_ref[...], g_ref[...], aux_ref[...] = owner_expert(
+            x_ref[...], r_ref[...], w1_ref[0], w2_ref[0], gate_ref[...], ids[first + step], experts, scale)
+
+    for k in range(num_pairs):
+        if num_pairs == 1:
+            one_expert(weights[0], weights[1])
+        else:
+            pl.when(step // per == k)(functools.partial(one_expert, weights[2 * k], weights[2 * k + 1]))
+
+
+def owner_group(ids, picked_x, picked_r, pairs, gate_pad, bufs, first, picks, experts, scale):
+    per, cols, width = pairs[0][0].shape
+    num = per * len(pairs)
     total = picked_x.shape[0]
     rows = lambda i, ids: (first + i, 0)
-    weight = lambda i, ids: (i, 0, 0)
+
+    def weight(k):
+        return lambda i, ids: (jnp.clip(i - k * per, 0, per - 1), 0, 0)
+
     in_specs = [pl.BlockSpec((picks, cols), rows), pl.BlockSpec((picks, cols), rows),
-                pl.BlockSpec((1, cols, width), weight), pl.BlockSpec((1, width, cols), weight),
                 pl.BlockSpec(gate_pad.shape, lambda i, ids: (0, 0))]
+    for k in range(len(pairs)):
+        in_specs += [pl.BlockSpec((1, cols, width), weight(k)), pl.BlockSpec((1, width, cols), weight(k))]
     alias = {}
     if bufs:
+        alias = {1 + len(in_specs) + j: j for j in range(3)}
         in_specs += [pl.BlockSpec(memory_space=pl.ANY)] * 3
-        alias = {6: 0, 7: 1, 8: 2}
     return pl.pallas_call(
-        functools.partial(owner_body, first=first, experts=experts, scale=scale),
+        functools.partial(owner_body, first=first, per=per, num_pairs=len(pairs), experts=experts, scale=scale),
         grid_spec=pltpu.PrefetchScalarGridSpec(
             num_scalar_prefetch=1, grid=(num,), in_specs=in_specs,
             out_specs=[pl.BlockSpec((picks, cols), rows), pl.BlockSpec((picks, cols), rows),
@@ -152,8 +167,8 @@
         out_shape=[jax.ShapeDtypeStruct((total, cols), BF16), jax.ShapeDtypeStruct((total, cols), BF16),
                    jax.ShapeDtypeStruct((total, LANES), F32)],
         input_output_aliases=alias,
-        compiler_params=pltpu.CompilerParams(dimension_semantics=("arbitrary",), vmem_limit_bytes=40 * MIB),
-        cost_estimate=pl.CostEstimate(flops=num * 1_000_000_000, bytes_accessed=num * 4 * MIB, transcendentals=0))(ids, picked_x, picked_r, w1, w2, gate_pad, *bufs)
+        compiler_params=pltpu.CompilerParams(dimension_semantics=("arbitrary",), vmem_limit_bytes=48 * MIB),
+        cost_estimate=pl.CostEstimate(flops=num * 1_000_000_000, bytes_accessed=num * 4 * MIB, transcendentals=0))(ids, picked_x, picked_r, gate_pad, *[w for pair in pairs for w in pair], *bufs)
 
 
 def expert_body(ids, x_ref, r_ref, w1_ref, w2_ref, gate_ref, up_ref, down_ref, up_acc, down_acc, *, experts, scale):
@@ -203,83 +218,253 @@
         name="expert_grads")(ids, rows_x, rows_r, w1, w2, gate_pad)
 
 
-def combine_body(idx, tok, x_ref, r_ref, h_ref, g_ref, aux_ref, gate_ref, y_ref, gx_ref, part_ref,
-                 y_acc, g_acc, s_acc, y_stage, g_stage, *, chunks, blocks, experts, scale):
+def add_block(idx, tok, base, h_ref, g_ref, aux_ref, y_acc, g_acc, s_acc, y_stage, g_stage):
+    picks = h_ref.shape[0]
+    put_rows(y_stage, 0, h_ref[...].astype(F32) * aux_ref[:, 64:65])
+    put_rows(g_stage, 0, g_ref[...].astype(F32))
+    unroll = 16
+
+    def body(i, carry):
+        at = [pl.ds(idx[base + i * unroll + j], 8, stride=8) for j in range(unroll)]
+        staged = [pl.ds(i * (unroll * 8) + (j // 8) * 64 + j % 8, 8, stride=8) for j in range(unroll)]
+        for acc, stage in ((y_acc, y_stage), (g_acc, g_stage)):
+            sums = [acc[at[j], :] + stage[staged[j], :] for j in range(unroll)]
+            for j in range(unroll):
+                acc[at[j], :] = sums[j]
+        row = [pl.ds(tok[base + i * unroll + j], 1) for j in range(unroll)]
+        sums = [s_acc[row[j], :] + aux_ref[pl.ds(i * unroll + j, 1), :] for j in range(unroll)]
+        for j in range(unroll):
+            s_acc[row[j], :] = sums[j]
+        return carry
+
+    lax.fori_loop(0, picks // unroll, body, 0)
+
+
+def start_all(pairs, sem):
+    copies = [pltpu.make_async_copy(a, b, sem.at[k]) for k, (a, b) in enumerate(pairs)]
+    for copy in copies:
+        copy.start()
+    return copies
+
+
+def wait_all(copies):
+    for copy in copies:
+        copy.wait()
+
+
+def acc_shapes(tokens):
+    return [(tokens * 8, LANES), (tokens * 8, LANES), (tokens, LANES)]
+
+
+def combine_first_body(idx, tok, x_ref, r_ref, h_ref, g_ref, aux_ref, gate_ref, y_out, g_out, s_out, probs_ref,
+                       y_acc, g_acc, s_acc, y_stage, g_stage, sem, *, chunks, blocks, experts, scale):
     step = pl.program_id(0)
-    picks = h_ref.shape[0]
 
     @pl.when(step < chunks)
     def _():
         put_rows(y_acc, step * CHUNK, x_ref[...].astype(F32))
         put_rows(g_acc, step * CHUNK, r_ref[...].astype(F32) * scale)
         s_acc[pl.ds(step * CHUNK, CHUNK), :] = jnp.zeros((CHUNK, LANES), F32)
-
-    @pl.when((step >= chunks) & (step < chunks + blocks))
-    def _():
-        put_rows(y_stage, 0, h_ref[...].astype(F32) * aux_ref[:, 64:65])
-        put_rows(g_stage, 0, g_ref[...].astype(F32))
-        base = (step - chunks) * picks
-        unroll = 8
-
-        def body(i, carry):
-            at = [idx[base + i * unroll + j] for j in range(unroll)]
-            row = [tok[base + i * unroll + j] for j in range(unroll)]
-            ys = [y_acc[pl.ds(at[j], 8, stride=8), :] + y_stage[pl.ds(i * 64 + j, 8, stride=8), :] for j in range(unroll)]
-            gs = [g_acc[pl.ds(at[j], 8, stride=8), :] + g_stage[pl.ds(i * 64 + j, 8, stride=8), :] for j in range(unroll)]
-            ss = [s_acc[pl.ds(row[j], 1), :] + aux_ref[pl.ds(i * unroll + j, 1), :] for j in range(unroll)]
-            for j in range(unroll):
-                y_acc[pl.ds(at[j], 8, stride=8), :] = ys[j]
-                g_acc[pl.ds(at[j], 8, stride=8), :] = gs[j]
-                s_acc[pl.ds(row[j], 1), :] = ss[j]
-            return carry
-
-        lax.fori_loop(0, picks // unroll, body, 0)
-
-    @pl.when(step >= chunks + blocks)
-    def _():
-        start = (step - chunks - blocks) * CHUNK
-        cols = x_ref.shape[1]
-        x_rows = x_ref[...]
-        probs, lane = softmax_rows(x_rows, gate_ref[...], experts)
-        dprobs = jnp.where(lane < experts, s_acc[pl.ds(start, CHUNK), :], 0.0)
-        dlogits = (probs * (dprobs - jnp.sum(probs * dprobs, axis=1, keepdims=True))).astype(BF16)
-        gx_ref[...] = (get_rows(g_acc, start, CHUNK, cols) + dot_nt(dlogits, gate_ref[...])).astype(BF16)
-        y = get_rows(y_acc, start, CHUNK, cols).astype(BF16)
-        y_ref[...] = y
-        prod = y.astype(F32) * r_ref[...].astype(F32)
-
-        @pl.when(step == chunks + blocks)
-        def _():
-            part_ref[...] = jnp.zeros_like(part_ref)
-
-        part_ref[0:experts, :] += dot_tn(dlogits, x_rows)[0:experts]
-        part_ref[experts:experts + 8, :] += prod.reshape(CHUNK // 8, 8, cols).sum(axis=0)
-
-
-def combine(idx, tok, x, loss_w, h, g, aux, gate_pad, picks, experts, scale):
+        probs_ref[...] = softmax_rows(x_ref[...], gate_ref[...], experts)[0]
+
+    @pl.when(step >= chunks)
+    def _():
+        add_block(idx, tok, (step - chunks) * h_ref.shape[0], h_ref, g_ref, aux_ref, y_acc, g_acc, s_acc, y_stage, g_stage)
+
+    @pl.when(step == chunks + blocks - 1)
+    def _():
+        wait_all(start_all(((y_acc, y_out), (g_acc, g_out), (s_acc, s_out)), sem))
+
+
+def combine_first(idx, tok, x, loss_w, h, g, aux, gate_pad, picks, blocks, experts, scale):
     tokens, cols = x.shape
-    chunks, blocks = tokens // CHUNK, h.shape[0] // picks
-    token_map = lambda i, idx, tok: (jnp.where(i < chunks, i, jnp.maximum(i - chunks - blocks, 0)), 0)
-    block_map = lambda i, idx, tok: (jnp.clip(i - chunks, 0, blocks - 1), 0)
-    out_map = lambda i, idx, tok: (jnp.maximum(i - chunks - blocks, 0), 0)
-    whole = lambda i, idx, tok: (0, 0)
+    chunks = tokens // CHUNK
+    token_map = lambda i, idx, tok: (jnp.minimum(i, chunks - 1), 0)
+    block_map = lambda i, idx, tok: (jnp.maximum(i - chunks, 0), 0)
     return pl.pallas_call(
-        functools.partial(combine_body, chunks=chunks, blocks=blocks, experts=experts, scale=scale),
+        functools.partial(combine_first_body, chunks=chunks, blocks=blocks, experts=experts, scale=scale),
         grid_spec=pltpu.PrefetchScalarGridSpec(
-            num_scalar_prefetch=2, grid=(2 * chunks + blocks,),
+            num_scalar_prefetch=2, grid=(chunks + blocks,),
             in_specs=[pl.BlockSpec((CHUNK, cols), token_map), pl.BlockSpec((CHUNK, cols), token_map),
                       pl.BlockSpec((picks, cols), block_map), pl.BlockSpec((picks, cols), block_map),
-                      pl.BlockSpec((picks, LANES), block_map), pl.BlockSpec(gate_pad.shape, whole)],
-            out_specs=[pl.BlockSpec((CHUNK, cols), out_map), pl.BlockSpec((CHUNK, cols), out_map),
-                       pl.BlockSpec((experts + 8, cols), whole)],
-            scratch_shapes=[pltpu.VMEM((tokens * 8, LANES), F32), pltpu.VMEM((tokens * 8, LANES), F32),
-                            pltpu.VMEM((tokens, LANES), F32),
-                            pltpu.VMEM((picks * 8, LANES), F32), pltpu.VMEM((picks * 8, LANES), F32)]),
+                      pl.BlockSpec((picks, LANES), block_map), pl.BlockSpec(gate_pad.shape, lambda i, idx, tok: (0, 0))],
+            out_specs=[pl.BlockSpec(memory_space=pl.ANY)] * 3 + [pl.BlockSpec((CHUNK, LANES), token_map)],
+            scratch_shapes=[pltpu.VMEM(s, F32) for s in acc_shapes(tokens)]
+            + [pltpu.VMEM((picks * 8, LANES), F32)] * 2 + [pltpu.SemaphoreType.DMA((3,))]),
+        out_shape=[jax.ShapeDtypeStruct(s, F32) for s in acc_shapes(tokens) + [(tokens, LANES)]],
+        compiler_params=pltpu.CompilerParams(dimension_semantics=("arbitrary",), vmem_limit_bytes=56 * MIB),
+        cost_estimate=pl.CostEstimate(flops=30_000_000_000, bytes_accessed=64 * MIB, transcendentals=0),
+        name="combine_first")(idx, tok, x, loss_w, h, g, aux, gate_pad)
+
+
+def combine_mid_body(idx, tok, h_ref, g_ref, aux_ref, y_in, g_in, s_in, y_out, g_out, s_out,
+                     y_acc, g_acc, s_acc, y_stage, g_stage, sem, *, first, blocks):
+    step = pl.program_id(0)
+
+    @pl.when(step == 0)
+    def _():
+        wait_all(start_all(((y_in, y_acc), (g_in, g_acc), (s_in, s_acc)), sem))
+
+    add_block(idx, tok, (first + step) * h_ref.shape[0], h_ref, g_ref, aux_ref, y_acc, g_acc, s_acc, y_stage, g_stage)
+
+    @pl.when(step == blocks - 1)
+    def _():
+        wait_all(start_all(((y_acc, y_out), (g_acc, g_out), (s_acc, s_out)), sem))
+
+
+def combine_mid(idx, tok, h, g, aux, accs, picks, first, blocks):
+    cols, tokens = h.shape[1], accs[2].shape[0]
+    block_map = lambda i, idx, tok: (first + i, 0)
+    return pl.pallas_call(
+        functools.partial(combine_mid_body, first=first, blocks=blocks),
+        grid_spec=pltpu.PrefetchScalarGridSpec(
+            num_scalar_prefetch=2, grid=(blocks,),
+            in_specs=[pl.BlockSpec((picks, cols), block_map), pl.BlockSpec((picks, cols), block_map),
+                      pl.BlockSpec((picks, LANES), block_map)] + [pl.BlockSpec(memory_space=pl.ANY)] * 3,
+            out_specs=[pl.BlockSpec(memory_space=pl.ANY)] * 3,
+            scratch_shapes=[pltpu.VMEM(s, F32) for s in acc_shapes(tokens)]
+            + [pltpu.VMEM((picks * 8, LANES), F32)] * 2 + [pltpu.SemaphoreType.DMA((3,))]),
+        out_shape=[jax.ShapeDtypeStruct(s, F32) for s in acc_shapes(tokens)],
+        compiler_params=pltpu.CompilerParams(dimension_semantics=("arbitrary",), vmem_limit_bytes=56 * MIB),
+        cost_estimate=pl.CostEstimate(flops=20_000_000_000, bytes_accessed=64 * MIB, transcendentals=0),
+        name="combine_mid")(idx, tok, h, g, aux, *accs)
+
+
+DEPTH = 3
+
+
+def combine_last_body(ids, idx, tok, px_ref, pr_ref, w1_ref, w2_ref, gate_ref, h_ref, g_ref, aux_ref,
+                      x_in, r_in, y_in, g_in, s_in, probs_in, y_out, gx_out, part_ref,
+                      y_acc, g_acc, s_acc, y_stage, g_stage, h_own, g_own, aux_own, probs, dlogits, sem,
+                      x_buf, r_buf, y_buf, gx_buf, in_sem, out_sem,
+                      *, own_first, own, first, blocks, experts, scale):
+    step = pl.program_id(0)
+    picks = h_ref.shape[0]
+    loads = ((y_in, y_acc), (g_in, g_acc), (s_in, s_acc), (probs_in, probs))
+    state = (y_acc, g_acc, s_acc, y_stage, g_stage)
+    rows, cols = x_buf.shape[1:]
+    lead = 2 * own + blocks
+    passes = x_in.shape[0] // rows
+
+    def fetch(k):
+        at, slot = pl.ds(pl.multiple_of(k * rows, rows), rows), lax.rem(k, DEPTH)
+        return [pltpu.make_async_copy(x_in.at[at], x_buf.at[slot], in_sem.at[0, slot]),
+                pltpu.make_async_copy(r_in.at[at], r_buf.at[slot], in_sem.at[1, slot])]
+
+    def flush(k):
+        at, slot = pl.ds(pl.multiple_of(k * rows, rows), rows), lax.rem(k, DEPTH)
+        return [pltpu.make_async_copy(y_buf.at[slot], y_out.at[at], out_sem.at[0, slot]),
+                pltpu.make_async_copy(gx_buf.at[slot], gx_out.at[at], out_sem.at[1, slot])]
+
+    @pl.when(step == 0)
+    def _():
+        start_all(loads, sem)
+
+    @pl.when(step < own)
+    def _():
+        h_own[step], g_own[step], aux_own[step] = owner_expert(
+            px_ref[...], pr_ref[...], w1_ref[0], w2_ref[0], gate_ref[...], ids[own_first + step], experts, scale)
+
+    @pl.when(step == own)
+    def _():
+        wait_all([pltpu.make_async_copy(a, b, sem.at[k]) for k, (a, b) in enumerate(loads)])
+
+    @pl.when((step >= own) & (step < 2 * own))
+    def _():
+        k = step - own
+        add_block(idx, tok, (own_first + k) * picks, h_own.at[k], g_own.at[k], aux_own.at[k], *state)
+
+    @pl.when((step >= 2 * own) & (step < 2 * own + blocks))
+    def _():
+        add_block(idx, tok, (first + step - 2 * own) * picks, h_ref, g_ref, aux_ref, *state)
+
+    @pl.when(step == lead - 1)
+    def _():
+        for k in range(DEPTH - 1):
+            for copy in fetch(k):
+                copy.start()
+
+    def one_pass(k, carry):
+        slot = lax.rem(k, DEPTH)
+        start = pl.multiple_of(k * rows, rows)
+
+        @pl.when(k + DEPTH - 1 < passes)
+        def _():
+            for copy in fetch(k + DEPTH - 1):
+                copy.start()
+
+        @pl.when(k >= DEPTH)
+        def _():
+            wait_all(flush(k - DEPTH))
+
+        wait_all(fetch(k))
+        dl = dlogits[pl.ds(start, rows), :]
+        part_ref[0:experts, :] += dot_tn(dl, x_buf[slot])[0:experts]
+        wide = 256
+        for c in range(0, cols, wide):
+            at = pl.ds(c, wide)
+            extra = dot_nt(dl, gate_ref[at, :])
+            gx_buf[slot, :, at] = (get_rows(g_acc, start, rows, cols, c, wide) + extra).astype(BF16)
+            y = get_rows(y_acc, start, rows, cols, c, wide).astype(BF16)
+            y_buf[slot, :, at] = y
+            prod = y.astype(F32) * r_buf[slot, :, at].astype(F32)
+            part_ref[experts:experts + 8, at] += prod.reshape(rows // 8, 8, wide).sum(axis=0)
+        for copy in flush(k):
+            copy.start()
+        return carry
+
+    @pl.when(step == lead)
+    def _():
+        part_ref[...] = jnp.zeros_like(part_ref)
+        live = lax.broadcasted_iota(jnp.int32, (CHUNK, LANES), 1) < experts
+
+        def softmax_grad(k, carry):
+            at = pl.ds(pl.multiple_of(k * CHUNK, CHUNK), CHUNK)
+            p = probs[at, :]
+            dp = jnp.where(live, s_acc[at, :], 0.0)
+            dlogits[at, :] = (p * (dp - jnp.sum(p * dp, axis=1, keepdims=True))).astype(BF16)
+            return carry
+
+        lax.fori_loop(0, x_in.shape[0] // CHUNK, softmax_grad, 0)
+        lax.fori_loop(0, passes, one_pass, 0)
+        for late in range(DEPTH):
+            wait_all(flush(passes - DEPTH + late))
+
+
+def combine_last(ids, idx, tok, x, loss_w, picked_x, picked_r, w1, w2, h, g, aux, gate_pad, accs, probs, picks, first, experts, scale):
+    tokens, cols = x.shape
+    rows = 256
+    own, width = w1.shape[0], w1.shape[2]
+    own_first = h.shape[0] // picks - own
+    blocks = own_first - first
+    lead = 2 * own + blocks
+    own_map = lambda i, *_: (own_first + jnp.minimum(i, own - 1), 0)
+    weight_map = lambda i, *_: (jnp.minimum(i, own - 1), 0, 0)
+    block_map = lambda i, *_: (first + jnp.clip(i - 2 * own, 0, blocks - 1), 0)
+    whole = lambda i, *_: (0, 0)
+    return pl.pallas_call(
+        functools.partial(combine_last_body, own_first=own_first, own=own, first=first, blocks=blocks,
+                          experts=experts, scale=scale),
+        grid_spec=pltpu.PrefetchScalarGridSpec(
+            num_scalar_prefetch=3, grid=(lead + 1,),
+            in_specs=[pl.BlockSpec((picks, cols), own_map), pl.BlockSpec((picks, cols), own_map),
+                      pl.BlockSpec((1, cols, width), weight_map), pl.BlockSpec((1, width, cols), weight_map),
+                      pl.BlockSpec(gate_pad.shape, whole),
+                      pl.BlockSpec((picks, cols), block_map), pl.BlockSpec((picks, cols), block_map),
+                      pl.BlockSpec((picks, LANES), block_map)]
+            + [pl.BlockSpec(memory_space=pl.ANY)] * 6,
+            out_specs=[pl.BlockSpec(memory_space=pl.ANY)] * 2 + [pl.BlockSpec((experts + 8, cols), whole)],
+            scratch_shapes=[pltpu.VMEM(s, F32) for s in acc_shapes(tokens)]
+            + [pltpu.VMEM((picks * 8, LANES), F32)] * 2
+            + [pltpu.VMEM((own, picks, cols), BF16)] * 2 + [pltpu.VMEM((own, picks, LANES), F32)]
+            + [pltpu.VMEM((tokens, LANES), F32), pltpu.VMEM((tokens, LANES), BF16)]
+            + [pltpu.SemaphoreType.DMA((4,))] + [pltpu.VMEM((DEPTH, rows, cols), BF16)] * 4
+            + [pltpu.SemaphoreType.DMA((2, DEPTH))] * 2),
         out_shape=[jax.ShapeDtypeStruct(x.shape, BF16), jax.ShapeDtypeStruct(x.shape, BF16),
                    jax.ShapeDtypeStruct((experts + 8, cols), F32)],
-        compiler_params=pltpu.CompilerParams(dimension_semantics=("arbitrary",), vmem_limit_bytes=58 * MIB),
+        compiler_params=pltpu.CompilerParams(dimension_semantics=("arbitrary",), vmem_limit_bytes=60 * MIB),
         cost_estimate=pl.CostEstimate(flops=50_000_000_000, bytes_accessed=64 * MIB, transcendentals=0),
-        name="combine")(idx, tok, x, loss_w, h, g, aux, gate_pad)
+        name="combine_last")(ids, idx, tok, picked_x, picked_r, w1, w2, gate_pad, h, g, aux, x, loss_w, *accs, probs)
 
 
 def rank_picks(tok, tokens, distinct):
@@ -332,7 +517,7 @@
         wanted = (jnp.take(wanted, order, axis=1) - (order * tokens)[None, :, None]).transpose(1, 0, 2)
 
         half = local // 2
-        part_a = after((up_w[:half], down_w[:half]), asked)
+        part_a = (up_w[:half], down_w[:half])
         xa, ya = [permute(v, 2) for v in part_a], [permute(v, 4) for v in part_a]
         partner = [permute(up_w, 1), permute(down_w, 1)]
 
@@ -342,12 +527,16 @@
         send_r = gather_rows(after(send_idx, send_x), [loss_w], group * distinct)
         got_x, got_r = dispatch(send_x), dispatch(send_r)
 
-        part_b = after((up_w[half:], down_w[half:]), send_r)
+        part_b = [w[half:] for w in after((up_w, down_w), send_r)]
         xb, yb = [permute(v, 2) for v in part_b], [permute(v, 4) for v in part_b]
 
-        own_tok = asked.reshape(-1)
+        spans = [(0, 0, local), (1, 0, local)] + [(m, 0, half) for m in (2, 4, 3, 5)]
+        early = sum(s[2] for s in spans)
+        spans += [(m, half, half) for m in (2, 4, 3, 5)] + [(6, 0, half), (7, 0, half), (6, half, half), (7, half, half)]
+        ids_by_mask = order[:, None] * local + jnp.arange(local)[None, :]
+        own_ids = jnp.concatenate([ids_by_mask[m, s:s + n] for m, s, n in spans])
+        own_tok = jnp.concatenate([asked[m, s:s + n] for m, s, n in spans]).reshape(-1)
         own_idx = row_base(own_tok)
-        own_ids = (order[:, None] * local + jnp.arange(local)[None, :]).reshape(-1)
         picked_x = gather_rows(after(own_idx, send_r), [x], experts * picks)
         picked_r = gather_rows(after(own_idx, picked_x), [loss_w], experts * picks)
 
@@ -357,32 +546,35 @@
         da, db = relay(xa, ya), relay(xb, yb)
         xa1, ya1, xb1, yb1, da1, db1 = ([permute(v, 1) for v in vs] for vs in (xa, ya, xb, yb, da, db))
 
-        def owner(bufs, first, weights):
+        def owner(bufs, first, *pairs):
             ids = after(own_ids, bufs[2]) if bufs else own_ids
-            return owner_group(ids, picked_x, picked_r, *weights, gate_pad, bufs, first, picks, experts, scale)
+            return owner_group(ids, picked_x, picked_r, pairs, gate_pad, bufs, first, picks, experts, scale)
 
         bufs = owner([], 0, (up_w, down_w))
         bufs = owner(bufs, local, partner)
-        for m, weights in ((2, xa), (4, ya), (3, xa1), (5, ya1)):
-            bufs = owner(bufs, m * local, weights)
+        bufs = owner(bufs, 2 * local, xa, ya, xa1, ya1)
 
         _, place = rank_picks(wanted.reshape(group, -1), tokens, distinct)
         rows_idx = row_base(place.reshape(group, local, picks) + jnp.arange(group)[:, None, None] * distinct)
         rows_idx = rows_idx.transpose(1, 0, 2).reshape(-1)
         my_ids = me * local + jnp.arange(local)
         rows_x = gather_rows(after(rows_idx, bufs[2]), got_x, local * capacity)
-        rows_r = gather_rows(after(rows_idx, rows_x), got_r, local * capacity)
+        *accs, probs = combine_first(after(own_idx, rows_x), own_tok, x, loss_w, *bufs, gate_pad, picks, early, experts, scale)
+        rows_r = gather_rows(after(rows_idx, accs[2]), got_r, local * capacity)
         grad_up, grad_down = expert_grads(my_ids, rows_x, rows_r, up_w, down_w, gate_pad, experts, scale)
 
         own_ids = after(own_ids, grad_down)
-        for m, weights in ((2, xb), (4, yb), (3, xb1), (5, yb1)):
-            bufs = owner(bufs, m * local + half, weights)
-        for m, start, weights in ((6, 0, da), (7, 0, da1), (6, half, db), (7, half, db1)):
-            bufs = owner(bufs, m * local + start, weights)
-
-        y, grad_x, part = combine(own_idx, own_tok, x, loss_w, *bufs, gate_pad, picks, experts, scale)
-        for mask in (1, 2, 4):
-            part = part + permute(part, mask)
+        bufs = owner(bufs, 4 * local, xb, yb)
+        bufs = owner(bufs, 5 * local, xb1, yb1)
+        accs = combine_mid(own_idx, own_tok, *bufs, accs, picks, early, 2 * local)
+        own_ids = after(own_ids, accs[2])
+        bufs = owner(bufs, 6 * local, da)
+        bufs = owner(bufs, 6 * local + half, da1)
+        bufs = owner(bufs, 7 * local, db)
+        y, grad_x, part = combine_last(own_ids, own_idx, own_tok, x, loss_w, picked_x, picked_r, *db1, *bufs, gate_pad,
+                                       accs, probs, picks, 6 * local, experts, scale)
+        part = part + permute(part, 1)
+        part = (part + permute(part, 2)) + (permute(part, 4) + permute(part, 6))
         return y, jnp.sum(part[experts:]) * scale, grad_x, grad_up, grad_down, part[:experts].T
 
     return jax.shard_map(device_step, mesh=mesh,

time: 845 us -> 761 us (0.901)
  waiting for transfers between devices: 386 us -> 254 us
  Pallas kernels: 358 us -> 399 us
    ppermute x43 -> x44, waiting for transfers between devices: 384 us -> 252 us  [permute(): return lax.ppermute(value, 'ep', [(i, i ^ mask) for i in range(group)])]
    pallas_call x15 -> x11, Pallas kernels: 181 us -> 221 us  [the longest x8 83.1 us: owner_group(): pl.pallas_call(functools.partial(owner_body, first=first, per=per, num_pa...]
    unnamed x82 -> x84, local copies, waits for them, and re-layouts: 25.3 us -> 21.8 us
    ppermute x43 -> x44, starting transfers between devices: 29.9 us -> 28.1 us  [permute(): return lax.ppermute(value, 'ep', [(i, i ^ mask) for i in range(group)])]
  transfers between devices with their start and end apart: 44 -> 45, of which waited for: 18 -> 13; matrix products, arithmetic and copies ran while one was open for 2% -> 3% of each run, Pallas kernels for 30% -> 45%
where the time goes in v2:
time: 761 us; the launch traced here: 751 us
  Pallas kernels  399 us (52%)
  waiting for transfers between devices  254 us (33%)
  local copies, waits for them, and re-layouts  46.2 us (6%)
  starting transfers between devices  32.4 us (4%)
  other arithmetic  12.3 us (2%)
    ppermute x44, waiting for transfers between devices, permute(): return lax.ppermute(value, 'ep', [(i, i ^ mask) for i in range(group)])  252 us
    pallas_call x6, Pallas kernels, gather_rows(): pl.pallas_call(functools.partial(gather_body, num_src=len(srcs), rows=row...  116 us
    pallas_call x8, Pallas kernels, owner_group(): pl.pallas_call(functools.partial(owner_body, first=first, per=per, num_pa...  83.1 us
    pallas_call x1, Pallas kernels, expert_grads(): pl.pallas_call(functools.partial(expert_body, experts=experts, scale=scal...  61.6 us
    pallas_call x1, Pallas kernels, combine_first(): pl.pallas_call(functools.partial(combine_first_body, chunks=chunks, block...  54.3 us
    pallas_call x1, Pallas kernels, combine_last(): pl.pallas_call(functools.partial(combine_last_body, own_first=own_first,...  45.3 us
    pallas_call x1, Pallas kernels, combine_mid(): pl.pallas_call(functools.partial(combine_mid_body, first=first, blocks=bl...  38.6 us
    ppermute x44, starting transfers between devices, permute(): return lax.ppermute(value, 'ep', [(i, i ^ mask) for i in range(group)])  28.1 us
  transfers between devices with their start and end apart: 45, of which 13 were waited for; matrix products, arithmetic and copies ran while one was open for 3% of the time, Pallas kernels for 45%

profile of v2, /device:TPU:0, one launch (start us, length us, event | category | flops | bytes accessed | tf_op | source)
XLA Modules:
  0.0 751.1 jit_solution(8118428263085029838)
XLA Ops:
  0.6 4.3 all-to-all-start
  5.0 1.4 gather_fusion
  7.5 2.2 all-to-all-done
  12.0 8.8 %convert_reduce_fusion = s32[8,512]{1,0:T(8,128)S(1)} fusion(f32[8,4096]{1,0:T(8,128)S(1)} %le.48), kind=kLoop, calls=%fused_computation.2 | loop fusion | flops 50327552 | bytes 147456 | tf_op jit(solution)/shard_map/reduce_sum | solution.py:485
  20.8 15.3 %shard_map.109 = bf16[4096,1024]{1,0:T(8,128)(2,1)S(1)} custom-call(s32[4096]{0:T(1024)S(1)} %bitcast.93, bf16[4096,1024]{1,0:T(8,128)(2,1)} %x_in.1), custom_call_target="tpu_custom_call" | custom-call | flops 4096000000 | bytes 16777216 | tf_op jit(solution)/shard_map/pallas_call | solution.py:72
  36.1 2.2 fusion.32
  38.9 1.3 collective-permute-start.12
  40.7 1.1 collective-permute-start.14
  43.6 15.3 %shard_map.110 = bf16[4096,1024]{1,0:T(8,128)(2,1)S(1)} custom-call(s32[4096]{0:T(1024)S(1)} %bitcast.94, bf16[4096,1024]{1,0:T(8,128)(2,1)} %r_in.1), custom_call_target="tpu_custom_call" | custom-call | flops 4096000000 | bytes 16777216 | tf_op jit(solution)/shard_map/pallas_call | solution.py:72
  58.9 5.4 collective-permute-done.11.refs_2_
  64.3 2.0 fusion.31
  66.3 19.5 %collective-permute-done.12.refs_3_ = bf16[512,1024]{1,0:T(8,128)(2,1)S(1)} collective-permute-done((bf16[512,1024]{1,0:T(8,128)(2,1)S(1)}, bf16[512,1024]{1,0:T(8,128)(2,1)S(1)}, u32[]{:S(2)}, u32[]{:S(2)}) %collective-permute-start.12) | collective-permute-done | bytes 1048608 | tf_op jit(solution)/shard_map/ppermute | solution.py:497
  85.9 1.0 collective-permute-start.17
  86.9 3.0 slice.186
  90.6 41.6 %collective-permute-done.14.refs_5_ = bf16[512,1024]{1,0:T(8,128)(2,1)S(1)} collective-permute-done((bf16[512,1024]{1,0:T(8,128)(2,1)S(1)}, bf16[512,1024]{1,0:T(8,128)(2,1)S(1)}, u32[]{:S(2)}, u32[]{:S(2)}) %collective-permute-start.14) | collective-permute-done | bytes 1048608 | tf_op jit(solution)/shard_map/ppermute | solution.py:497
  133.6 1.0 copy-done.24
  136.0 3.1 slice.187
  139.1 60.1 %collective-permute-done.18.refs_2_ = bf16[512,1024]{1,0:T(8,128)(2,1)S(1)} collective-permute-done((bf16[512,1024]{1,0:T(8,128)(2,1)S(1)}, bf16[512,1024]{1,0:T(8,128)(2,1)S(1)}, u32[]{:S(2)}, u32[]{:S(2)}) %collective-permute-start.18) | collective-permute-done | bytes 1048608 | tf_op jit(solution)/shard_map/ppermute | solution.py:497
  199.2 1.0 copy-done.22
  200.8 20.0 %collective-permute-done.19.refs_3_ = bf16[512,1024]{1,0:T(8,128)(2,1)S(1)} collective-permute-done((bf16[512,1024]{1,0:T(8,128)(2,1)S(1)}, bf16[512,1024]{1,0:T(8,128)(2,1)S(1)}, u32[]{:S(2)}, u32[]{:S(2)}) %collective-permute-start.19) | collective-permute-done | bytes 1048608 | tf_op jit(solution)/shard_map/ppermute | solution.py:497
  220.7 1.0 copy-done.26
  223.1 1.0 copy-done.28
  226.7 1.0 pad.4.gate_ref
  229.2 1.7 select_reduce_fusion.1
  231.6 1.5 concatenate.7
  233.1 15.9 %collective-permute-done.5.refs_3_ = bf16[2,512,1024]{2,1,0:T(8,128)(2,1)} collective-permute-done((bf16[2,512,1024]{2,1,0:T(8,128)(2,1)}, bf16[2,512,1024]{2,1,0:T(8,128)(2,1)}, u32[]{:S(2)}, u32[]{:S(2)}) %collective-permute-start.5) | collective-permute-done | bytes 2097184 | tf_op jit(solution)/shard_map/ppermute | solution.py:497
  249.0 3.4 copy-done.3
  252.4 21.1 %shard_map.111.x_ref.px_ref = bf16[8192,1024]{1,0:T(8,128)(2,1)} custom-call(s32[8192]{0:T(1024)S(1)} %and_or_fusion.idx, bf16[4096,1024]{1,0:T(8,128)(2,1)S(1)} %copy-done.3), custom_call_target="tpu_custom_call" | custom-call | flops 8192000000 | bytes 33554432 | tf_op jit(solution)/shard_map/pallas_call | solution.py:72
  274.0 18.2 %collective-permute-done.4.refs_2_ = bf16[2,1024,512]{2,1,0:T(8,128)(2,1)} collective-permute-done((bf16[2,1024,512]{2,1,0:T(8,128)(2,1)}, bf16[2,1024,512]{2,1,0:T(8,128)(2,1)}, u32[]{:S(2)}, u32[]{:S(2)}) %collective-permute-start.4) | collective-permute-done | bytes 2097184 | tf_op jit(solution)/shard_map/ppermute | solution.py:497
  292.7 3.4 copy-done.4
  296.1 21.5 %shard_map.112.r_ref.pr_ref = bf16[8192,1024]{1,0:T(8,128)(2,1)} custom-call(s32[8192]{0:T(1024)S(1)} %and_or_fusion.idx, bf16[4096,1024]{1,0:T(8,128)(2,1)S(1)} %copy-done.4), custom_call_target="tpu_custom_call" | custom-call | flops 8192000000 | bytes 33554432 | tf_op jit(solution)/shard_map/pallas_call | solution.py:72
  317.6 10.4 %shard_map.113 = (bf16[8192,1024]{1,0:T(8,128)(2,1)}, bf16[8192,1024]{1,0:T(8,128)(2,1)}, f32[8192,128]{1,0:T(8,128)S(1)}) custom-call(s32[32]{0:T(128)S(1)} %concatenate.6.ids, bf16[8192,1024]{1,0:T(8,128)(2,1)} %shard_map.111.x_ref.px_ref, bf16[8192,1024]{1,0:T(8,128)(2,1)} %shard_map.112.r_ref.pr_ref, bf16[1024,128]{1,0:T(8,128)(2,1)S(1)} %pad.4.gate_ref, ...), custom_call_target="tpu_custom_call" | custom-call | flops 4000000000 | bytes 16777216 | tf_op jit(solution)/shard_map/pallas_call | solution.py:161
  328.0 3.0 slice.204
  331.1 3.1 slice.205
  336.1 10.5 %shard_map.114 = (bf16[8192,1024]{1,0:T(8,128)(2,1)}, bf16[8192,1024]{1,0:T(8,128)(2,1)}, f32[8192,128]{1,0:T(8,128)S(1)}) custom-call(s32[32]{0:T(128)S(1)} %concatenate.6.ids, bf16[8192,1024]{1,0:T(8,128)(2,1)} %shard_map.111.x_ref.px_ref, bf16[8192,1024]{1,0:T(8,128)(2,1)} %shard_map.112.r_ref.pr_ref, ...), custom_call_target="tpu_custom_call", output_to_operand_aliasing={{0}: (6, {}), {1}: (7, {}), {2}: (8, {})} | custom-call | flops 4000000000 | bytes 16777216 | tf_op jit(solution)/shard_map/pallas_call | solution.py:161
  346.6 2.0 copy-done
  349.0 1.9 collective-permute-start.22
  350.9 1.4 collective-permute-start.23
  352.4 20.6 %shard_map.115 = (bf16[8192,1024]{1,0:T(8,128)(2,1)}, bf16[8192,1024]{1,0:T(8,128)(2,1)}, f32[8192,128]{1,0:T(8,128)}) custom-call(s32[32]{0:T(128)S(1)} %concatenate.6.ids, bf16[8192,1024]{1,0:T(8,128)(2,1)} %shard_map.111.x_ref.px_ref, bf16[8192,1024]{1,0:T(8,128)(2,1)} %shard_map.112.r_ref.pr_ref, ...), custom_call_target="tpu_custom_call", output_to_operand_aliasing={{0}: (12, {}), {1}: (13, {}), {2}: (14, {})} | custom-call | flops 8000000000 | bytes 33554432 | tf_op jit(solution)/shard_map/pallas_call | solution.py:161
  373.1 21.2 %shard_map.116.x_ref = bf16[8192,1024]{1,0:T(8,128)(2,1)} custom-call(s32[8192]{0:T(1024)S(1)} %bitcast.95, bf16[512,1024]{1,0:T(8,128)(2,1)S(1)} %copy-done.5, bf16[512,1024]{1,0:T(8,128)(2,1)S(1)} %copy-done.11, bf16[512,1024]{1,0:T(8,128)(2,1)S(1)} %copy-done.13, bf16[512,1024]{1,0:T(8,128)(2,1)S(1)} %copy-done.15, bf16[512,1024]{1,0:T(8,128)(2,1)S(1)} %copy-done.17, ...), custom_call_target="tpu_custom_call" | custom-call | flops 8192000000 | bytes 33554432 | tf_op jit(solution)/shard_map/pallas_call | solution.py:72
  394.4 54.6 %collective-permute-done.21.refs_5_ = bf16[512,1024]{1,0:T(8,128)(2,1)S(1)} collective-permute-done((bf16[512,1024]{1,0:T(8,128)(2,1)}, bf16[512,1024]{1,0:T(8,128)(2,1)S(1)}, u32[]{:S(2)}, u32[]{:S(2)}) %collective-permute-start.21) | collective-permute-done | bytes 1048608 | tf_op jit(solution)/shard_map/ppermute | solution.py:497
  450.0 1.5 collective-permute-start.25
  452.3 1.1 collective-permute-start.36
  454.0 54.3 %combine_first.1 = (f32[32768,128]{1,0:T(8,128)}, f32[32768,128]{1,0:T(8,128)}, f32[4096,128]{1,0:T(8,128)}, f32[4096,128]{1,0:T(8,128)}) custom-call(s32[8192]{0:T(1024)} %copy-done.7, s32[8192]{0:T(1024)} %bitcast.103, bf16[4096,1024]{1,0:T(8,128)(2,1)} %x_in.1, bf16[4096,1024]{1,0:T(8,128)(2,1)} %r_in.1, ...), custom_call_target="tpu_custom_call" | custom-call | flops 30000001024 | bytes 67108864 | tf_op jit(solution)/shard_map/combine_first/pallas_call | solution.py:284
  508.3 1.2 copy-done.9
  509.5 1.2 copy-done.23
  510.8 1.2 copy-done.27
  512.0 1.2 copy-done.29
  513.2 1.2 copy-done.31
  514.4 22.0 %shard_map.117.r_ref = bf16[8192,1024]{1,0:T(8,128)(2,1)} custom-call(s32[8192]{0:T(1024)S(1)} %bitcast.96, bf16[512,1024]{1,0:T(8,128)(2,1)S(1)} %get-tuple-element.122.refs_0_, bf16[512,1024]{1,0:T(8,128)(2,1)S(1)} %copy-done.9, bf16[512,1024]{1,0:T(8,128)(2,1)S(1)} %copy-done.23, bf16[512,1024]{1,0:T(8,128)(2,1)S(1)} %copy-done.27, ...), custom_call_target="tpu_custom_call" | custom-call | flops 8192000000 | bytes 33554432 | tf_op jit(solution)/shard_map/pallas_call | solution.py:72
  537.6 7.5 %collective-permute-done.36.refs_0_ = bf16[2,1024,512]{2,1,0:T(8,128)(2,1)S(1)} collective-permute-done((bf16[2,1024,512]{2,1,0:T(8,128)(2,1)S(1)}, bf16[2,1024,512]{2,1,0:T(8,128)(2,1)S(1)}, u32[]{:S(2)}, u32[]{:S(2)}) %collective-permute-start.36) | collective-permute-done | bytes 2097184 | tf_op jit(solution)/shard_map/ppermute | solution.py:497
  546.2 61.6 %expert_grads.1 = (bf16[4,1024,512]{2,1,0:T(8,128)(2,1)}, bf16[4,512,1024]{2,1,0:T(8,128)(2,1)}) custom-call(s32[4]{0:T(128)S(1)} %iota_add_fusion.1.ids, bf16[8192,1024]{1,0:T(8,128)(2,1)} %shard_map.116.x_ref, bf16[8192,1024]{1,0:T(8,128)(2,1)} %shard_map.117.r_ref, bf16[4,1024,512]{2,1,0:T(8,128)(2,1)} %w1_ref.1, bf16[4,512,1024]{2,1,0:T(8,128)(2,1)} %w2_ref.1, ...), custom_call_target="tpu_custom_call" | custom-call | flops 44999999488 | bytes 50331648 | tf_op jit(solution)/shard_map/expert_grads/pallas_call | solution.py:206
  607.8 11.4 %shard_map.118 = (bf16[8192,1024]{1,0:T(8,128)(2,1)}, bf16[8192,1024]{1,0:T(8,128)(2,1)}, f32[8192,128]{1,0:T(8,128)}) custom-call(s32[32]{0:T(128)S(1)} %concatenate.6.ids, bf16[8192,1024]{1,0:T(8,128)(2,1)} %shard_map.111.x_ref.px_ref, bf16[8192,1024]{1,0:T(8,128)(2,1)} %shard_map.112.r_ref.pr_ref, ...), custom_call_target="tpu_custom_call", output_to_operand_aliasing={{0}: (8, {}), {1}: (9, {}), {2}: (10, {})} | custom-call | flops 4000000000 | bytes 16777216 | tf_op jit(solution)/shard_map/pallas_call | solution.py:161
  620.3 11.4 %shard_map.119 = (bf16[8192,1024]{1,0:T(8,128)(2,1)}, bf16[8192,1024]{1,0:T(8,128)(2,1)}, f32[8192,128]{1,0:T(8,128)}) custom-call(s32[32]{0:T(128)S(1)} %concatenate.6.ids, bf16[8192,1024]{1,0:T(8,128)(2,1)} %shard_map.111.x_ref.px_ref, bf16[8192,1024]{1,0:T(8,128)(2,1)} %shard_map.112.r_ref.pr_ref, ...), custom_call_target="tpu_custom_call", output_to_operand_aliasing={{0}: (8, {}), {1}: (9, {}), {2}: (10, {})} | custom-call | flops 4000000000 | bytes 16777216 | tf_op jit(solution)/shard_map/pallas_call | solution.py:161
  631.6 38.6 %combine_mid.1 = (f32[32768,128]{1,0:T(8,128)}, f32[32768,128]{1,0:T(8,128)}, f32[4096,128]{1,0:T(8,128)}) custom-call(s32[8192]{0:T(1024)} %copy-done.7, s32[8192]{0:T(1024)} %bitcast.104, bf16[8192,1024]{1,0:T(8,128)(2,1)} %get-tuple-element.87.h_ref.refs_2_, bf16[8192,1024]{1,0:T(8,128)(2,1)} %get-tuple-element.88.g_ref.refs_3_, ...), custom_call_target="tpu_custom_call" | custom-call | flops 20000000000 | bytes 67108864 | tf_op jit(solution)/shard_map/combine_mid/pallas_call | solution.py:318
  670.2 6.0 shard_map.120
  676.1 6.6 shard_map.121
  682.7 6.3 shard_map.122
  689.0 45.3 %combine_last.1 = (bf16[4096,1024]{1,0:T(8,128)(2,1)}, bf16[4096,1024]{1,0:T(8,128)(2,1)}, f32[40,1024]{1,0:T(8,128)}) custom-call(s32[32]{0:T(128)} %copy-done.6, s32[8192]{0:T(1024)} %copy-done.7, s32[8192]{0:T(1024)} %bitcast.105, bf16[8192,1024]{1,0:T(8,128)(2,1)} %shard_map.111.x_ref.px_ref, bf16[8192,1024]{1,0:T(8,128)(2,1)} %shard_map.112.r_ref.pr_ref, ...), custom_call_target="tpu_custom_call" | custom-call | flops 49999998976 | bytes 67108864 | tf_op jit(solution)/shard_map/combine_last/pallas_call | solution.py:445
  734.3 1.6 collective-permute-done.40
  736.9 1.5 collective-permute-start.41
  739.2 1.2 collective-permute-start.43
  740.4 3.6 collective-permute-done.41
  744.0 3.9 collective-permute-done.42
  (180 shorter events, 28.8 us)
Async XLA Ops:
  0.6 9.1 %all-to-all-start = ((s32[4,8,256]{2,0,1:T(4,128)}), s32[4,8,256]{2,0,1:T(4,128)S(1)}, u32[]{:S(2)}, u32[]{:S(2)}) async-start(s32[4,8,256]{2,0,1:T(4,128)} %bitcast.100), calls=%async_computation | async-start | bytes 65536 | tf_op jit(solution)/shard_map/all_to_all | solution.py:515
  38.3 3.5 collective-permute-start.10
  38.3 26.0 %collective-permute-start.11 = (bf16[512,1024]{1,0:T(8,128)(2,1)S(1)}, bf16[512,1024]{1,0:T(8,128)(2,1)S(1)}, u32[]{:S(2)}, u32[]{:S(2)}) collective-permute-start(bf16[512,1024]{1,0:T(8,128)(2,1)S(1)} %get-tuple-element.128), channel_id=1, source_target_pairs={{0,2},{1,3},{2,0},{3,1},{4,6},{5,7},{6,4},{7,5}} | collective-permute-start | bytes 3145736 | tf_op jit(solution)/shard_map/ppermute | solution.py:497
  38.9 47.0 %collective-permute-start.12 = (bf16[512,1024]{1,0:T(8,128)(2,1)S(1)}, bf16[512,1024]{1,0:T(8,128)(2,1)S(1)}, u32[]{:S(2)}, u32[]{:S(2)}) collective-permute-start(bf16[512,1024]{1,0:T(8,128)(2,1)S(1)} %get-tuple-element.127), channel_id=1, source_target_pairs={{0,3},{1,2},{2,1},{3,0},{4,7},{5,6},{6,5},{7,4}} | collective-permute-start | bytes 3145736 | tf_op jit(solution)/shard_map/ppermute | solution.py:497
  40.1 49.8 %collective-permute-start.13 = (bf16[512,1024]{1,0:T(8,128)(2,1)S(1)}, bf16[512,1024]{1,0:T(8,128)(2,1)S(1)}, u32[]{:S(2)}, u32[]{:S(2)}) collective-permute-start(bf16[512,1024]{1,0:T(8,128)(2,1)S(1)} %get-tuple-element.126), channel_id=1, source_target_pairs={{0,4},{1,5},{2,6},{3,7},{4,0},{5,1},{6,2},{7,3}} | collective-permute-start | bytes 3145736 | tf_op jit(solution)/shard_map/ppermute | solution.py:497
  40.7 91.5 %collective-permute-start.14 = (bf16[512,1024]{1,0:T(8,128)(2,1)S(1)}, bf16[512,1024]{1,0:T(8,128)(2,1)S(1)}, u32[]{:S(2)}, u32[]{:S(2)}) collective-permute-start(bf16[512,1024]{1,0:T(8,128)(2,1)S(1)} %get-tuple-element.125), channel_id=1, source_target_pairs={{0,5},{1,4},{2,7},{3,6},{4,1},{5,0},{6,3},{7,2}} | collective-permute-start | bytes 3145736 | tf_op jit(solution)/shard_map/ppermute | solution.py:497
  42.8 90.3 %collective-permute-start.15 = (bf16[512,1024]{1,0:T(8,128)(2,1)S(1)}, bf16[512,1024]{1,0:T(8,128)(2,1)S(1)}, u32[]{:S(2)}, u32[]{:S(2)}) collective-permute-start(bf16[512,1024]{1,0:T(8,128)(2,1)S(1)} %get-tuple-element.124), channel_id=1, source_target_pairs={{0,6},{1,7},{2,4},{3,5},{4,2},{5,3},{6,0},{7,1}} | collective-permute-start | bytes 3145736 | tf_op jit(solution)/shard_map/ppermute | solution.py:497
  64.3 69.3 %collective-permute-start.16 = (bf16[512,1024]{1,0:T(8,128)(2,1)S(1)}, bf16[512,1024]{1,0:T(8,128)(2,1)S(1)}, u32[]{:S(2)}, u32[]{:S(2)}) collective-permute-start(bf16[512,1024]{1,0:T(8,128)(2,1)S(1)} %get-tuple-element.123), channel_id=1, source_target_pairs={{0,7},{1,6},{2,5},{3,4},{4,3},{5,2},{6,1},{7,0}} | collective-permute-start | bytes 3145736 | tf_op jit(solution)/shard_map/ppermute | solution.py:497
  85.9 49.6 %collective-permute-start.17 = (bf16[512,1024]{1,0:T(8,128)(2,1)S(1)}, bf16[512,1024]{1,0:T(8,128)(2,1)S(1)}, u32[]{:S(2)}, u32[]{:S(2)}) collective-permute-start(bf16[512,1024]{1,0:T(8,128)(2,1)S(1)} %get-tuple-element.121), channel_id=1, source_target_pairs={{0,1},{1,0},{2,3},{3,2},{4,5},{5,4},{6,7},{7,6}} | collective-permute-start | bytes 3145736 | tf_op jit(solution)/shard_map/ppermute | solution.py:497
  90.0 49.1 %copy-start.16 = (bf16[512,1024]{1,0:T(8,128)(2,1)}, bf16[512,1024]{1,0:T(8,128)(2,1)S(1)}, u32[]{:S(2)}) copy-start(bf16[512,1024]{1,0:T(8,128)(2,1)S(1)} %collective-permute-done.13.refs_4_) | copy-start | bytes 3145732
  90.0 134.7 %collective-permute-start.2 = (bf16[2,1024,512]{2,1,0:T(8,128)(2,1)}, bf16[2,1024,512]{2,1,0:T(8,128)(2,1)S(1)}, u32[]{:S(2)}, u32[]{:S(2)}) collective-permute-start(bf16[2,1024,512]{2,1,0:T(8,128)(2,1)} %slice.186), channel_id=1, source_target_pairs={{0,2},{1,3},{2,0},{3,1},{4,6},{5,7},{6,4},{7,5}} | collective-permute-start | bytes 6291464 | tf_op jit(solution)/shard_map/ppermute | solution.py:497
  132.2 6.9 copy-start.18
  132.2 160.0 %collective-permute-start = (bf16[4,1024,512]{2,1,0:T(8,128)(2,1)}, bf16[4,1024,512]{2,1,0:T(8,128)(2,1)}, u32[]{:S(2)}, u32[]{:S(2)}) collective-permute-start(bf16[4,1024,512]{2,1,0:T(8,128)(2,1)} %w1_ref.1), channel_id=1, source_target_pairs={{0,1},{1,0},{2,3},{3,2},{4,5},{5,4},{6,7},{7,6}} | collective-permute-start | bytes 12582920 | tf_op jit(solution)/shard_map/ppermute | solution.py:497
  133.0 6.1 copy-start.20
  133.0 66.2 %collective-permute-start.18 = (bf16[512,1024]{1,0:T(8,128)(2,1)S(1)}, bf16[512,1024]{1,0:T(8,128)(2,1)S(1)}, u32[]{:S(2)}, u32[]{:S(2)}) collective-permute-start(bf16[512,1024]{1,0:T(8,128)(2,1)S(1)} %get-tuple-element.120), channel_id=1, source_target_pairs={{0,2},{1,3},{2,0},{3,1},{4,6},{5,7},{6,4},{7,5}} | collective-permute-start | bytes 3145736 | tf_op jit(solution)/shard_map/ppermute | solution.py:497
  134.6 86.1 %collective-permute-start.19 = (bf16[512,1024]{1,0:T(8,128)(2,1)S(1)}, bf16[512,1024]{1,0:T(8,128)(2,1)S(1)}, u32[]{:S(2)}, u32[]{:S(2)}) collective-permute-start(bf16[512,1024]{1,0:T(8,128)(2,1)S(1)} %get-tuple-element.119), channel_id=1, source_target_pairs={{0,3},{1,2},{2,1},{3,0},{4,7},{5,6},{6,5},{7,4}} | collective-permute-start | bytes 3145736 | tf_op jit(solution)/shard_map/ppermute | solution.py:497
  135.4 90.4 %copy-start.37 = (bf16[1024,32]{0,1:T(8,128)(2,1)S(1)}, bf16[1024,32]{0,1:T(8,128)(2,1)}, u32[]{:S(2)}) copy-start(bf16[1024,32]{0,1:T(8,128)(2,1)} %param.9) | copy-start | bytes 196612
  135.4 87.6 %collective-permute-start.20 = (bf16[512,1024]{1,0:T(8,128)(2,1)S(1)}, bf16[512,1024]{1,0:T(8,128)(2,1)S(1)}, u32[]{:S(2)}, u32[]{:S(2)}) collective-permute-start(bf16[512,1024]{1,0:T(8,128)(2,1)S(1)} %get-tuple-element.118), channel_id=1, source_target_pairs={{0,4},{1,5},{2,6},{3,7},{4,0},{5,1},{6,2},{7,3}} | collective-permute-start | bytes 3145736 | tf_op jit(solution)/shard_map/ppermute | solution.py:497
  200.2 48.8 %collective-permute-start.5 = (bf16[2,512,1024]{2,1,0:T(8,128)(2,1)}, bf16[2,512,1024]{2,1,0:T(8,128)(2,1)}, u32[]{:S(2)}, u32[]{:S(2)}) collective-permute-start(bf16[2,512,1024]{2,1,0:T(8,128)(2,1)} %slice.187), channel_id=1, source_target_pairs={{0,4},{1,5},{2,6},{3,7},{4,0},{5,1},{6,2},{7,3}} | collective-permute-start | bytes 6291464 | tf_op jit(solution)/shard_map/ppermute | solution.py:497
  221.7 113.1 %collective-permute-start.1 = (bf16[4,512,1024]{2,1,0:T(8,128)(2,1)}, bf16[4,512,1024]{2,1,0:T(8,128)(2,1)}, u32[]{:S(2)}, u32[]{:S(2)}) collective-permute-start(bf16[4,512,1024]{2,1,0:T(8,128)(2,1)} %w2_ref.1), channel_id=1, source_target_pairs={{0,1},{1,0},{2,3},{3,2},{4,5},{5,4},{6,7},{7,6}} | collective-permute-start | bytes 12582920 | tf_op jit(solution)/shard_map/ppermute | solution.py:497
  224.1 49.4 %collective-permute-start.3 = (bf16[2,512,1024]{2,1,0:T(8,128)(2,1)}, bf16[2,512,1024]{2,1,0:T(8,128)(2,1)}, u32[]{:S(2)}, u32[]{:S(2)}) collective-permute-start(bf16[2,512,1024]{2,1,0:T(8,128)(2,1)} %slice.187), channel_id=1, source_target_pairs={{0,2},{1,3},{2,0},{3,1},{4,6},{5,7},{6,4},{7,5}} | collective-permute-start | bytes 6291464 | tf_op jit(solution)/shard_map/ppermute | solution.py:497
  224.6 67.5 %collective-permute-start.4 = (bf16[2,1024,512]{2,1,0:T(8,128)(2,1)}, bf16[2,1024,512]{2,1,0:T(8,128)(2,1)}, u32[]{:S(2)}, u32[]{:S(2)}) collective-permute-start(bf16[2,1024,512]{2,1,0:T(8,128)(2,1)} %slice.186), channel_id=1, source_target_pairs={{0,4},{1,5},{2,6},{3,7},{4,0},{5,1},{6,2},{7,3}} | collective-permute-start | bytes 6291464 | tf_op jit(solution)/shard_map/ppermute | solution.py:497
  227.7 124.6 %copy-start.1 = (bf16[1024,128]{1,0:T(8,128)(2,1)}, bf16[1024,128]{1,0:T(8,128)(2,1)S(1)}, u32[]{:S(2)}) copy-start(bf16[1024,128]{1,0:T(8,128)(2,1)S(1)} %pad.4.gate_ref) | copy-start | bytes 786436
  228.6 454.1 %copy-start.6 = (s32[32]{0:T(128)}, s32[32]{0:T(128)S(1)}, u32[]{:S(2)}) copy-start(s32[32]{0:T(128)S(1)} %concatenate.6.ids) | copy-start | bytes 388
  233.1 40.4 %copy-start.36 = (s32[4,2,8,128]{3,1,2,0:T(2,128)}, s32[4,2,8,128]{3,1,2,0:T(2,128)S(1)}, u32[]{:S(2)}) copy-start(s32[4,2,8,128]{3,1,2,0:T(2,128)S(1)} %copy.41) | copy-start | bytes 98308
  233.1 59.6 %copy-start.7 = (s32[8192]{0:T(1024)}, s32[8192]{0:T(1024)S(1)}, u32[]{:S(2)}) copy-start(s32[8192]{0:T(1024)S(1)} %and_or_fusion.idx) | copy-start | bytes 98308
  249.0 86.3 %collective-permute-start.6 = (bf16[2,1024,512]{2,1,0:T(8,128)(2,1)S(1)}, bf16[2,1024,512]{2,1,0:T(8,128)(2,1)S(1)}, u32[]{:S(2)}, u32[]{:S(2)}) collective-permute-start(bf16[2,1024,512]{2,1,0:T(8,128)(2,1)S(1)} %collective-permute-done.2.refs_0_), channel_id=1, source_target_pairs={{0,1},{1,0},{2,3},{3,2},{4,5},{5,4},{6,7},{7,6}} | collective-permute-start | bytes 6291464 | tf_op jit(solution)/shard_map/ppermute | solution.py:497
  273.5 75.1 %collective-permute-start.9 = (bf16[2,512,1024]{2,1,0:T(8,128)(2,1)}, bf16[2,512,1024]{2,1,0:T(8,128)(2,1)S(1)}, u32[]{:S(2)}, u32[]{:S(2)}) collective-permute-start(bf16[2,512,1024]{2,1,0:T(8,128)(2,1)} %collective-permute-done.5.refs_3_), channel_id=1, source_target_pairs={{0,1},{1,0},{2,3},{3,2},{4,5},{5,4},{6,7},{7,6}} | collective-permute-start | bytes 6291464 | tf_op jit(solution)/shard_map/ppermute | solution.py:497
  292.2 56.8 %collective-permute-start.7 = (bf16[2,512,1024]{2,1,0:T(8,128)(2,1)}, bf16[2,512,1024]{2,1,0:T(8,128)(2,1)S(1)}, u32[]{:S(2)}, u32[]{:S(2)}) collective-permute-start(bf16[2,512,1024]{2,1,0:T(8,128)(2,1)} %collective-permute-done.3.refs_1_), channel_id=1, source_target_pairs={{0,1},{1,0},{2,3},{3,2},{4,5},{5,4},{6,7},{7,6}} | collective-permute-start | bytes 6291464 | tf_op jit(solution)/shard_map/ppermute | solution.py:497
  292.2 58.7 %collective-permute-start.8 = (bf16[2,1024,512]{2,1,0:T(8,128)(2,1)}, bf16[2,1024,512]{2,1,0:T(8,128)(2,1)}, u32[]{:S(2)}, u32[]{:S(2)}) collective-permute-start(bf16[2,1024,512]{2,1,0:T(8,128)(2,1)} %collective-permute-done.4.refs_2_), channel_id=1, source_target_pairs={{0,1},{1,0},{2,3},{3,2},{4,5},{5,4},{6,7},{7,6}} | collective-permute-start | bytes 6291464 | tf_op jit(solution)/shard_map/ppermute | solution.py:497
  331.1 4.9 copy-start.38
  334.8 118.7 %collective-permute-start.24 = (bf16[2,1024,512]{2,1,0:T(8,128)(2,1)}, bf16[2,1024,512]{2,1,0:T(8,128)(2,1)}, u32[]{:S(2)}, u32[]{:S(2)}) collective-permute-start(bf16[2,1024,512]{2,1,0:T(8,128)(2,1)} %slice.204), channel_id=1, source_target_pairs={{0,2},{1,3},{2,0},{3,1},{4,6},{5,7},{6,4},{7,5}} | collective-permute-start | bytes 6291464 | tf_op jit(solution)/shard_map/ppermute | solution.py:497
  335.3 11.2 %copy-start.32 = (bf16[2,1024,512]{2,1,0:T(8,128)(2,1)}, bf16[2,1024,512]{2,1,0:T(8,128)(2,1)S(1)}, u32[]{:S(2)}) copy-start(bf16[2,1024,512]{2,1,0:T(8,128)(2,1)S(1)} %collective-permute-done.6.refs_4_) | copy-start | bytes 6291460
  335.3 118.7 %collective-permute-start.27 = (bf16[2,512,1024]{2,1,0:T(8,128)(2,1)}, bf16[2,512,1024]{2,1,0:T(8,128)(2,1)}, u32[]{:S(2)}, u32[]{:S(2)}) collective-permute-start(bf16[2,512,1024]{2,1,0:T(8,128)(2,1)} %slice.205), channel_id=1, source_target_pairs={{0,4},{1,5},{2,6},{3,7},{4,0},{5,1},{6,2},{7,3}} | collective-permute-start | bytes 6291464 | tf_op jit(solution)/shard_map/ppermute | solution.py:497
  348.6 100.4 %collective-permute-start.21 = (bf16[512,1024]{1,0:T(8,128)(2,1)}, bf16[512,1024]{1,0:T(8,128)(2,1)S(1)}, u32[]{:S(2)}, u32[]{:S(2)}) collective-permute-start(bf16[512,1024]{1,0:T(8,128)(2,1)} %get-tuple-element.117), channel_id=1, source_target_pairs={{0,5},{1,4},{2,7},{3,6},{4,1},{5,0},{6,3},{7,2}} | collective-permute-start | bytes 3145736 | tf_op jit(solution)/shard_map/ppermute | solution.py:497
  349.0 102.4 %collective-permute-start.22 = (bf16[512,1024]{1,0:T(8,128)(2,1)}, bf16[512,1024]{1,0:T(8,128)(2,1)}, u32[]{:S(2)}, u32[]{:S(2)}) collective-permute-start(bf16[512,1024]{1,0:T(8,128)(2,1)} %get-tuple-element.116), channel_id=1, source_target_pairs={{0,6},{1,7},{2,4},{3,5},{4,2},{5,3},{6,0},{7,1}} | collective-permute-start | bytes 3145736 | tf_op jit(solution)/shard_map/ppermute | solution.py:497
  350.9 101.4 %collective-permute-start.23 = (bf16[512,1024]{1,0:T(8,128)(2,1)}, bf16[512,1024]{1,0:T(8,128)(2,1)}, u32[]{:S(2)}, u32[]{:S(2)}) collective-permute-start(bf16[512,1024]{1,0:T(8,128)(2,1)} %get-tuple-element.115), channel_id=1, source_target_pairs={{0,7},{1,6},{2,5},{3,4},{4,3},{5,2},{6,1},{7,0}} | collective-permute-start | bytes 3145736 | tf_op jit(solution)/shard_map/ppermute | solution.py:497
  352.3 20.7 %copy-start.5 = (bf16[512,1024]{1,0:T(8,128)(2,1)S(1)}, bf16[512,1024]{1,0:T(8,128)(2,1)}, u32[]{:S(2)}) copy-start(bf16[512,1024]{1,0:T(8,128)(2,1)} %get-tuple-element.130.refs_0_) | copy-start | bytes 3145732
  352.3 20.7 %copy-start.11 = (bf16[512,1024]{1,0:T(8,128)(2,1)S(1)}, bf16[512,1024]{1,0:T(8,128)(2,1)}, u32[]{:S(2)}) copy-start(bf16[512,1024]{1,0:T(8,128)(2,1)} %copy-done.10) | copy-start | bytes 3145732
  352.3 20.7 %copy-start.13 = (bf16[512,1024]{1,0:T(8,128)(2,1)S(1)}, bf16[512,1024]{1,0:T(8,128)(2,1)}, u32[]{:S(2)}) copy-start(bf16[512,1024]{1,0:T(8,128)(2,1)} %copy-done.12) | copy-start | bytes 3145732
  352.4 20.7 %copy-start.15 = (bf16[512,1024]{1,0:T(8,128)(2,1)S(1)}, bf16[512,1024]{1,0:T(8,128)(2,1)}, u32[]{:S(2)}) copy-start(bf16[512,1024]{1,0:T(8,128)(2,1)} %copy-done.14) | copy-start | bytes 3145732
  352.4 20.7 %copy-start.17 = (bf16[512,1024]{1,0:T(8,128)(2,1)S(1)}, bf16[512,1024]{1,0:T(8,128)(2,1)}, u32[]{:S(2)}) copy-start(bf16[512,1024]{1,0:T(8,128)(2,1)} %copy-done.16) | copy-start | bytes 3145732
  352.4 20.7 %copy-start.19 = (bf16[512,1024]{1,0:T(8,128)(2,1)S(1)}, bf16[512,1024]{1,0:T(8,128)(2,1)}, u32[]{:S(2)}) copy-start(bf16[512,1024]{1,0:T(8,128)(2,1)} %copy-done.18) | copy-start | bytes 3145732
  352.4 20.7 %copy-start.21 = (bf16[512,1024]{1,0:T(8,128)(2,1)S(1)}, bf16[512,1024]{1,0:T(8,128)(2,1)}, u32[]{:S(2)}) copy-start(bf16[512,1024]{1,0:T(8,128)(2,1)} %copy-done.20) | copy-start | bytes 3145732
  352.4 20.7 %copy-start.25 = (bf16[512,1024]{1,0:T(8,128)(2,1)S(1)}, bf16[512,1024]{1,0:T(8,128)(2,1)}, u32[]{:S(2)}) copy-start(bf16[512,1024]{1,0:T(8,128)(2,1)} %copy-done.24) | copy-start | bytes 3145732
  450.0 86.5 %collective-permute-start.25 = (bf16[2,512,1024]{2,1,0:T(8,128)(2,1)}, bf16[2,512,1024]{2,1,0:T(8,128)(2,1)}, u32[]{:S(2)}, u32[]{:S(2)}) collective-permute-start(bf16[2,512,1024]{2,1,0:T(8,128)(2,1)} %slice.205), channel_id=1, source_target_pairs={{0,2},{1,3},{2,0},{3,1},{4,6},{5,7},{6,4},{7,5}} | collective-permute-start | bytes 6291464 | tf_op jit(solution)/shard_map/ppermute | solution.py:497
  451.4 85.9 %collective-permute-start.26 = (bf16[2,1024,512]{2,1,0:T(8,128)(2,1)}, bf16[2,1024,512]{2,1,0:T(8,128)(2,1)}, u32[]{:S(2)}, u32[]{:S(2)}) collective-permute-start(bf16[2,1024,512]{2,1,0:T(8,128)(2,1)} %slice.204), channel_id=1, source_target_pairs={{0,4},{1,5},{2,6},{3,7},{4,0},{5,1},{6,2},{7,3}} | collective-permute-start | bytes 6291464 | tf_op jit(solution)/shard_map/ppermute | solution.py:497
  452.3 92.8 %collective-permute-start.36 = (bf16[2,1024,512]{2,1,0:T(8,128)(2,1)S(1)}, bf16[2,1024,512]{2,1,0:T(8,128)(2,1)S(1)}, u32[]{:S(2)}, u32[]{:S(2)}) collective-permute-start(bf16[2,1024,512]{2,1,0:T(8,128)(2,1)S(1)} %collective-permute-done.2.refs_0_), channel_id=1, source_target_pairs={{0,4},{1,5},{2,6},{3,7},{4,0},{5,1},{6,2},{7,3}} | collective-permute-start | bytes 6291464 | tf_op jit(solution)/shard_map/ppermute | solution.py:497
  453.5 92.2 %collective-permute-start.37 = (bf16[2,512,1024]{2,1,0:T(8,128)(2,1)}, bf16[2,512,1024]{2,1,0:T(8,128)(2,1)S(1)}, u32[]{:S(2)}, u32[]{:S(2)}) collective-permute-start(bf16[2,512,1024]{2,1,0:T(8,128)(2,1)} %collective-permute-done.5.refs_3_), channel_id=1, source_target_pairs={{0,2},{1,3},{2,0},{3,1},{4,6},{5,7},{6,4},{7,5}} | collective-permute-start | bytes 6291464 | tf_op jit(solution)/shard_map/ppermute | solution.py:497
  454.0 91.6 %collective-permute-start.28 = (bf16[2,1024,512]{2,1,0:T(8,128)(2,1)}, bf16[2,1024,512]{2,1,0:T(8,128)(2,1)}, u32[]{:S(2)}, u32[]{:S(2)}) collective-permute-start(bf16[2,1024,512]{2,1,0:T(8,128)(2,1)} %collective-permute-done.24.refs_0_), channel_id=1, source_target_pairs={{0,1},{1,0},{2,3},{3,2},{4,5},{5,4},{6,7},{7,6}} | collective-permute-start | bytes 6291464 | tf_op jit(solution)/shard_map/ppermute | solution.py:497
  514.4 31.7 %copy-start.2 = (bf16[1024,128]{1,0:T(8,128)(2,1)S(1)}, bf16[1024,128]{1,0:T(8,128)(2,1)}, u32[]{:S(2)}) copy-start(bf16[1024,128]{1,0:T(8,128)(2,1)} %copy-done.1) | copy-start | bytes 786436
  536.4 83.3 %collective-permute-start.32 = (bf16[2,1024,512]{2,1,0:T(8,128)(2,1)}, bf16[2,1024,512]{2,1,0:T(8,128)(2,1)}, u32[]{:S(2)}, u32[]{:S(2)}) collective-permute-start(bf16[2,1024,512]{2,1,0:T(8,128)(2,1)} %collective-permute-done.24.refs_0_), channel_id=1, source_target_pairs={{0,4},{1,5},{2,6},{3,7},{4,0},{5,1},{6,2},{7,3}} | collective-permute-start | bytes 6291464 | tf_op jit(solution)/shard_map/ppermute | solution.py:497
  537.4 81.8 %collective-permute-start.31 = (bf16[2,512,1024]{2,1,0:T(8,128)(2,1)}, bf16[2,512,1024]{2,1,0:T(8,128)(2,1)}, u32[]{:S(2)}, u32[]{:S(2)}) collective-permute-start(bf16[2,512,1024]{2,1,0:T(8,128)(2,1)} %collective-permute-done.27.refs_3_), channel_id=1, source_target_pairs={{0,1},{1,0},{2,3},{3,2},{4,5},{5,4},{6,7},{7,6}} | collective-permute-start | bytes 6291464 | tf_op jit(solution)/shard_map/ppermute | solution.py:497
  545.1 74.7 %collective-permute-start.34 = (bf16[2,512,1024]{2,1,0:T(8,128)(2,1)}, bf16[2,512,1024]{2,1,0:T(8,128)(2,1)S(1)}, u32[]{:S(2)}, u32[]{:S(2)}) collective-permute-start(bf16[2,512,1024]{2,1,0:T(8,128)(2,1)} %collective-permute-done.27.refs_3_), channel_id=1, source_target_pairs={{0,2},{1,3},{2,0},{3,1},{4,6},{5,7},{6,4},{7,5}} | collective-permute-start | bytes 6291464 | tf_op jit(solution)/shard_map/ppermute | solution.py:497
  545.6 73.6 %collective-permute-start.29 = (bf16[2,512,1024]{2,1,0:T(8,128)(2,1)}, bf16[2,512,1024]{2,1,0:T(8,128)(2,1)S(1)}, u32[]{:S(2)}, u32[]{:S(2)}) collective-permute-start(bf16[2,512,1024]{2,1,0:T(8,128)(2,1)} %collective-permute-done.25.refs_1_), channel_id=1, source_target_pairs={{0,1},{1,0},{2,3},{3,2},{4,5},{5,4},{6,7},{7,6}} | collective-permute-start | bytes 6291464 | tf_op jit(solution)/shard_map/ppermute | solution.py:497
  545.7 74.6 %collective-permute-start.30 = (bf16[2,1024,512]{2,1,0:T(8,128)(2,1)}, bf16[2,1024,512]{2,1,0:T(8,128)(2,1)}, u32[]{:S(2)}, u32[]{:S(2)}) collective-permute-start(bf16[2,1024,512]{2,1,0:T(8,128)(2,1)} %collective-permute-done.26.refs_2_), channel_id=1, source_target_pairs={{0,1},{1,0},{2,3},{3,2},{4,5},{5,4},{6,7},{7,6}} | collective-permute-start | bytes 6291464 | tf_op jit(solution)/shard_map/ppermute | solution.py:497
  619.2 56.9 %collective-permute-start.38 = (bf16[2,1024,512]{2,1,0:T(8,128)(2,1)S(1)}, bf16[2,1024,512]{2,1,0:T(8,128)(2,1)}, u32[]{:S(2)}, u32[]{:S(2)}) collective-permute-start(bf16[2,1024,512]{2,1,0:T(8,128)(2,1)S(1)} %collective-permute-done.36.refs_0_), channel_id=1, source_target_pairs={{0,1},{1,0},{2,3},{3,2},{4,5},{5,4},{6,7},{7,6}} | collective-permute-start | bytes 6291464 | tf_op jit(solution)/shard_map/ppermute | solution.py:497
  619.3 56.9 %collective-permute-start.39 = (bf16[2,512,1024]{2,1,0:T(8,128)(2,1)S(1)}, bf16[2,512,1024]{2,1,0:T(8,128)(2,1)}, u32[]{:S(2)}, u32[]{:S(2)}) collective-permute-start(bf16[2,512,1024]{2,1,0:T(8,128)(2,1)S(1)} %collective-permute-done.37.refs_1_), channel_id=1, source_target_pairs={{0,1},{1,0},{2,3},{3,2},{4,5},{5,4},{6,7},{7,6}} | collective-permute-start | bytes 6291464 | tf_op jit(solution)/shard_map/ppermute | solution.py:497
  619.8 69.2 %collective-permute-start.33 = (bf16[2,1024,512]{2,1,0:T(8,128)(2,1)}, bf16[2,1024,512]{2,1,0:T(8,128)(2,1)}, u32[]{:S(2)}, u32[]{:S(2)}) collective-permute-start(bf16[2,1024,512]{2,1,0:T(8,128)(2,1)} %collective-permute-done.32.refs_0_), channel_id=1, source_target_pairs={{0,1},{1,0},{2,3},{3,2},{4,5},{5,4},{6,7},{7,6}} | collective-permute-start | bytes 6291464 | tf_op jit(solution)/shard_map/ppermute | solution.py:497
  619.8 69.2 %collective-permute-start.35 = (bf16[2,512,1024]{2,1,0:T(8,128)(2,1)S(1)}, bf16[2,512,1024]{2,1,0:T(8,128)(2,1)}, u32[]{:S(2)}, u32[]{:S(2)}) collective-permute-start(bf16[2,512,1024]{2,1,0:T(8,128)(2,1)S(1)} %collective-permute-done.34.refs_1_), channel_id=1, source_target_pairs={{0,1},{1,0},{2,3},{3,2},{4,5},{5,4},{6,7},{7,6}} | collective-permute-start | bytes 6291464 | tf_op jit(solution)/shard_map/ppermute | solution.py:497
  734.3 1.6 collective-permute-start.40
  736.9 7.1 collective-permute-start.41
  738.4 9.5 %collective-permute-start.42 = (f32[40,1024]{1,0:T(8,128)S(1)}, f32[40,1024]{1,0:T(8,128)S(1)}, u32[]{:S(2)}, u32[]{:S(2)}) collective-permute-start(f32[40,1024]{1,0:T(8,128)S(1)} %add.100), channel_id=1, source_target_pairs={{0,4},{1,5},{2,6},{3,7},{4,0},{5,1},{6,2},{7,3}} | collective-permute-start | bytes 491528 | tf_op jit(solution)/shard_map/ppermute | solution.py:497
  739.2 8.6 %collective-permute-start.43 = (f32[40,1024]{1,0:T(8,128)S(1)}, f32[40,1024]{1,0:T(8,128)S(1)}, u32[]{:S(2)}, u32[]{:S(2)}) collective-permute-start(f32[40,1024]{1,0:T(8,128)S(1)} %add.100), channel_id=1, source_target_pairs={{0,6},{1,7},{2,4},{3,5},{4,2},{5,3},{6,0},{7,1}} | collective-permute-start | bytes 491528 | tf_op jit(solution)/shard_map/ppermute | solution.py:497
  (20 other events, 41.9 us)

commit v3 on v2

--- a/solution.py
+++ b/solution.py
@@ -12,6 +12,8 @@
 LANES = 128
 CHUNK = 512
 MIB = 2**20
+GRANT = 60 * MIB
+WEIGHTS = 3
 
 
 def as_tiles(ref, cols):
@@ -35,24 +37,31 @@
     return ((row >> 3) << 6) | (row & 7)
 
 
-def gather_body(idx, *refs, num_src, rows, block):
-    srcs = refs[:num_src]
-    out, src32, stage, buf, sem = refs[num_src:]
+def gather_body(idx, *refs, num_src, rows, block, split):
+    srcs, outs = refs[:num_src], refs[num_src:num_src + split + 1]
+    src32, stage, buf, sem = refs[num_src + split + 1:num_src + split + 5]
     step = pl.program_id(0)
     chunks = rows // CHUNK
 
     @pl.when(step == 0)
     def _():
-        def load(k):
-            src = srcs[k] if num_src > 1 else srcs[0].at[pl.ds(k * CHUNK, CHUNK)]
+        def load(src, k):
             return pltpu.make_async_copy(src, buf.at[k % 2], sem.at[k % 2])
 
-        load(0).start()
-        for k in range(chunks):
-            if k + 1 < chunks:
-                load(k + 1).start()
-            load(k).wait()
+        def start(k):
+            if num_src == 1:
+                load(srcs[0].at[pl.ds(pl.multiple_of(k * CHUNK, CHUNK), CHUNK)], k).start()
+            for i in range(num_src if num_src > 1 else 0):
+                pl.when(k == i)(lambda i=i: load(srcs[i], i).start())
+
+        def convert(k, carry):
+            pl.when(k + 1 < chunks)(lambda: start(k + 1))
+            load(srcs[0].at[pl.ds(0, CHUNK)], k).wait()
             put_rows(src32, k * CHUNK, buf[k % 2].astype(F32))
+            return carry
+
+        start(jnp.int32(0))
+        lax.fori_loop(0, chunks, convert, 0)
 
     unroll = 16
 
@@ -63,22 +72,51 @@
         return carry
 
     lax.fori_loop(0, block // unroll, body, 0)
-    out[...] = get_rows(stage, 0, block, out.shape[1]).astype(BF16)
-
-
-def gather_rows(idx, srcs, num_out):
+    cols = srcs[0].shape[1]
+    if not split:
+        outs[0][...] = get_rows(stage, 0, block, cols).astype(BF16)
+        return
+
+    out_buf, out_sem = refs[-2:]
+    slot = lax.rem(step, 2)
+
+    def save(dst, at):
+        return pltpu.make_async_copy(out_buf.at[at], dst, out_sem.at[at])
+
+    first_rows = outs[-1].at[pl.ds(0, block)]
+    pl.when(step >= 2)(lambda: save(first_rows, slot).wait())
+    out_buf[slot] = get_rows(stage, 0, block, cols).astype(BF16)
+    for i in range(split):
+        pl.when(step == i)(lambda i=i: save(outs[i], slot).start())
+
+    @pl.when(step >= split)
+    def _():
+        save(outs[-1].at[pl.ds(pl.multiple_of((step - split) * block, block), block)], slot).start()
+
+    @pl.when(step == pl.num_programs(0) - 1)
+    def _():
+        save(first_rows, 1 - slot).wait()
+        save(first_rows, slot).wait()
+
+
+def gather_rows(idx, srcs, num_out, split=0):
     rows, cols = sum(s.shape[0] for s in srcs), srcs[0].shape[1]
     block = 512
+    scratch = [pltpu.VMEM((rows * 8, LANES), F32), pltpu.VMEM((block * 8, LANES), F32),
+               pltpu.VMEM((2, CHUNK, cols), BF16), pltpu.SemaphoreType.DMA((2,))]
+    out_specs = pl.BlockSpec((block, cols), lambda i, idx: (i, 0))
+    out_shape = jax.ShapeDtypeStruct((num_out, cols), BF16)
+    if split:
+        scratch += [pltpu.VMEM((2, block, cols), BF16), pltpu.SemaphoreType.DMA((2,))]
+        out_specs = [pl.BlockSpec(memory_space=pl.ANY)] * (split + 1)
+        out_shape = [jax.ShapeDtypeStruct((block, cols), BF16)] * split + [jax.ShapeDtypeStruct((num_out - split * block, cols), BF16)]
     return pl.pallas_call(
-        functools.partial(gather_body, num_src=len(srcs), rows=rows, block=block),
+        functools.partial(gather_body, num_src=len(srcs), rows=rows, block=block, split=split),
         grid_spec=pltpu.PrefetchScalarGridSpec(
             num_scalar_prefetch=1, grid=(num_out // block,),
-            in_specs=[pl.BlockSpec(memory_space=pl.ANY)] * len(srcs),
-            out_specs=pl.BlockSpec((block, cols), lambda i, idx: (i, 0)),
-            scratch_shapes=[pltpu.VMEM((rows * 8, LANES), F32), pltpu.VMEM((block * 8, LANES), F32),
-                            pltpu.VMEM((2, CHUNK, cols), BF16), pltpu.SemaphoreType.DMA((2,))]),
-        out_shape=jax.ShapeDtypeStruct((num_out, cols), BF16),
-        compiler_params=pltpu.CompilerParams(dimension_semantics=("arbitrary",), vmem_limit_bytes=40 * MIB),
+            in_specs=[pl.BlockSpec(memory_space=pl.ANY)] * len(srcs), out_specs=out_specs, scratch_shapes=scratch),
+        out_shape=out_shape,
+        compiler_params=pltpu.CompilerParams(dimension_semantics=("arbitrary",), vmem_limit_bytes=GRANT),
         cost_estimate=pl.CostEstimate(flops=num_out * 1_000_000, bytes_accessed=num_out * cols * 4, transcendentals=0))(idx, *srcs)
 
 
@@ -127,18 +165,36 @@
 
 def owner_body(ids, x_ref, r_ref, gate_ref, *refs, first, per, num_pairs, experts, scale):
     weights = refs[:2 * num_pairs]
-    h_ref, g_ref, aux_ref = refs[-3:]
     step = pl.program_id(0)
-
-    def one_expert(w1_ref, w2_ref):
+    if num_pairs == 1:
+        h_ref, g_ref, aux_ref = refs[-3:]
         h_ref[...], g_ref[...], aux_ref[...] = owner_expert(
-            x_ref[...], r_ref[...], w1_ref[0], w2_ref[0], gate_ref[...], ids[first + step], experts, scale)
-
-    for k in range(num_pairs):
-        if num_pairs == 1:
-            one_expert(weights[0], weights[1])
-        else:
-            pl.when(step // per == k)(functools.partial(one_expert, weights[2 * k], weights[2 * k + 1]))
+            x_ref[...], r_ref[...], weights[0][0], weights[1][0], gate_ref[...], ids[first + step], experts, scale)
+        return
+    h_ref, g_ref, aux_ref, w1_buf, w2_buf, sem = refs[-6:]
+    num = per * num_pairs
+
+    def load(w1, w2, at, i):
+        slot = lax.rem(i, WEIGHTS)
+        return [pltpu.make_async_copy(w1.at[at], w1_buf.at[slot], sem.at[0, slot]),
+                pltpu.make_async_copy(w2.at[at], w2_buf.at[slot], sem.at[1, slot])]
+
+    def start(i):
+        for k in range(num_pairs):
+            @pl.when((i >= k * per) & (i < (k + 1) * per))
+            def _():
+                start_all(load(weights[2 * k], weights[2 * k + 1], i - k * per, i))
+
+    @pl.when(step == 0)
+    def _():
+        for i in range(min(WEIGHTS - 1, num)):
+            start(jnp.int32(i))
+
+    start(step + WEIGHTS - 1)
+    wait_all(load(weights[0], weights[1], 0, step))
+    slot = lax.rem(step, WEIGHTS)
+    h_ref[...], g_ref[...], aux_ref[...] = owner_expert(
+        x_ref[...], r_ref[...], w1_buf[slot], w2_buf[slot], gate_ref[...], ids[first + step], experts, scale)
 
 
 def owner_group(ids, picked_x, picked_r, pairs, gate_pad, bufs, first, picks, experts, scale):
@@ -146,14 +202,16 @@
     num = per * len(pairs)
     total = picked_x.shape[0]
     rows = lambda i, ids: (first + i, 0)
-
-    def weight(k):
-        return lambda i, ids: (jnp.clip(i - k * per, 0, per - 1), 0, 0)
-
     in_specs = [pl.BlockSpec((picks, cols), rows), pl.BlockSpec((picks, cols), rows),
                 pl.BlockSpec(gate_pad.shape, lambda i, ids: (0, 0))]
-    for k in range(len(pairs)):
-        in_specs += [pl.BlockSpec((1, cols, width), weight(k)), pl.BlockSpec((1, width, cols), weight(k))]
+    scratch = []
+    if len(pairs) == 1:
+        weight = lambda i, ids: (i, 0, 0)
+        in_specs += [pl.BlockSpec((1, cols, width), weight), pl.BlockSpec((1, width, cols), weight)]
+    else:
+        in_specs += [pl.BlockSpec(memory_space=pl.ANY)] * (2 * len(pairs))
+        scratch = [pltpu.VMEM((WEIGHTS, cols, width), BF16), pltpu.VMEM((WEIGHTS, width, cols), BF16),
+                   pltpu.SemaphoreType.DMA((2, WEIGHTS))]
     alias = {}
     if bufs:
         alias = {1 + len(in_specs) + j: j for j in range(3)}
@@ -163,15 +221,17 @@
         grid_spec=pltpu.PrefetchScalarGridSpec(
             num_scalar_prefetch=1, grid=(num,), in_specs=in_specs,
             out_specs=[pl.BlockSpec((picks, cols), rows), pl.BlockSpec((picks, cols), rows),
-                       pl.BlockSpec((picks, LANES), rows)]),
+                       pl.BlockSpec((picks, LANES), rows)],
+            scratch_shapes=scratch),
         out_shape=[jax.ShapeDtypeStruct((total, cols), BF16), jax.ShapeDtypeStruct((total, cols), BF16),
                    jax.ShapeDtypeStruct((total, LANES), F32)],
         input_output_aliases=alias,
-        compiler_params=pltpu.CompilerParams(dimension_semantics=("arbitrary",), vmem_limit_bytes=48 * MIB),
+        compiler_params=pltpu.CompilerParams(dimension_semantics=("arbitrary",), vmem_limit_bytes=GRANT),
         cost_estimate=pl.CostEstimate(flops=num * 1_000_000_000, bytes_accessed=num * 4 * MIB, transcendentals=0))(ids, picked_x, picked_r, gate_pad, *[w for pair in pairs for w in pair], *bufs)
 
 
-def expert_body(ids, x_ref, r_ref, w1_ref, w2_ref, gate_ref, up_ref, down_ref, up_acc, down_acc, *, experts, scale):
+def expert_body(ids, x_ref, r_ref, w1_ref, w2_ref, gate_ref, *refs, carried, experts, scale):
+    up_ref, down_ref, up_acc, down_acc = refs[-4:]
     expert = ids[pl.program_id(0)]
     step = pl.program_id(1)
     x_rows = x_ref[...]
@@ -185,37 +245,42 @@
 
     @pl.when(step == 0)
     def _():
-        up_acc[...] = jnp.zeros_like(up_acc)
-        down_acc[...] = jnp.zeros_like(down_acc)
+        if carried:
+            up_acc[...] = refs[0][0]
+            down_acc[...] = refs[1][0]
+        else:
+            up_acc[...] = jnp.zeros_like(up_acc)
+            down_acc[...] = jnp.zeros_like(down_acc)
 
     down_acc[...] += dot_tn(act.astype(BF16), dh)
     up_acc[...] += dot_tn(x_rows, da)
 
     @pl.when(step == pl.num_programs(1) - 1)
     def _():
-        up_ref[0] = up_acc[...].astype(BF16)
-        down_ref[0] = down_acc[...].astype(BF16)
-
-
-def expert_grads(ids, rows_x, rows_r, w1, w2, gate_pad, experts, scale):
+        up_ref[0] = up_acc[...].astype(up_ref.dtype)
+        down_ref[0] = down_acc[...].astype(down_ref.dtype)
+
+
+def expert_grads(ids, rows_x, first_x, rows_r, w1, w2, gate_pad, sums, out_type, experts, scale):
     num, cols, width = w1.shape
     block = 512
-    steps = rows_x.shape[0] // num // block
-    rows = lambda e, i, ids: (e * steps + i, 0)
+    steps = rows_r.shape[0] // num // block
+    skip = first_x // block
     weight = lambda e, i, ids: (e, 0, 0)
+    grads = [pl.BlockSpec((1, cols, width), weight), pl.BlockSpec((1, width, cols), weight)]
     return pl.pallas_call(
-        functools.partial(expert_body, experts=experts, scale=scale),
+        functools.partial(expert_body, carried=bool(sums), experts=experts, scale=scale),
         grid_spec=pltpu.PrefetchScalarGridSpec(
             num_scalar_prefetch=1, grid=(num, steps),
-            in_specs=[pl.BlockSpec((block, cols), rows), pl.BlockSpec((block, cols), rows),
+            in_specs=[pl.BlockSpec((block, cols), lambda e, i, ids: (skip + e * steps + i, 0)),
+                      pl.BlockSpec((block, cols), lambda e, i, ids: (e * steps + i, 0)),
                       pl.BlockSpec((1, cols, width), weight), pl.BlockSpec((1, width, cols), weight),
-                      pl.BlockSpec(gate_pad.shape, lambda e, i, ids: (0, 0))],
-            out_specs=[pl.BlockSpec((1, cols, width), weight), pl.BlockSpec((1, width, cols), weight)],
+                      pl.BlockSpec(gate_pad.shape, lambda e, i, ids: (0, 0))] + (grads if sums else []),
+            out_specs=grads,
             scratch_shapes=[pltpu.VMEM((cols, width), F32), pltpu.VMEM((width, cols), F32)]),
-        out_shape=[jax.ShapeDtypeStruct(w1.shape, BF16), jax.ShapeDtypeStruct(w2.shape, BF16)],
-        compiler_params=pltpu.CompilerParams(dimension_semantics=("arbitrary", "arbitrary"), vmem_limit_bytes=48 * MIB),
-        cost_estimate=pl.CostEstimate(flops=45_000_000_000, bytes_accessed=48 * MIB, transcendentals=0),
-        name="expert_grads")(ids, rows_x, rows_r, w1, w2, gate_pad)
+        out_shape=[jax.ShapeDtypeStruct(w1.shape, out_type), jax.ShapeDtypeStruct(w2.shape, out_type)],
+        compiler_params=pltpu.CompilerParams(dimension_semantics=("arbitrary", "arbitrary"), vmem_limit_bytes=GRANT),
+        cost_estimate=pl.CostEstimate(flops=num * steps * 3_000_000_000, bytes_accessed=48 * MIB, transcendentals=0))(ids, rows_x, rows_r, w1, w2, gate_pad, *sums)
 
 
 def add_block(idx, tok, base, h_ref, g_ref, aux_ref, y_acc, g_acc, s_acc, y_stage, g_stage):
@@ -240,11 +305,15 @@
     lax.fori_loop(0, picks // unroll, body, 0)
 
 
-def start_all(pairs, sem):
+def start_pairs(pairs, sem):
     copies = [pltpu.make_async_copy(a, b, sem.at[k]) for k, (a, b) in enumerate(pairs)]
+    start_all(copies)
+    return copies
+
+
+def start_all(copies):
     for copy in copies:
         copy.start()
-    return copies
 
 
 def wait_all(copies):
@@ -273,7 +342,7 @@
 
     @pl.when(step == chunks + blocks - 1)
     def _():
-        wait_all(start_all(((y_acc, y_out), (g_acc, g_out), (s_acc, s_out)), sem))
+        wait_all(start_pairs(((y_acc, y_out), (g_acc, g_out), (s_acc, s_out)), sem))
 
 
 def combine_first(idx, tok, x, loss_w, h, g, aux, gate_pad, picks, blocks, experts, scale):
@@ -292,7 +361,7 @@
             scratch_shapes=[pltpu.VMEM(s, F32) for s in acc_shapes(tokens)]
             + [pltpu.VMEM((picks * 8, LANES), F32)] * 2 + [pltpu.SemaphoreType.DMA((3,))]),
         out_shape=[jax.ShapeDtypeStruct(s, F32) for s in acc_shapes(tokens) + [(tokens, LANES)]],
-        compiler_params=pltpu.CompilerParams(dimension_semantics=("arbitrary",), vmem_limit_bytes=56 * MIB),
+        compiler_params=pltpu.CompilerParams(dimension_semantics=("arbitrary",), vmem_limit_bytes=GRANT),
         cost_estimate=pl.CostEstimate(flops=30_000_000_000, bytes_accessed=64 * MIB, transcendentals=0),
         name="combine_first")(idx, tok, x, loss_w, h, g, aux, gate_pad)
 
@@ -303,13 +372,13 @@
 
     @pl.when(step == 0)
     def _():
-        wait_all(start_all(((y_in, y_acc), (g_in, g_acc), (s_in, s_acc)), sem))
+        wait_all(start_pairs(((y_in, y_acc), (g_in, g_acc), (s_in, s_acc)), sem))
 
     add_block(idx, tok, (first + step) * h_ref.shape[0], h_ref, g_ref, aux_ref, y_acc, g_acc, s_acc, y_stage, g_stage)
 
     @pl.when(step == blocks - 1)
     def _():
-        wait_all(start_all(((y_acc, y_out), (g_acc, g_out), (s_acc, s_out)), sem))
+        wait_all(start_pairs(((y_acc, y_out), (g_acc, g_out), (s_acc, s_out)), sem))
 
 
 def combine_mid(idx, tok, h, g, aux, accs, picks, first, blocks):
@@ -325,7 +394,7 @@
             scratch_shapes=[pltpu.VMEM(s, F32) for s in acc_shapes(tokens)]
             + [pltpu.VMEM((picks * 8, LANES), F32)] * 2 + [pltpu.SemaphoreType.DMA((3,))]),
         out_shape=[jax.ShapeDtypeStruct(s, F32) for s in acc_shapes(tokens)],
-        compiler_params=pltpu.CompilerParams(dimension_semantics=("arbitrary",), vmem_limit_bytes=56 * MIB),
+        compiler_params=pltpu.CompilerParams(dimension_semantics=("arbitrary",), vmem_limit_bytes=GRANT),
         cost_estimate=pl.CostEstimate(flops=20_000_000_000, bytes_accessed=64 * MIB, transcendentals=0),
         name="combine_mid")(idx, tok, h, g, aux, *accs)
 
@@ -358,7 +427,7 @@
 
     @pl.when(step == 0)
     def _():
-        start_all(loads, sem)
+        start_pairs(loads, sem)
 
     @pl.when(step < own)
     def _():
@@ -462,12 +531,12 @@
             + [pltpu.SemaphoreType.DMA((2, DEPTH))] * 2),
         out_shape=[jax.ShapeDtypeStruct(x.shape, BF16), jax.ShapeDtypeStruct(x.shape, BF16),
                    jax.ShapeDtypeStruct((experts + 8, cols), F32)],
-        compiler_params=pltpu.CompilerParams(dimension_semantics=("arbitrary",), vmem_limit_bytes=60 * MIB),
+        compiler_params=pltpu.CompilerParams(dimension_semantics=("arbitrary",), vmem_limit_bytes=GRANT),
         cost_estimate=pl.CostEstimate(flops=50_000_000_000, bytes_accessed=64 * MIB, transcendentals=0),
         name="combine_last")(ids, idx, tok, picked_x, picked_r, w1, w2, gate_pad, h, g, aux, x, loss_w, *accs, probs)
 
 
-def rank_picks(tok, tokens, distinct):
+def rank_picks(tok, distinct):
     side = 64
     steps = jnp.arange(side)
     hi = (tok // side)[..., None] == steps
@@ -481,9 +550,13 @@
     row = jnp.einsum('tph,thl->tpl', hi.astype(BF16), within.astype(BF16), preferred_element_type=F32)
     start = jnp.sum(jnp.where(hi, before[:, None, :], 0.0), axis=-1)
     place = (jnp.sum(jnp.where(lo, row, 0.0), axis=-1) + start - 1.0).astype(jnp.int32)
-    flat = count.reshape(tok.shape[0], 1, tokens)
-    listed = jnp.sum((flat <= jnp.arange(distinct, dtype=F32)[None, :, None]).astype(jnp.int32), axis=-1)
-    return listed, place
+    places = jnp.arange(distinct, dtype=F32)
+    hi_list = jnp.sum((count[:, None, :, -1] <= places[None, :, None]).astype(jnp.int32), axis=-1)
+    in_row = hi_list[..., None] == steps
+    row = jnp.einsum('tsh,thl->tsl', in_row.astype(BF16), within.astype(BF16), preferred_element_type=F32)
+    start = jnp.sum(jnp.where(in_row, before[:, None, :], 0.0), axis=-1)
+    lo_list = jnp.sum((row + start[..., None] <= places[None, :, None]).astype(jnp.int32), axis=-1)
+    return hi_list * side + lo_list, place
 
 
 def after(value, *earlier):
@@ -496,9 +569,8 @@
     def permute(value, mask):
         return lax.ppermute(value, 'ep', [(i, i ^ mask) for i in range(group)])
 
-    def dispatch(rows):
-        size = rows.shape[0] // group
-        return [rows[:size]] + [permute(rows[m * size:(m + 1) * size], m) for m in range(1, group)]
+    def dispatch(rows, masks):
+        return [permute(rows[m], m) if m else rows[m] for m in masks]
 
     def device_step(x, gate_w, up_w, down_w, expert_picks, loss_w):
         tokens, cols = x.shape
@@ -521,15 +593,7 @@
         xa, ya = [permute(v, 2) for v in part_a], [permute(v, 4) for v in part_a]
         partner = [permute(up_w, 1), permute(down_w, 1)]
 
-        send_list, _ = rank_picks(asked.reshape(group, -1), tokens, distinct)
-        send_idx = row_base(send_list).reshape(-1)
-        send_x = gather_rows(send_idx, [x], group * distinct)
-        send_r = gather_rows(after(send_idx, send_x), [loss_w], group * distinct)
-        got_x, got_r = dispatch(send_x), dispatch(send_r)
-
-        part_b = [w[half:] for w in after((up_w, down_w), send_r)]
-        xb, yb = [permute(v, 2) for v in part_b], [permute(v, 4) for v in part_b]
-
+        send_list, _ = rank_picks(asked.reshape(group, -1), distinct)
         spans = [(0, 0, local), (1, 0, local)] + [(m, 0, half) for m in (2, 4, 3, 5)]
         early = sum(s[2] for s in spans)
         spans += [(m, half, half) for m in (2, 4, 3, 5)] + [(6, 0, half), (7, 0, half), (6, half, half), (7, half, half)]
@@ -537,8 +601,14 @@
         own_ids = jnp.concatenate([ids_by_mask[m, s:s + n] for m, s, n in spans])
         own_tok = jnp.concatenate([asked[m, s:s + n] for m, s, n in spans]).reshape(-1)
         own_idx = row_base(own_tok)
-        picked_x = gather_rows(after(own_idx, send_r), [x], experts * picks)
-        picked_r = gather_rows(after(own_idx, picked_x), [loss_w], experts * picks)
+        gather_idx = jnp.concatenate([row_base(send_list).reshape(-1), own_idx])
+        *send_x, picked_x = gather_rows(gather_idx, [x], gather_idx.size, group)
+        *send_r, picked_r = gather_rows(after(gather_idx, picked_x), [loss_w], gather_idx.size, group)
+        near, far = range(6), range(6, group)
+        got_x, near_r, far_r = dispatch(send_x, range(group)), dispatch(send_r, near), dispatch(send_r, far)
+
+        part_b = [w[half:] for w in after((up_w, down_w), picked_r)]
+        xb, yb = [permute(v, 2) for v in part_b], [permute(v, 4) for v in part_b]
 
         def relay(vx, vy):
             return [permute(vx[0], 4), permute(vy[1], 2)]
@@ -554,16 +624,17 @@
         bufs = owner(bufs, local, partner)
         bufs = owner(bufs, 2 * local, xa, ya, xa1, ya1)
 
-        _, place = rank_picks(wanted.reshape(group, -1), tokens, distinct)
+        _, place = rank_picks(wanted.reshape(group, -1), distinct)
         rows_idx = row_base(place.reshape(group, local, picks) + jnp.arange(group)[:, None, None] * distinct)
-        rows_idx = rows_idx.transpose(1, 0, 2).reshape(-1)
+        near_idx, far_idx = (rows_idx[r.start:r.stop].transpose(1, 0, 2).reshape(-1) for r in (near, far))
         my_ids = me * local + jnp.arange(local)
-        rows_x = gather_rows(after(rows_idx, bufs[2]), got_x, local * capacity)
-        *accs, probs = combine_first(after(own_idx, rows_x), own_tok, x, loss_w, *bufs, gate_pad, picks, early, experts, scale)
-        rows_r = gather_rows(after(rows_idx, accs[2]), got_r, local * capacity)
-        grad_up, grad_down = expert_grads(my_ids, rows_x, rows_r, up_w, down_w, gate_pad, experts, scale)
-
-        own_ids = after(own_ids, grad_down)
+        *accs, probs = combine_first(after(own_idx, bufs[2]), own_tok, x, loss_w, *bufs, gate_pad, picks, early, experts, scale)
+        both_idx = jnp.concatenate([near_idx, far_idx])
+        rows_x = gather_rows(after(both_idx, accs[2]), got_x, local * capacity)
+        near_rows = gather_rows(after(near_idx, rows_x), near_r, near_idx.size)
+        sums = expert_grads(my_ids, rows_x, 0, near_rows, up_w, down_w, gate_pad, [], F32, experts, scale)
+
+        own_ids = after(own_ids, sums[1])
         bufs = owner(bufs, 4 * local, xb, yb)
         bufs = owner(bufs, 5 * local, xb1, yb1)
         accs = combine_mid(own_idx, own_tok, *bufs, accs, picks, early, 2 * local)
@@ -574,7 +645,11 @@
         y, grad_x, part = combine_last(own_ids, own_idx, own_tok, x, loss_w, picked_x, picked_r, *db1, *bufs, gate_pad,
                                        accs, probs, picks, 6 * local, experts, scale)
         part = part + permute(part, 1)
-        part = (part + permute(part, 2)) + (permute(part, 4) + permute(part, 6))
+        far_rows = gather_rows(after(far_idx - row_base(far.start * distinct), part), far_r, far_idx.size)
+        grad_up, grad_down = expert_grads(my_ids, rows_x, near_idx.size, far_rows, up_w, down_w, gate_pad, sums, BF16,
+                                          experts, scale)
+        others = [permute(part, mask) for mask in (2, 4, 6)]
+        part = (part + others[0]) + (others[1] + others[2])
         return y, jnp.sum(part[experts:]) * scale, grad_x, grad_up, grad_down, part[:experts].T
 
     return jax.shard_map(device_step, mesh=mesh,

time: 761 us -> 773 us (1.016)
  waiting for transfers between devices: 254 us -> 296 us
  local copies, waits for them, and re-layouts: 46.2 us -> 16.8 us
  Pallas kernels: 399 us -> 410 us
    ppermute x44, waiting for transfers between devices: 252 us -> 294 us  [permute(): return lax.ppermute(value, 'ep', [(i, i ^ mask) for i in range(group)])]
    unnamed x84 -> x37, local copies, waits for them, and re-layouts: 21.8 us -> 0.28 us
    reduce_sum x1 -> x2, other arithmetic: 8.78 us -> 0.37 us  [the longest x1 0.19 us: rank_picks(): jnp.sum((count[:, None, :, -1] <= places[None, :, None]).astype(jnp.int32...]
    pallas_call x1 -> x2, Pallas kernels: 61.6 us -> 68.6 us  [expert_grads(): pl.pallas_call(functools.partial(expert_body, carried=bool(sums), experts...]
    pallas_call x6 -> x5, Pallas kernels: 116 us -> 120 us  [gather_rows(): pl.pallas_call(functools.partial(gather_body, num_src=len(srcs), rows=row...]
  transfers between devices with their start and end apart: 45 -> 45, of which waited for: 13 -> 12; matrix products, arithmetic and copies ran while one was open for 3% -> 3% of each run, Pallas kernels for 45% -> 49%
where the time goes in v3:
time: 773 us; the launch traced here: 770 us
  Pallas kernels  410 us (53%)
  waiting for transfers between devices  296 us (38%)
  starting transfers between devices  34.5 us (4%)
  local copies, waits for them, and re-layouts  16.8 us (2%)
    ppermute x44, waiting for transfers between devices, permute(): return lax.ppermute(value, 'ep', [(i, i ^ mask) for i in range(group)])  294 us
    pallas_call x5, Pallas kernels, gather_rows(): pl.pallas_call(functools.partial(gather_body, num_src=len(srcs), rows=row...  120 us
    pallas_call x8, Pallas kernels, owner_group(): pl.pallas_call(functools.partial(owner_body, first=first, per=per, num_pa...  84 us
    pallas_call x2, Pallas kernels, expert_grads(): pl.pallas_call(functools.partial(expert_body, carried=bool(sums), experts...  68.6 us
    pallas_call x1, Pallas kernels, combine_first(): pl.pallas_call(functools.partial(combine_first_body, chunks=chunks, block...  54.4 us
    pallas_call x1, Pallas kernels, combine_last(): pl.pallas_call(functools.partial(combine_last_body, own_first=own_first,...  45 us
    pallas_call x1, Pallas kernels, combine_mid(): pl.pallas_call(functools.partial(combine_mid_body, first=first, blocks=bl...  38.6 us
    ppermute x44, starting transfers between devices, permute(): return lax.ppermute(value, 'ep', [(i, i ^ mask) for i in range(group)])  30.3 us
  transfers between devices with their start and end apart: 45, of which 12 were waited for; matrix products, arithmetic and copies ran while one was open for 3% of the time, Pallas kernels for 49%

profile of v3, /device:TPU:0, one launch (start us, length us, event | category | flops | bytes accessed | tf_op | source)
XLA Modules:
  0.0 770.2 jit_solution(6347378984505254232)
XLA Ops:
  0.6 4.3 all-to-all-start
  5.0 1.4 gather_fusion
  6.5 0.7 fusion.26
  7.5 2.2 all-to-all-done
  10.6 0.7 fusion.27
  13.2 0.6 pad_add_fusion.idx
  13.8 33.7 %shard_map.109 = (bf16[512,1024]{1,0:T(8,128)(2,1)}, bf16[512,1024]{1,0:T(8,128)(2,1)}, bf16[512,1024]{1,0:T(8,128)(2,1)}, bf16[512,1024]{1,0:T(8,128)(2,1)}, bf...) custom-call(s32[12288]{0:T(1024)} %pad_add_fusion.idx, ...), custom_call_target="tpu_custom_call" | custom-call | flops 12288000000 | bytes 50331648 | tf_op jit(solution)/shard_map/pallas_call | solution.py:113
  48.1 1.3 collective-permute-start.12
  49.7 3.0 slice.150
  53.3 0.8 collective-permute-start.13
  54.1 19.8 %collective-permute-done.11.refs_2_ = bf16[512,1024]{1,0:T(8,128)(2,1)} collective-permute-done((bf16[512,1024]{1,0:T(8,128)(2,1)}, bf16[512,1024]{1,0:T(8,128)(2,1)}, u32[]{:S(2)}, u32[]{:S(2)}) %collective-permute-start.11) | collective-permute-done | bytes 1048608 | tf_op jit(solution)/shard_map/ppermute | solution.py:570
  73.9 21.5 %collective-permute-done.12.refs_3_ = bf16[512,1024]{1,0:T(8,128)(2,1)} collective-permute-done((bf16[512,1024]{1,0:T(8,128)(2,1)}, bf16[512,1024]{1,0:T(8,128)(2,1)}, u32[]{:S(2)}, u32[]{:S(2)}) %collective-permute-start.12) | collective-permute-done | bytes 1048608 | tf_op jit(solution)/shard_map/ppermute | solution.py:570
  95.4 0.7 collective-permute-start.15
  96.0 33.7 %shard_map.110 = (bf16[512,1024]{1,0:T(8,128)(2,1)}, bf16[512,1024]{1,0:T(8,128)(2,1)}, bf16[512,1024]{1,0:T(8,128)(2,1)}, bf16[512,1024]{1,0:T(8,128)(2,1)}, bf...) custom-call(s32[12288]{0:T(1024)} %pad_add_fusion.idx, ...), custom_call_target="tpu_custom_call" | custom-call | flops 12288000000 | bytes 50331648 | tf_op jit(solution)/shard_map/pallas_call | solution.py:113
  129.8 2.7 collective-permute-start.16
  132.5 31.3 %collective-permute-done.15.refs_6_ = bf16[512,1024]{1,0:T(8,128)(2,1)} collective-permute-done((bf16[512,1024]{1,0:T(8,128)(2,1)}, bf16[512,1024]{1,0:T(8,128)(2,1)}, u32[]{:S(2)}, u32[]{:S(2)}) %collective-permute-start.15) | collective-permute-done | bytes 1048608 | tf_op jit(solution)/shard_map/ppermute | solution.py:570
  163.8 0.8 collective-permute-start.18
  164.6 3.1 slice.151
  167.7 17.5 %collective-permute-done.16.refs_7_ = bf16[512,1024]{1,0:T(8,128)(2,1)S(1)} collective-permute-done((bf16[512,1024]{1,0:T(8,128)(2,1)S(1)}, bf16[512,1024]{1,0:T(8,128)(2,1)S(1)}, u32[]{:S(2)}, u32[]{:S(2)}) %collective-permute-start.16) | collective-permute-done | bytes 1048608 | tf_op jit(solution)/shard_map/ppermute | solution.py:570
  185.2 0.8 collective-permute-start.1
  186.0 1.5 collective-permute-start.5
  187.4 20.7 %collective-permute-done.18.refs_2_ = bf16[512,1024]{1,0:T(8,128)(2,1)S(1)} collective-permute-done((bf16[512,1024]{1,0:T(8,128)(2,1)}, bf16[512,1024]{1,0:T(8,128)(2,1)S(1)}, u32[]{:S(2)}, u32[]{:S(2)}) %collective-permute-start.18) | collective-permute-done | bytes 1048608 | tf_op jit(solution)/shard_map/ppermute | solution.py:570
  208.7 0.7 collective-permute-start.4
  209.4 25.4 %collective-permute-done.5.refs_3_ = bf16[2,512,1024]{2,1,0:T(8,128)(2,1)} collective-permute-done((bf16[2,512,1024]{2,1,0:T(8,128)(2,1)}, bf16[2,512,1024]{2,1,0:T(8,128)(2,1)}, u32[]{:S(2)}, u32[]{:S(2)}) %collective-permute-start.5) | collective-permute-done | bytes 2097184 | tf_op jit(solution)/shard_map/ppermute | solution.py:570
  235.0 0.7 pad.4.gate_ref
  235.9 19.8 %collective-permute-done.3.refs_1_ = bf16[2,512,1024]{2,1,0:T(8,128)(2,1)} collective-permute-done((bf16[2,512,1024]{2,1,0:T(8,128)(2,1)}, bf16[2,512,1024]{2,1,0:T(8,128)(2,1)}, u32[]{:S(2)}, u32[]{:S(2)}) %collective-permute-start.3) | collective-permute-done | bytes 2097184 | tf_op jit(solution)/shard_map/ppermute | solution.py:570
  255.7 23.1 %collective-permute-done.4.refs_2_ = bf16[2,1024,512]{2,1,0:T(8,128)(2,1)} collective-permute-done((bf16[2,1024,512]{2,1,0:T(8,128)(2,1)}, bf16[2,1024,512]{2,1,0:T(8,128)(2,1)}, u32[]{:S(2)}, u32[]{:S(2)}) %collective-permute-start.4) | collective-permute-done | bytes 2097184 | tf_op jit(solution)/shard_map/ppermute | solution.py:570
  280.5 0.8 select_reduce_fusion.1
  281.2 11.0 %shard_map.111 = (bf16[8192,1024]{1,0:T(8,128)(2,1)}, bf16[8192,1024]{1,0:T(8,128)(2,1)}, f32[8192,128]{1,0:T(8,128)}) custom-call(s32[32]{0:T(128)} %concatenate.12.ids, bf16[8192,1024]{1,0:T(8,128)(2,1)} %get-tuple-element.79.x_ref.px_ref, bf16[8192,1024]{1,0:T(8,128)(2,1)} %get-tuple-element.81.r_ref.pr_ref, bf16[1024,128]{1,0:T(8,128)(2,1)} %pad.4.gate_ref, ...), custom_call_target="tpu_custom_call" | custom-call | flops 4000000000 | bytes 16777216 | tf_op jit(solution)/shard_map/pallas_call | solution.py:219
  292.2 3.0 slice.152
  295.3 3.2 slice.153
  299.0 0.8 collective-permute-start.22
  299.9 1.2 collective-permute-start.23
  301.2 0.6 pad_add_fusion.1.idx
  301.9 1.5 collective-permute-start.20
  303.4 0.8 collective-permute-start.21
  304.1 11.0 %shard_map.112 = (bf16[8192,1024]{1,0:T(8,128)(2,1)}, bf16[8192,1024]{1,0:T(8,128)(2,1)}, f32[8192,128]{1,0:T(8,128)}) custom-call(s32[32]{0:T(128)} %concatenate.12.ids, bf16[8192,1024]{1,0:T(8,128)(2,1)} %get-tuple-element.79.x_ref.px_ref, ...), custom_call_target="tpu_custom_call", output_to_operand_aliasing={{0}: (6, {}), {1}: (7, {}), {2}: (8, {})} | custom-call | flops 4000000000 | bytes 16777216 | tf_op jit(solution)/shard_map/pallas_call | solution.py:219
  315.1 18.2 %shard_map.113 = (bf16[8192,1024]{1,0:T(8,128)(2,1)}, bf16[8192,1024]{1,0:T(8,128)(2,1)}, f32[8192,128]{1,0:T(8,128)}) custom-call(s32[32]{0:T(128)} %concatenate.12.ids, bf16[8192,1024]{1,0:T(8,128)(2,1)} %get-tuple-element.79.x_ref.px_ref, ...), custom_call_target="tpu_custom_call", output_to_operand_aliasing={{0}: (12, {}), {1}: (13, {}), {2}: (14, {})} | custom-call | flops 8000000000 | bytes 33554432 | tf_op jit(solution)/shard_map/pallas_call | solution.py:219
  333.3 80.0 %collective-permute-done.19.refs_3_ = bf16[512,1024]{1,0:T(8,128)(2,1)} collective-permute-done((bf16[512,1024]{1,0:T(8,128)(2,1)}, bf16[512,1024]{1,0:T(8,128)(2,1)}, u32[]{:S(2)}, u32[]{:S(2)}) %collective-permute-start.19) | collective-permute-done | bytes 1048608 | tf_op jit(solution)/shard_map/ppermute | solution.py:570
  413.3 1.5 collective-permute-start.24
  415.4 1.5 collective-permute-start.34
  417.4 54.4 %combine_first.1 = (f32[32768,128]{1,0:T(8,128)}, f32[32768,128]{1,0:T(8,128)}, f32[4096,128]{1,0:T(8,128)}, f32[4096,128]{1,0:T(8,128)}) custom-call(s32[8192]{0:T(1024)} %copy-done.3, s32[8192]{0:T(1024)} %bitcast.102, bf16[4096,1024]{1,0:T(8,128)(2,1)} %x_in.1, bf16[4096,1024]{1,0:T(8,128)(2,1)} %r_in.1, ...), custom_call_target="tpu_custom_call" | custom-call | flops 30000001024 | bytes 67108864 | tf_op jit(solution)/shard_map/combine_first/pallas_call | solution.py:353
  471.9 25.1 %shard_map.114.x_ref = bf16[8192,1024]{1,0:T(8,128)(2,1)} custom-call(s32[8192]{0:T(1024)} %pad_add_fusion.1.idx, bf16[512,1024]{1,0:T(8,128)(2,1)} %get-tuple-element.96.refs_0_, bf16[512,1024]{1,0:T(8,128)(2,1)} %collective-permute-done.10.refs_1_, bf16[512,1024]{1,0:T(8,128)(2,1)} %collective-permute-done.11.refs_2_, ...), custom_call_target="tpu_custom_call" | custom-call | flops 8192000000 | bytes 33554432 | tf_op jit(solution)/shard_map/pallas_call | solution.py:113
  497.0 19.4 %shard_map.115.r_ref = bf16[6144,1024]{1,0:T(8,128)(2,1)} custom-call(s32[6144]{0:T(1024)} %copy-done.5, bf16[512,1024]{1,0:T(8,128)(2,1)} %get-tuple-element.105.refs_0_, bf16[512,1024]{1,0:T(8,128)(2,1)} %copy-done.11, bf16[512,1024]{1,0:T(8,128)(2,1)} %copy-done.12, bf16[512,1024]{1,0:T(8,128)(2,1)} %collective-permute-done.19.refs_3_, ...), custom_call_target="tpu_custom_call" | custom-call | flops 6144000000 | bytes 25165824 | tf_op jit(solution)/shard_map/pallas_call | solution.py:113
  516.4 0.8 collective-permute-start.30
  517.5 34.6 %collective-permute-done.34.refs_0_ = bf16[2,1024,512]{2,1,0:T(8,128)(2,1)} collective-permute-done((bf16[2,1024,512]{2,1,0:T(8,128)(2,1)S(1)}, bf16[2,1024,512]{2,1,0:T(8,128)(2,1)}, u32[]{:S(2)}, u32[]{:S(2)}) %collective-permute-start.34) | collective-permute-done | bytes 2097184 | tf_op jit(solution)/shard_map/ppermute | solution.py:570
  552.1 0.8 collective-permute-start.32
  553.4 49.2 %shard_map.116 = (f32[4,1024,512]{2,1,0:T(8,128)}, f32[4,512,1024]{2,1,0:T(8,128)}) custom-call(s32[4]{0:T(128)} %iota_add_fusion.1.ids, bf16[8192,1024]{1,0:T(8,128)(2,1)} %shard_map.114.x_ref, bf16[6144,1024]{1,0:T(8,128)(2,1)} %shard_map.115.r_ref, bf16[4,1024,512]{2,1,0:T(8,128)(2,1)} %w1_ref.3, bf16[4,512,1024]{2,1,0:T(8,128)(2,1)} %w2_ref.3, ...), custom_call_target="tpu_custom_call" | custom-call | flops 35999997952 | bytes 50331648 | tf_op jit(solution)/shard_map/pallas_call | solution.py:271
  602.6 11.2 %shard_map.117 = (bf16[8192,1024]{1,0:T(8,128)(2,1)}, bf16[8192,1024]{1,0:T(8,128)(2,1)}, f32[8192,128]{1,0:T(8,128)}) custom-call(s32[32]{0:T(128)} %concatenate.12.ids, bf16[8192,1024]{1,0:T(8,128)(2,1)} %get-tuple-element.79.x_ref.px_ref, ...), custom_call_target="tpu_custom_call", output_to_operand_aliasing={{0}: (8, {}), {1}: (9, {}), {2}: (10, {})} | custom-call | flops 4000000000 | bytes 16777216 | tf_op jit(solution)/shard_map/pallas_call | solution.py:219
  613.8 2.1 collective-permute-start.42
  617.0 11.2 %shard_map.118 = (bf16[8192,1024]{1,0:T(8,128)(2,1)}, bf16[8192,1024]{1,0:T(8,128)(2,1)}, f32[8192,128]{1,0:T(8,128)}) custom-call(s32[32]{0:T(128)} %concatenate.12.ids, bf16[8192,1024]{1,0:T(8,128)(2,1)} %get-tuple-element.79.x_ref.px_ref, ...), custom_call_target="tpu_custom_call", output_to_operand_aliasing={{0}: (8, {}), {1}: (9, {}), {2}: (10, {})} | custom-call | flops 4000000000 | bytes 16777216 | tf_op jit(solution)/shard_map/pallas_call | solution.py:219
  628.2 38.6 %combine_mid.1 = (f32[32768,128]{1,0:T(8,128)}, f32[32768,128]{1,0:T(8,128)}, f32[4096,128]{1,0:T(8,128)}) custom-call(s32[8192]{0:T(1024)} %copy-done.3, s32[8192]{0:T(1024)} %bitcast.103, bf16[8192,1024]{1,0:T(8,128)(2,1)} %get-tuple-element.120.h_ref.refs_2_, bf16[8192,1024]{1,0:T(8,128)(2,1)} %get-tuple-element.121.g_ref.refs_3_, ...), custom_call_target="tpu_custom_call" | custom-call | flops 20000000000 | bytes 67108864 | tf_op jit(solution)/shard_map/combine_mid/pallas_call | solution.py:387
  666.8 7.2 shard_map.119
  674.5 7.3 shard_map.120
  681.7 7.0 shard_map.121
  688.8 45.0 %combine_last.1 = (bf16[4096,1024]{1,0:T(8,128)(2,1)}, bf16[4096,1024]{1,0:T(8,128)(2,1)}, f32[40,1024]{1,0:T(8,128)}) custom-call(s32[32]{0:T(128)} %concatenate.12.ids, s32[8192]{0:T(1024)} %copy-done.3, s32[8192]{0:T(1024)} %bitcast.104, bf16[8192,1024]{1,0:T(8,128)(2,1)} %get-tuple-element.79.x_ref.px_ref, ...), custom_call_target="tpu_custom_call" | custom-call | flops 49999998976 | bytes 67108864 | tf_op jit(solution)/shard_map/combine_last/pallas_call | solution.py:514
  734.9 0.6 collective-permute-done.38
  735.5 0.9 add.117
  736.5 1.4 collective-permute-start.39
  737.9 1.3 collective-permute-start.40
  739.2 0.8 collective-permute-start.41
  740.0 7.7 shard_map.122.r_ref
  747.7 19.4 %shard_map.123 = (bf16[4,1024,512]{2,1,0:T(8,128)(2,1)}, bf16[4,512,1024]{2,1,0:T(8,128)(2,1)}) custom-call(s32[4]{0:T(128)} %iota_add_fusion.1.ids, bf16[8192,1024]{1,0:T(8,128)(2,1)} %shard_map.114.x_ref, bf16[2048,1024]{1,0:T(8,128)(2,1)} %shard_map.122.r_ref, bf16[4,1024,512]{2,1,0:T(8,128)(2,1)} %w1_ref.3, bf16[4,512,1024]{2,1,0:T(8,128)(2,1)} %w2_ref.3, ...), custom_call_target="tpu_custom_call" | custom-call | flops 12000000000 | bytes 50331648 | tf_op jit(solution)/shard_map/pallas_call | solution.py:271
  767.2 0.7 slice_bitcast_fusion
  (137 shorter events, 13.0 us)
Async XLA Ops:
  0.6 9.1 %all-to-all-start = ((s32[4,8,256]{2,0,1:T(4,128)}), s32[4,8,256]{2,0,1:T(4,128)S(1)}, u32[]{:S(2)}, u32[]{:S(2)}) async-start(s32[4,8,256]{2,0,1:T(4,128)} %bitcast.99), calls=%async_computation | async-start | bytes 65536 | tf_op jit(solution)/shard_map/all_to_all | solution.py:587
  13.1 34.4 %copy-start.4 = (s32[4,2,8,128]{3,1,2,0:T(2,128)}, s32[4,2,8,128]{3,1,2,0:T(2,128)S(1)}, u32[]{:S(2)}) copy-start(s32[4,2,8,128]{3,1,2,0:T(2,128)S(1)} %copy.39) | copy-start | bytes 98308
  13.1 34.3 %copy-start.3 = (s32[8192]{0:T(1024)}, s32[8192]{0:T(1024)S(1)}, u32[]{:S(2)}) copy-start(s32[8192]{0:T(1024)S(1)} %and_or_fusion.idx) | copy-start | bytes 98308
  47.5 5.8 collective-permute-start.10
  47.5 26.4 %collective-permute-start.11 = (bf16[512,1024]{1,0:T(8,128)(2,1)}, bf16[512,1024]{1,0:T(8,128)(2,1)}, u32[]{:S(2)}, u32[]{:S(2)}) collective-permute-start(bf16[512,1024]{1,0:T(8,128)(2,1)} %get-tuple-element.98), channel_id=1, source_target_pairs={{0,2},{1,3},{2,0},{3,1},{4,6},{5,7},{6,4},{7,5}} | collective-permute-start | bytes 3145736 | tf_op jit(solution)/shard_map/ppermute | solution.py:570
  48.1 47.3 %collective-permute-start.12 = (bf16[512,1024]{1,0:T(8,128)(2,1)}, bf16[512,1024]{1,0:T(8,128)(2,1)}, u32[]{:S(2)}, u32[]{:S(2)}) collective-permute-start(bf16[512,1024]{1,0:T(8,128)(2,1)} %get-tuple-element.99), channel_id=1, source_target_pairs={{0,3},{1,2},{2,1},{3,0},{4,7},{5,6},{6,5},{7,4}} | collective-permute-start | bytes 3145736 | tf_op jit(solution)/shard_map/ppermute | solution.py:570
  49.4 229.4 %collective-permute-start = (bf16[4,1024,512]{2,1,0:T(8,128)(2,1)}, bf16[4,1024,512]{2,1,0:T(8,128)(2,1)}, u32[]{:S(2)}, u32[]{:S(2)}) collective-permute-start(bf16[4,1024,512]{2,1,0:T(8,128)(2,1)} %w1_ref.3), channel_id=1, source_target_pairs={{0,1},{1,0},{2,3},{3,2},{4,5},{5,4},{6,7},{7,6}} | collective-permute-start | bytes 12582920 | tf_op jit(solution)/shard_map/ppermute | solution.py:570
  52.7 156.0 %collective-permute-start.2 = (bf16[2,1024,512]{2,1,0:T(8,128)(2,1)}, bf16[2,1024,512]{2,1,0:T(8,128)(2,1)S(1)}, u32[]{:S(2)}, u32[]{:S(2)}) collective-permute-start(bf16[2,1024,512]{2,1,0:T(8,128)(2,1)} %slice.150), channel_id=1, source_target_pairs={{0,2},{1,3},{2,0},{3,1},{4,6},{5,7},{6,4},{7,5}} | collective-permute-start | bytes 6291464 | tf_op jit(solution)/shard_map/ppermute | solution.py:570
  53.3 76.4 %collective-permute-start.13 = (bf16[512,1024]{1,0:T(8,128)(2,1)}, bf16[512,1024]{1,0:T(8,128)(2,1)}, u32[]{:S(2)}, u32[]{:S(2)}) collective-permute-start(bf16[512,1024]{1,0:T(8,128)(2,1)} %get-tuple-element.100), channel_id=1, source_target_pairs={{0,4},{1,5},{2,6},{3,7},{4,0},{5,1},{6,2},{7,3}} | collective-permute-start | bytes 3145736 | tf_op jit(solution)/shard_map/ppermute | solution.py:570
  73.9 58.6 %collective-permute-start.14 = (bf16[512,1024]{1,0:T(8,128)(2,1)}, bf16[512,1024]{1,0:T(8,128)(2,1)}, u32[]{:S(2)}, u32[]{:S(2)}) collective-permute-start(bf16[512,1024]{1,0:T(8,128)(2,1)} %get-tuple-element.101), channel_id=1, source_target_pairs={{0,5},{1,4},{2,7},{3,6},{4,1},{5,0},{6,3},{7,2}} | collective-permute-start | bytes 3145736 | tf_op jit(solution)/shard_map/ppermute | solution.py:570
  95.4 34.4 %copy-start.14 = (bf16[512,1024]{1,0:T(8,128)(2,1)S(1)}, bf16[512,1024]{1,0:T(8,128)(2,1)}, u32[]{:S(2)}) copy-start(bf16[512,1024]{1,0:T(8,128)(2,1)} %get-tuple-element.103) | copy-start | bytes 3145732
  95.4 68.4 %collective-permute-start.15 = (bf16[512,1024]{1,0:T(8,128)(2,1)}, bf16[512,1024]{1,0:T(8,128)(2,1)}, u32[]{:S(2)}, u32[]{:S(2)}) collective-permute-start(bf16[512,1024]{1,0:T(8,128)(2,1)} %get-tuple-element.102), channel_id=1, source_target_pairs={{0,6},{1,7},{2,4},{3,5},{4,2},{5,3},{6,0},{7,1}} | collective-permute-start | bytes 3145736 | tf_op jit(solution)/shard_map/ppermute | solution.py:570
  129.8 55.4 %collective-permute-start.16 = (bf16[512,1024]{1,0:T(8,128)(2,1)S(1)}, bf16[512,1024]{1,0:T(8,128)(2,1)S(1)}, u32[]{:S(2)}, u32[]{:S(2)}) collective-permute-start(bf16[512,1024]{1,0:T(8,128)(2,1)S(1)} %copy-done.14), channel_id=1, source_target_pairs={{0,7},{1,6},{2,5},{3,4},{4,3},{5,2},{6,1},{7,0}} | collective-permute-start | bytes 3145736 | tf_op jit(solution)/shard_map/ppermute | solution.py:570
  132.5 53.5 %collective-permute-start.17 = (bf16[512,1024]{1,0:T(8,128)(2,1)}, bf16[512,1024]{1,0:T(8,128)(2,1)S(1)}, u32[]{:S(2)}, u32[]{:S(2)}) collective-permute-start(bf16[512,1024]{1,0:T(8,128)(2,1)} %get-tuple-element.106), channel_id=1, source_target_pairs={{0,1},{1,0},{2,3},{3,2},{4,5},{5,4},{6,7},{7,6}} | collective-permute-start | bytes 3145736 | tf_op jit(solution)/shard_map/ppermute | solution.py:570
  163.8 71.1 %copy-start.8 = (bf16[1024,32]{0,1:T(8,128)(2,1)S(1)}, bf16[1024,32]{0,1:T(8,128)(2,1)}, u32[]{:S(2)}) copy-start(bf16[1024,32]{0,1:T(8,128)(2,1)} %param.9) | copy-start | bytes 196612
  163.8 44.3 %collective-permute-start.18 = (bf16[512,1024]{1,0:T(8,128)(2,1)}, bf16[512,1024]{1,0:T(8,128)(2,1)S(1)}, u32[]{:S(2)}, u32[]{:S(2)}) collective-permute-start(bf16[512,1024]{1,0:T(8,128)(2,1)} %get-tuple-element.107), channel_id=1, source_target_pairs={{0,2},{1,3},{2,0},{3,1},{4,6},{5,7},{6,4},{7,5}} | collective-permute-start | bytes 3145736 | tf_op jit(solution)/shard_map/ppermute | solution.py:570
  185.2 49.6 %copy-start.10 = (bf16[512,1024]{1,0:T(8,128)(2,1)}, bf16[512,1024]{1,0:T(8,128)(2,1)S(1)}, u32[]{:S(2)}) copy-start(bf16[512,1024]{1,0:T(8,128)(2,1)S(1)} %collective-permute-done.16.refs_7_) | copy-start | bytes 3145732
  185.2 113.9 %collective-permute-start.1 = (bf16[4,512,1024]{2,1,0:T(8,128)(2,1)}, bf16[4,512,1024]{2,1,0:T(8,128)(2,1)}, u32[]{:S(2)}, u32[]{:S(2)}) collective-permute-start(bf16[4,512,1024]{2,1,0:T(8,128)(2,1)} %w2_ref.3), channel_id=1, source_target_pairs={{0,1},{1,0},{2,3},{3,2},{4,5},{5,4},{6,7},{7,6}} | collective-permute-start | bytes 12582920 | tf_op jit(solution)/shard_map/ppermute | solution.py:570
  186.0 48.8 %copy-start.11 = (bf16[512,1024]{1,0:T(8,128)(2,1)}, bf16[512,1024]{1,0:T(8,128)(2,1)S(1)}, u32[]{:S(2)}) copy-start(bf16[512,1024]{1,0:T(8,128)(2,1)S(1)} %collective-permute-done.17.refs_1_) | copy-start | bytes 3145732
  186.0 48.8 %collective-permute-start.5 = (bf16[2,512,1024]{2,1,0:T(8,128)(2,1)}, bf16[2,512,1024]{2,1,0:T(8,128)(2,1)}, u32[]{:S(2)}, u32[]{:S(2)}) collective-permute-start(bf16[2,512,1024]{2,1,0:T(8,128)(2,1)} %slice.151), channel_id=1, source_target_pairs={{0,4},{1,5},{2,6},{3,7},{4,0},{5,1},{6,2},{7,3}} | collective-permute-start | bytes 6291464 | tf_op jit(solution)/shard_map/ppermute | solution.py:570
  208.1 26.7 %copy-start.12 = (bf16[512,1024]{1,0:T(8,128)(2,1)}, bf16[512,1024]{1,0:T(8,128)(2,1)S(1)}, u32[]{:S(2)}) copy-start(bf16[512,1024]{1,0:T(8,128)(2,1)S(1)} %collective-permute-done.18.refs_2_) | copy-start | bytes 3145732
  208.1 47.6 %collective-permute-start.3 = (bf16[2,512,1024]{2,1,0:T(8,128)(2,1)}, bf16[2,512,1024]{2,1,0:T(8,128)(2,1)}, u32[]{:S(2)}, u32[]{:S(2)}) collective-permute-start(bf16[2,512,1024]{2,1,0:T(8,128)(2,1)} %slice.151), channel_id=1, source_target_pairs={{0,2},{1,3},{2,0},{3,1},{4,6},{5,7},{6,4},{7,5}} | collective-permute-start | bytes 6291464 | tf_op jit(solution)/shard_map/ppermute | solution.py:570
  208.7 83.5 %copy-start = (bf16[2,1024,512]{2,1,0:T(8,128)(2,1)}, bf16[2,1024,512]{2,1,0:T(8,128)(2,1)S(1)}, u32[]{:S(2)}) copy-start(bf16[2,1024,512]{2,1,0:T(8,128)(2,1)S(1)} %collective-permute-done.2.refs_0_) | copy-start | bytes 6291460
  208.7 70.1 %collective-permute-start.4 = (bf16[2,1024,512]{2,1,0:T(8,128)(2,1)}, bf16[2,1024,512]{2,1,0:T(8,128)(2,1)}, u32[]{:S(2)}, u32[]{:S(2)}) collective-permute-start(bf16[2,1024,512]{2,1,0:T(8,128)(2,1)} %slice.150), channel_id=1, source_target_pairs={{0,4},{1,5},{2,6},{3,7},{4,0},{5,1},{6,2},{7,3}} | collective-permute-start | bytes 6291464 | tf_op jit(solution)/shard_map/ppermute | solution.py:570
  234.8 65.1 %collective-permute-start.6 = (bf16[2,1024,512]{2,1,0:T(8,128)(2,1)S(1)}, bf16[2,1024,512]{2,1,0:T(8,128)(2,1)}, u32[]{:S(2)}, u32[]{:S(2)}) collective-permute-start(bf16[2,1024,512]{2,1,0:T(8,128)(2,1)S(1)} %collective-permute-done.2.refs_0_), channel_id=1, source_target_pairs={{0,1},{1,0},{2,3},{3,2},{4,5},{5,4},{6,7},{7,6}} | collective-permute-start | bytes 6291464 | tf_op jit(solution)/shard_map/ppermute | solution.py:570
  255.7 46.2 %collective-permute-start.9 = (bf16[2,512,1024]{2,1,0:T(8,128)(2,1)}, bf16[2,512,1024]{2,1,0:T(8,128)(2,1)}, u32[]{:S(2)}, u32[]{:S(2)}) collective-permute-start(bf16[2,512,1024]{2,1,0:T(8,128)(2,1)} %collective-permute-done.5.refs_3_), channel_id=1, source_target_pairs={{0,1},{1,0},{2,3},{3,2},{4,5},{5,4},{6,7},{7,6}} | collective-permute-start | bytes 6291464 | tf_op jit(solution)/shard_map/ppermute | solution.py:570
  278.8 23.1 %collective-permute-start.7 = (bf16[2,512,1024]{2,1,0:T(8,128)(2,1)}, bf16[2,512,1024]{2,1,0:T(8,128)(2,1)}, u32[]{:S(2)}, u32[]{:S(2)}) collective-permute-start(bf16[2,512,1024]{2,1,0:T(8,128)(2,1)} %collective-permute-done.3.refs_1_), channel_id=1, source_target_pairs={{0,1},{1,0},{2,3},{3,2},{4,5},{5,4},{6,7},{7,6}} | collective-permute-start | bytes 6291464 | tf_op jit(solution)/shard_map/ppermute | solution.py:570
  278.8 24.5 %collective-permute-start.8 = (bf16[2,1024,512]{2,1,0:T(8,128)(2,1)}, bf16[2,1024,512]{2,1,0:T(8,128)(2,1)}, u32[]{:S(2)}, u32[]{:S(2)}) collective-permute-start(bf16[2,1024,512]{2,1,0:T(8,128)(2,1)} %collective-permute-done.4.refs_2_), channel_id=1, source_target_pairs={{0,1},{1,0},{2,3},{3,2},{4,5},{5,4},{6,7},{7,6}} | collective-permute-start | bytes 6291464 | tf_op jit(solution)/shard_map/ppermute | solution.py:570
  295.3 8.1 %copy-start.13 = (bf16[512,1024]{1,0:T(8,128)(2,1)S(1)}, bf16[512,1024]{1,0:T(8,128)(2,1)}, u32[]{:S(2)}) copy-start(bf16[512,1024]{1,0:T(8,128)(2,1)} %get-tuple-element.110) | copy-start | bytes 3145732
  299.0 117.8 %collective-permute-start.22 = (bf16[2,1024,512]{2,1,0:T(8,128)(2,1)}, bf16[2,1024,512]{2,1,0:T(8,128)(2,1)}, u32[]{:S(2)}, u32[]{:S(2)}) collective-permute-start(bf16[2,1024,512]{2,1,0:T(8,128)(2,1)} %slice.152), channel_id=1, source_target_pairs={{0,2},{1,3},{2,0},{3,1},{4,6},{5,7},{6,4},{7,5}} | collective-permute-start | bytes 6291464 | tf_op jit(solution)/shard_map/ppermute | solution.py:570
  299.9 117.6 %collective-permute-start.23 = (bf16[2,512,1024]{2,1,0:T(8,128)(2,1)}, bf16[2,512,1024]{2,1,0:T(8,128)(2,1)}, u32[]{:S(2)}, u32[]{:S(2)}) collective-permute-start(bf16[2,512,1024]{2,1,0:T(8,128)(2,1)} %slice.153), channel_id=1, source_target_pairs={{0,2},{1,3},{2,0},{3,1},{4,6},{5,7},{6,4},{7,5}} | collective-permute-start | bytes 6291464 | tf_op jit(solution)/shard_map/ppermute | solution.py:570
  301.2 13.9 %copy-start.5 = (s32[6144]{0:T(1024)}, s32[6144]{0:T(1024)S(1)}, u32[]{:S(2)}) copy-start(s32[6144]{0:T(1024)S(1)} %reshape.189.idx) | copy-start | bytes 73732
  301.2 13.9 %copy-start.6 = (s32[4,2,2,128]{3,1,2,0:T(2,128)}, s32[4,2,2,128]{3,1,2,0:T(2,128)S(1)}, u32[]{:S(2)}) copy-start(s32[4,2,2,128]{3,1,2,0:T(2,128)S(1)} %copy.38) | copy-start | bytes 24580
  301.9 111.5 %collective-permute-start.19 = (bf16[512,1024]{1,0:T(8,128)(2,1)}, bf16[512,1024]{1,0:T(8,128)(2,1)}, u32[]{:S(2)}, u32[]{:S(2)}) collective-permute-start(bf16[512,1024]{1,0:T(8,128)(2,1)} %get-tuple-element.108), channel_id=1, source_target_pairs={{0,3},{1,2},{2,1},{3,0},{4,7},{5,6},{6,5},{7,4}} | collective-permute-start | bytes 3145736 | tf_op jit(solution)/shard_map/ppermute | solution.py:570
  301.9 112.9 %collective-permute-start.20 = (bf16[512,1024]{1,0:T(8,128)(2,1)}, bf16[512,1024]{1,0:T(8,128)(2,1)}, u32[]{:S(2)}, u32[]{:S(2)}) collective-permute-start(bf16[512,1024]{1,0:T(8,128)(2,1)} %get-tuple-element.109), channel_id=1, source_target_pairs={{0,4},{1,5},{2,6},{3,7},{4,0},{5,1},{6,2},{7,3}} | collective-permute-start | bytes 3145736 | tf_op jit(solution)/shard_map/ppermute | solution.py:570
  303.4 112.0 %collective-permute-start.21 = (bf16[512,1024]{1,0:T(8,128)(2,1)S(1)}, bf16[512,1024]{1,0:T(8,128)(2,1)}, u32[]{:S(2)}, u32[]{:S(2)}) collective-permute-start(bf16[512,1024]{1,0:T(8,128)(2,1)S(1)} %copy-done.13), channel_id=1, source_target_pairs={{0,5},{1,4},{2,7},{3,6},{4,1},{5,0},{6,3},{7,2}} | collective-permute-start | bytes 3145736 | tf_op jit(solution)/shard_map/ppermute | solution.py:570
  315.1 100.3 %copy-start.1 = (bf16[2,1024,512]{2,1,0:T(8,128)(2,1)S(1)}, bf16[2,1024,512]{2,1,0:T(8,128)(2,1)}, u32[]{:S(2)}) copy-start(bf16[2,1024,512]{2,1,0:T(8,128)(2,1)} %copy-done) | copy-start | bytes 6291460
  413.3 103.0 %collective-permute-start.24 = (bf16[2,1024,512]{2,1,0:T(8,128)(2,1)}, bf16[2,1024,512]{2,1,0:T(8,128)(2,1)}, u32[]{:S(2)}, u32[]{:S(2)}) collective-permute-start(bf16[2,1024,512]{2,1,0:T(8,128)(2,1)} %slice.152), channel_id=1, source_target_pairs={{0,4},{1,5},{2,6},{3,7},{4,0},{5,1},{6,2},{7,3}} | collective-permute-start | bytes 6291464 | tf_op jit(solution)/shard_map/ppermute | solution.py:570
  414.8 102.4 %collective-permute-start.25 = (bf16[2,512,1024]{2,1,0:T(8,128)(2,1)}, bf16[2,512,1024]{2,1,0:T(8,128)(2,1)}, u32[]{:S(2)}, u32[]{:S(2)}) collective-permute-start(bf16[2,512,1024]{2,1,0:T(8,128)(2,1)} %slice.153), channel_id=1, source_target_pairs={{0,4},{1,5},{2,6},{3,7},{4,0},{5,1},{6,2},{7,3}} | collective-permute-start | bytes 6291464 | tf_op jit(solution)/shard_map/ppermute | solution.py:570
  415.4 136.7 %collective-permute-start.34 = (bf16[2,1024,512]{2,1,0:T(8,128)(2,1)S(1)}, bf16[2,1024,512]{2,1,0:T(8,128)(2,1)}, u32[]{:S(2)}, u32[]{:S(2)}) collective-permute-start(bf16[2,1024,512]{2,1,0:T(8,128)(2,1)S(1)} %copy-done.1), channel_id=1, source_target_pairs={{0,4},{1,5},{2,6},{3,7},{4,0},{5,1},{6,2},{7,3}} | collective-permute-start | bytes 6291464 | tf_op jit(solution)/shard_map/ppermute | solution.py:570
  416.8 136.0 %collective-permute-start.35 = (bf16[2,512,1024]{2,1,0:T(8,128)(2,1)}, bf16[2,512,1024]{2,1,0:T(8,128)(2,1)}, u32[]{:S(2)}, u32[]{:S(2)}) collective-permute-start(bf16[2,512,1024]{2,1,0:T(8,128)(2,1)} %collective-permute-done.5.refs_3_), channel_id=1, source_target_pairs={{0,2},{1,3},{2,0},{3,1},{4,6},{5,7},{6,4},{7,5}} | collective-permute-start | bytes 6291464 | tf_op jit(solution)/shard_map/ppermute | solution.py:570
  417.4 135.5 %collective-permute-start.26 = (bf16[2,1024,512]{2,1,0:T(8,128)(2,1)}, bf16[2,1024,512]{2,1,0:T(8,128)(2,1)}, u32[]{:S(2)}, u32[]{:S(2)}) collective-permute-start(bf16[2,1024,512]{2,1,0:T(8,128)(2,1)} %collective-permute-done.22.refs_0_), channel_id=1, source_target_pairs={{0,1},{1,0},{2,3},{3,2},{4,5},{5,4},{6,7},{7,6}} | collective-permute-start | bytes 6291464 | tf_op jit(solution)/shard_map/ppermute | solution.py:570
  516.4 100.1 %collective-permute-start.30 = (bf16[2,1024,512]{2,1,0:T(8,128)(2,1)}, bf16[2,1024,512]{2,1,0:T(8,128)(2,1)}, u32[]{:S(2)}, u32[]{:S(2)}) collective-permute-start(bf16[2,1024,512]{2,1,0:T(8,128)(2,1)} %collective-permute-done.22.refs_0_), channel_id=1, source_target_pairs={{0,4},{1,5},{2,6},{3,7},{4,0},{5,1},{6,2},{7,3}} | collective-permute-start | bytes 6291464 | tf_op jit(solution)/shard_map/ppermute | solution.py:570
  517.2 98.7 %collective-permute-start.29 = (bf16[2,512,1024]{2,1,0:T(8,128)(2,1)}, bf16[2,512,1024]{2,1,0:T(8,128)(2,1)}, u32[]{:S(2)}, u32[]{:S(2)}) collective-permute-start(bf16[2,512,1024]{2,1,0:T(8,128)(2,1)} %collective-permute-done.25.refs_3_), channel_id=1, source_target_pairs={{0,1},{1,0},{2,3},{3,2},{4,5},{5,4},{6,7},{7,6}} | collective-permute-start | bytes 6291464 | tf_op jit(solution)/shard_map/ppermute | solution.py:570
  552.1 64.4 %collective-permute-start.32 = (bf16[2,512,1024]{2,1,0:T(8,128)(2,1)}, bf16[2,512,1024]{2,1,0:T(8,128)(2,1)S(1)}, u32[]{:S(2)}, u32[]{:S(2)}) collective-permute-start(bf16[2,512,1024]{2,1,0:T(8,128)(2,1)} %collective-permute-done.25.refs_3_), channel_id=1, source_target_pairs={{0,2},{1,3},{2,0},{3,1},{4,6},{5,7},{6,4},{7,5}} | collective-permute-start | bytes 6291464 | tf_op jit(solution)/shard_map/ppermute | solution.py:570
  552.9 60.9 %collective-permute-start.27 = (bf16[2,512,1024]{2,1,0:T(8,128)(2,1)}, bf16[2,512,1024]{2,1,0:T(8,128)(2,1)}, u32[]{:S(2)}, u32[]{:S(2)}) collective-permute-start(bf16[2,512,1024]{2,1,0:T(8,128)(2,1)} %collective-permute-done.23.refs_1_), channel_id=1, source_target_pairs={{0,1},{1,0},{2,3},{3,2},{4,5},{5,4},{6,7},{7,6}} | collective-permute-start | bytes 6291464 | tf_op jit(solution)/shard_map/ppermute | solution.py:570
  552.9 63.1 %collective-permute-start.28 = (bf16[2,1024,512]{2,1,0:T(8,128)(2,1)}, bf16[2,1024,512]{2,1,0:T(8,128)(2,1)}, u32[]{:S(2)}, u32[]{:S(2)}) collective-permute-start(bf16[2,1024,512]{2,1,0:T(8,128)(2,1)} %collective-permute-done.24.refs_2_), channel_id=1, source_target_pairs={{0,1},{1,0},{2,3},{3,2},{4,5},{5,4},{6,7},{7,6}} | collective-permute-start | bytes 6291464 | tf_op jit(solution)/shard_map/ppermute | solution.py:570
  613.8 126.2 %collective-permute-start.42 = (bf16[512,1024]{1,0:T(8,128)(2,1)}, bf16[512,1024]{1,0:T(8,128)(2,1)}, u32[]{:S(2)}, u32[]{:S(2)}) collective-permute-start(bf16[512,1024]{1,0:T(8,128)(2,1)} %get-tuple-element.146), channel_id=1, source_target_pairs={{0,6},{1,7},{2,4},{3,5},{4,2},{5,3},{6,0},{7,1}} | collective-permute-start | bytes 3145736 | tf_op jit(solution)/shard_map/ppermute | solution.py:570
  616.0 58.0 %collective-permute-start.36 = (bf16[2,1024,512]{2,1,0:T(8,128)(2,1)}, bf16[2,1024,512]{2,1,0:T(8,128)(2,1)}, u32[]{:S(2)}, u32[]{:S(2)}) collective-permute-start(bf16[2,1024,512]{2,1,0:T(8,128)(2,1)} %collective-permute-done.34.refs_0_), channel_id=1, source_target_pairs={{0,1},{1,0},{2,3},{3,2},{4,5},{5,4},{6,7},{7,6}} | collective-permute-start | bytes 6291464 | tf_op jit(solution)/shard_map/ppermute | solution.py:570
  616.0 58.5 %collective-permute-start.37 = (bf16[2,512,1024]{2,1,0:T(8,128)(2,1)}, bf16[2,512,1024]{2,1,0:T(8,128)(2,1)}, u32[]{:S(2)}, u32[]{:S(2)}) collective-permute-start(bf16[2,512,1024]{2,1,0:T(8,128)(2,1)} %collective-permute-done.35.refs_1_), channel_id=1, source_target_pairs={{0,1},{1,0},{2,3},{3,2},{4,5},{5,4},{6,7},{7,6}} | collective-permute-start | bytes 6291464 | tf_op jit(solution)/shard_map/ppermute | solution.py:570
  616.5 72.3 %collective-permute-start.31 = (bf16[2,1024,512]{2,1,0:T(8,128)(2,1)}, bf16[2,1024,512]{2,1,0:T(8,128)(2,1)}, u32[]{:S(2)}, u32[]{:S(2)}) collective-permute-start(bf16[2,1024,512]{2,1,0:T(8,128)(2,1)} %collective-permute-done.30.refs_0_), channel_id=1, source_target_pairs={{0,1},{1,0},{2,3},{3,2},{4,5},{5,4},{6,7},{7,6}} | collective-permute-start | bytes 6291464 | tf_op jit(solution)/shard_map/ppermute | solution.py:570
  616.5 11.7 %copy-start.2 = (bf16[2,512,1024]{2,1,0:T(8,128)(2,1)}, bf16[2,512,1024]{2,1,0:T(8,128)(2,1)S(1)}, u32[]{:S(2)}) copy-start(bf16[2,512,1024]{2,1,0:T(8,128)(2,1)S(1)} %collective-permute-done.32.refs_1_) | copy-start | bytes 6291460
  616.5 72.3 %collective-permute-start.33 = (bf16[2,512,1024]{2,1,0:T(8,128)(2,1)S(1)}, bf16[2,512,1024]{2,1,0:T(8,128)(2,1)}, u32[]{:S(2)}, u32[]{:S(2)}) collective-permute-start(bf16[2,512,1024]{2,1,0:T(8,128)(2,1)S(1)} %collective-permute-done.32.refs_1_), channel_id=1, source_target_pairs={{0,1},{1,0},{2,3},{3,2},{4,5},{5,4},{6,7},{7,6}} | collective-permute-start | bytes 6291464 | tf_op jit(solution)/shard_map/ppermute | solution.py:570
  666.8 7.2 copy-start.9
  674.0 66.0 %collective-permute-start.43 = (bf16[512,1024]{1,0:T(8,128)(2,1)S(1)}, bf16[512,1024]{1,0:T(8,128)(2,1)}, u32[]{:S(2)}, u32[]{:S(2)}) collective-permute-start(bf16[512,1024]{1,0:T(8,128)(2,1)S(1)} %copy-done.9), channel_id=1, source_target_pairs={{0,7},{1,6},{2,5},{3,4},{4,3},{5,2},{6,1},{7,0}} | collective-permute-start | bytes 3145736 | tf_op jit(solution)/shard_map/ppermute | solution.py:570
  688.8 45.5 %copy-start.7 = (s32[4,2,2,128]{3,1,2,0:T(2,128)S(1)}, s32[4,2,2,128]{3,1,2,0:T(2,128)}, u32[]{:S(2)}) copy-start(s32[4,2,2,128]{3,1,2,0:T(2,128)} %copy-done.6) | copy-start | bytes 24580
  733.8 1.7 collective-permute-start.38
  736.5 30.6 %collective-permute-start.39 = (f32[40,1024]{1,0:T(8,128)S(1)}, f32[40,1024]{1,0:T(8,128)S(1)}, u32[]{:S(2)}, u32[]{:S(2)}) collective-permute-start(f32[40,1024]{1,0:T(8,128)S(1)} %add.117), channel_id=1, source_target_pairs={{0,2},{1,3},{2,0},{3,1},{4,6},{5,7},{6,4},{7,5}} | collective-permute-start | bytes 491528 | tf_op jit(solution)/shard_map/ppermute | solution.py:570
  737.9 29.2 %collective-permute-start.40 = (f32[40,1024]{1,0:T(8,128)S(1)}, f32[40,1024]{1,0:T(8,128)S(1)}, u32[]{:S(2)}, u32[]{:S(2)}) collective-permute-start(f32[40,1024]{1,0:T(8,128)S(1)} %add.117), channel_id=1, source_target_pairs={{0,4},{1,5},{2,6},{3,7},{4,0},{5,1},{6,2},{7,3}} | collective-permute-start | bytes 491528 | tf_op jit(solution)/shard_map/ppermute | solution.py:570
  739.2 28.0 %collective-permute-start.41 = (f32[40,1024]{1,0:T(8,128)S(1)}, f32[40,1024]{1,0:T(8,128)S(1)}, u32[]{:S(2)}, u32[]{:S(2)}) collective-permute-start(f32[40,1024]{1,0:T(8,128)S(1)} %add.117), channel_id=1, source_target_pairs={{0,6},{1,7},{2,4},{3,5},{4,2},{5,3},{6,0},{7,1}} | collective-permute-start | bytes 491528 | tf_op jit(solution)/shard_map/ppermute | solution.py:570
